TPU v7x, 32 devices: a whole 2x2x4 slice. The times are simulated.
32 devices in a mesh: dp: 8 (over z, y), ep: 4 (over x, core).
Axes of the slice: x: 2, y: 2, z: 4, core: 2. Of those that a mesh axis runs over, the one named last changes fastest.
Arguments:
- hidden_in: bfloat16 [4096, 2048], P(('dp', 'ep')), may hold values from -6 to 6
- cotangent: bfloat16 [4096, 2048], P(('dp', 'ep')), may hold values from -6 to 6
- deal_order: int32 [4096], P(('dp', 'ep')), may hold values from 0 to 4095, as said below
- seq_lengths: int32 [32, 3], P(('dp', 'ep')), may hold values from 1 to 80, 112 in all within a row
- expert_ids: int32 [4096, 8], P(('dp', 'ep')), may hold values from 0 to 15, all different within a row; in each aligned block of 128 rows (0 to 127, 128 to 255, ...) at most 80 rows name the same one
- w_query: bfloat16 [2048, 4096], P(('dp', 'ep')), may hold values from -0.125 to 0.125
- w_key: bfloat16 [2048, 512], P(('dp', 'ep')), may hold values from -0.125 to 0.125
- w_value: bfloat16 [2048, 512], P(('dp', 'ep')), may hold values from -0.125 to 0.125
- w_out: bfloat16 [4096, 2048], P(('dp', 'ep')), may hold values from -0.375 to 0.375
- w_router: bfloat16 [2048, 16], P(('dp', 'ep')), may hold values from -0.0625 to 0.0625
- gain_attn: bfloat16 [2048], P(('dp', 'ep')), may hold values from 0.5 to 1.5
- gain_moe: bfloat16 [2048], P(('dp', 'ep')), may hold values from 0.5 to 1.5
- gain_query: bfloat16 [128], replicated, may hold values from 0.5 to 1.5
- gain_key: bfloat16 [128], replicated, may hold values from 0.5 to 1.5
- w_gate: bfloat16 [16, 2048, 768], P('ep', 'dp'), may hold values from -0.125 to 0.125
- w_up: bfloat16 [16, 2048, 768], P('ep', 'dp'), may hold values from -0.125 to 0.125
- w_down: bfloat16 [16, 768, 2048], P('ep', None, 'dp'), may hold values from -0.875 to 0.875
- clip_threshold: float32 [32], replicated, may hold values from 0.1 to 1
Outputs:
- block_out: bfloat16 [4096, 2048], P(('dp', 'ep'))
- grad_input: float32 [4096, 2048], P(('dp', 'ep'))
- grad_query: float32 [2048, 4096], P(('dp', 'ep'))
- grad_key: float32 [2048, 512], P(('dp', 'ep'))
- grad_value: float32 [2048, 512], P(('dp', 'ep'))
- grad_out: float32 [4096, 2048], P(('dp', 'ep'))
- grad_router: float32 [2048, 16], P(('dp', 'ep'))
- grad_gain_attn: float32 [2048], P(('dp', 'ep'))
- grad_gain_moe: float32 [2048], P(('dp', 'ep'))
- grad_gain_query: float32 [128], replicated
- grad_gain_key: float32 [128], replicated
- grad_gate: float32 [16, 2048, 768], P('ep', 'dp')
- grad_up: float32 [16, 2048, 768], P('ep', 'dp')
- grad_down: float32 [16, 768, 2048], P('ep', None, 'dp')
- clip_factor: float32 [32], replicated
Inputs may be any that keep to these rules, and one draw needn't show every extreme that they name: `deal_order`: each aligned block of 128 entries is a permutation of that block's own row numbers. `seq_lengths`: each device's 3 lengths sum to 112, and the longest is exactly 80. `expert_ids`: A row names 8 different experts; within the rows of one device no expert is named more than 80 times, a bound that some block reaches.
All inputs are finite; a program needn't handle non-finite values.
Results may differ from a plain program's by a relative error of at most 0.017.
Values may be sent and summed in bfloat16 or wider, within the bound.
A program may use at most 320 MiB of HBM per device.

v0:
```python
import jax
import jax.numpy as jnp
from jax import lax
from jax.sharding import PartitionSpec as P

epsilon = 1e-06
theta_base = 1000000.0
masked_fill = -1e30


def rms_scale(values):
    return lax.rsqrt(jnp.mean(values * values, axis=-1, keepdims=True) + epsilon)


def rotate_half(values):
    half_dim = values.shape[-1] // 2
    return jnp.concatenate([-values[..., half_dim:], values[..., :half_dim]], axis=-1)


def rotate(values, cosine_table, sine_table):
    return values * cosine_table + rotate_half(values) * sine_table


def rotate_back(values, cosine_table, sine_table):
    scaled = values * sine_table
    half_dim = values.shape[-1] // 2
    turned = jnp.concatenate([scaled[..., half_dim:], -scaled[..., :half_dim]], axis=-1)
    return values * cosine_table + turned


def norm_back(grad_unit, unit_rows, inv_root):
    return inv_root * (
        grad_unit - unit_rows * jnp.mean(grad_unit * unit_rows, axis=-1, keepdims=True)
    )


def contract(left_side, right_side, pattern):
    return jnp.einsum(pattern, left_side, right_side, preferred_element_type=jnp.float32)


def layout(lens_row, tok_count):
    seq_ends = jnp.cumsum(lens_row)
    row_index = jnp.arange(tok_count, dtype=jnp.int32)
    segment = jnp.sum((row_index[:, None] >= seq_ends[None, :]).astype(jnp.int32), axis=1)
    starts_all = jnp.concatenate([jnp.zeros((1,), jnp.int32), seq_ends])
    seg_hot = segment[:, None] == jnp.arange(starts_all.shape[0], dtype=jnp.int32)[None, :]
    first_row = jnp.sum(jnp.where(seg_hot, starts_all[None, :], 0), axis=1)
    position = row_index - first_row
    valid_row = segment < lens_row.shape[0]
    allowed = (segment[:, None] == segment[None, :]) & (row_index[None, :] <= row_index[:, None])
    return (position, valid_row, allowed)


def rotary_tables(position, head_dim):
    half_dim = head_dim // 2
    frequency = theta_base ** (-(jnp.arange(half_dim, dtype=jnp.float32) * 2.0) / head_dim)
    angles = position.astype(jnp.float32)[:, None] * frequency[None, :]
    angles = jnp.concatenate([angles, angles], axis=-1)
    return (jnp.cos(angles), jnp.sin(angles))


def per_device(
    hidden_in,
    cotangent,
    deal_order,
    seq_lengths,
    expert_ids,
    w_query,
    w_key,
    w_value,
    w_out,
    w_router,
    gain_attn,
    gain_moe,
    gain_query,
    gain_key,
    w_gate,
    w_up,
    w_down,
    clip_threshold,
):
    tok_count = hidden_in.shape[0]
    model_width = hidden_in.shape[1]
    head_dim = gain_query.shape[0]
    local_order = deal_order % tok_count
    position, valid_row, allowed = layout(seq_lengths[0], tok_count)
    valid_col = valid_row.astype(jnp.float32)[:, None]
    cosine_table, sine_table = rotary_tables(position, head_dim)
    cosine_query = cosine_table[:, None, None, :]
    sine_query = sine_table[:, None, None, :]
    cosine_key = cosine_table[:, None, :]
    sine_key = sine_table[:, None, :]
    attn_params = (
        lax.all_gather(w_query, ("dp", "ep"), axis=0, tiled=True),
        lax.all_gather(w_key, ("dp", "ep"), axis=0, tiled=True),
        lax.all_gather(w_value, ("dp", "ep"), axis=0, tiled=True),
        lax.all_gather(w_out, ("dp", "ep"), axis=0, tiled=True),
        lax.all_gather(w_router, ("dp", "ep"), axis=0, tiled=True),
        lax.all_gather(gain_attn, ("dp", "ep"), axis=0, tiled=True),
        lax.all_gather(gain_moe, ("dp", "ep"), axis=0, tiled=True),
    )
    expert_params = (
        lax.all_gather(w_gate, "dp", axis=1, tiled=True),
        lax.all_gather(w_up, "dp", axis=1, tiled=True),
        lax.all_gather(w_down, "dp", axis=2, tiled=True),
    )
    query_full, key_full, value_full, out_full, router_full, gain_attn_full, gain_moe_full = (
        attn_params
    )
    gate_full, up_full, down_full = expert_params
    head_count = query_full.shape[1] // head_dim
    kv_count = key_full.shape[1] // head_dim
    group_size = head_count // kv_count
    experts = router_full.shape[1]
    top_count = expert_ids.shape[1]
    exp_local = w_gate.shape[0]
    ep_count = lax.axis_size("ep")
    capacity = (tok_count * top_count * 5 + 4 * experts - 1) // (4 * experts)
    score_scale = head_dim ** (-0.5)
    resid_in = hidden_in[local_order].astype(jnp.float32)
    inv_one = rms_scale(resid_in)
    unit_one = resid_in * inv_one
    gain_one = gain_attn_full.astype(jnp.float32)
    normed_in = (unit_one * gain_one).astype(jnp.bfloat16)
    query_raw = jnp.dot(normed_in, query_full, preferred_element_type=jnp.float32).reshape(
        tok_count, kv_count, group_size, head_dim
    )
    key_raw = jnp.dot(normed_in, key_full, preferred_element_type=jnp.float32).reshape(
        tok_count, kv_count, head_dim
    )
    value_rows = (
        jnp.dot(normed_in, value_full, preferred_element_type=jnp.float32)
        .astype(jnp.bfloat16)
        .reshape(tok_count, kv_count, head_dim)
    )
    inv_query = rms_scale(query_raw)
    unit_query = query_raw * inv_query
    gain_query_f = gain_query.astype(jnp.float32)
    query_rot = rotate(unit_query * gain_query_f, cosine_query, sine_query).astype(jnp.bfloat16)
    inv_key = rms_scale(key_raw)
    unit_key = key_raw * inv_key
    gain_key_f = gain_key.astype(jnp.float32)
    key_rot = rotate(unit_key * gain_key_f, cosine_key, sine_key).astype(jnp.bfloat16)
    scores = contract(query_rot, key_rot, "tkgd,ukd->kgtu") * score_scale
    masked = jnp.where(allowed, scores, masked_fill)
    row_top = jnp.max(masked, axis=-1, keepdims=True)
    exponent = jnp.exp(masked - row_top)
    row_total = jnp.sum(exponent, axis=-1, keepdims=True)
    log_total = row_top + jnp.log(row_total)
    probs_low = (exponent / row_total).astype(jnp.bfloat16)
    mixed_heads = (
        contract(probs_low, value_rows, "kgtu,ukd->tkgd")
        .astype(jnp.bfloat16)
        .reshape(tok_count, head_count * head_dim)
    )
    resid_mid = resid_in + jnp.dot(mixed_heads, out_full, preferred_element_type=jnp.float32)
    largest_local = jnp.max(
        jnp.where(allowed & valid_row[:, None], scores, masked_fill), axis=(2, 3)
    ).reshape(head_count)
    largest = lax.pmax(largest_local, ("dp", "ep"))
    clip_factor = jnp.sqrt(clip_threshold / jnp.maximum(largest, clip_threshold))
    inv_two = rms_scale(resid_mid)
    unit_two = resid_mid * inv_two
    gain_two = gain_moe_full.astype(jnp.float32)
    normed_mid = (unit_two * gain_two).astype(jnp.bfloat16)
    logits = jnp.dot(normed_mid, router_full, preferred_element_type=jnp.float32)
    choose = expert_ids[:, :, None] == jnp.arange(experts, dtype=jnp.int32)[None, None, :]
    picked = jnp.sum(jnp.where(choose, logits[:, None, :], 0.0), axis=2)
    gate_weights = jax.nn.softmax(picked, axis=-1)
    flat_ids = expert_ids.reshape(-1)
    flat_hot = (flat_ids[:, None] == jnp.arange(experts, dtype=jnp.int32)[None, :]).astype(
        jnp.int32
    )
    slot_rank = jnp.sum((jnp.cumsum(flat_hot, axis=0) - 1) * flat_hot, axis=1)
    slot_index = flat_ids * capacity + slot_rank
    pair_token = jnp.arange(tok_count * top_count, dtype=jnp.int32) // top_count
    send_rows = (
        jnp.zeros((experts * capacity, model_width), jnp.bfloat16)
        .at[slot_index]
        .set(normed_mid[pair_token])
    )
    send_rows = send_rows.reshape(ep_count, exp_local, capacity, model_width)
    arrived = lax.all_to_all(send_rows, "ep", split_axis=0, concat_axis=0, tiled=True)
    gate_part = contract(arrived, gate_full, "secd,edf->secf")
    up_part = contract(arrived, up_full, "secd,edf->secf")
    hidden_mid = (jax.nn.silu(gate_part) * up_part).astype(jnp.bfloat16)
    produced = contract(hidden_mid, down_full, "secf,efd->secd").astype(jnp.bfloat16)
    returned = lax.all_to_all(produced, "ep", split_axis=0, concat_axis=0, tiled=True)
    returned, arrived, gate_part, up_part = (returned, arrived, gate_part, up_part)
    pair_out = (
        returned.reshape(experts * capacity, model_width)[slot_index]
        .reshape(tok_count, top_count, model_width)
        .astype(jnp.float32)
    )
    resid_out = resid_mid + jnp.sum(gate_weights[:, :, None] * pair_out, axis=1)
    out_rows = (resid_out * valid_col).astype(jnp.bfloat16)
    block_out = jnp.zeros_like(out_rows).at[local_order].set(out_rows)
    attn_params = (
        lax.all_gather(w_query, ("dp", "ep"), axis=0, tiled=True),
        lax.all_gather(w_key, ("dp", "ep"), axis=0, tiled=True),
        lax.all_gather(w_value, ("dp", "ep"), axis=0, tiled=True),
        lax.all_gather(w_out, ("dp", "ep"), axis=0, tiled=True),
        lax.all_gather(w_router, ("dp", "ep"), axis=0, tiled=True),
        lax.all_gather(gain_attn, ("dp", "ep"), axis=0, tiled=True),
        lax.all_gather(gain_moe, ("dp", "ep"), axis=0, tiled=True),
    )
    expert_params = (
        lax.all_gather(w_gate, "dp", axis=1, tiled=True),
        lax.all_gather(w_up, "dp", axis=1, tiled=True),
        lax.all_gather(w_down, "dp", axis=2, tiled=True),
    )
    query_full, key_full, value_full, out_full, router_full, gain_attn_full, gain_moe_full = (
        attn_params
    )
    gate_full, up_full, down_full = expert_params
    grad_mid_out = cotangent[local_order].astype(jnp.float32) * valid_col
    grad_gates = jnp.sum(grad_mid_out[:, None, :] * pair_out, axis=2)
    grad_pair = (gate_weights[:, :, None] * grad_mid_out[:, None, :]).astype(jnp.bfloat16)
    send_grads = (
        jnp.zeros((experts * capacity, model_width), jnp.bfloat16)
        .at[slot_index]
        .set(grad_pair.reshape(-1, model_width))
    )
    send_grads = send_grads.reshape(ep_count, exp_local, capacity, model_width)
    grad_arrived = lax.all_to_all(send_grads, "ep", split_axis=0, concat_axis=0, tiled=True)
    grad_hidden = contract(grad_arrived, down_full, "secd,efd->secf")
    sigmoid_gate = jax.nn.sigmoid(gate_part)
    silu_gate = jax.nn.silu(gate_part)
    grad_gate_part = (
        grad_hidden * up_part * sigmoid_gate * (1.0 + gate_part * (1.0 - sigmoid_gate))
    ).astype(jnp.bfloat16)
    grad_up_part = (grad_hidden * silu_gate).astype(jnp.bfloat16)
    grad_rows = (
        contract(grad_gate_part, gate_full, "secf,edf->secd")
        + contract(grad_up_part, up_full, "secf,edf->secd")
    ).astype(jnp.bfloat16)
    grad_back = lax.all_to_all(grad_rows, "ep", split_axis=0, concat_axis=0, tiled=True)
    hidden_mid = (silu_gate * up_part).astype(jnp.bfloat16)
    grad_gate_w = contract(arrived, grad_gate_part, "secd,secf->edf")
    grad_up_w = contract(arrived, grad_up_part, "secd,secf->edf")
    grad_down_w = contract(hidden_mid, grad_arrived, "secf,secd->efd")
    grad_gate, grad_up, grad_down = (
        lax.psum_scatter(
            grad_gate_w.astype(jnp.bfloat16), "dp", scatter_dimension=1, tiled=True
        ).astype(jnp.float32),
        lax.psum_scatter(
            grad_up_w.astype(jnp.bfloat16), "dp", scatter_dimension=1, tiled=True
        ).astype(jnp.float32),
        lax.psum_scatter(
            grad_down_w.astype(jnp.bfloat16), "dp", scatter_dimension=2, tiled=True
        ).astype(jnp.float32),
    )
    mean_term = jnp.sum(gate_weights * grad_gates, axis=1, keepdims=True)
    grad_picked = gate_weights * (grad_gates - mean_term)
    grad_logits = jnp.sum(jnp.where(choose, grad_picked[:, :, None], 0.0), axis=1).astype(
        jnp.bfloat16
    )
    grad_router_w = contract(normed_mid, grad_logits, "td,te->de")
    pair_grads = (
        grad_back.reshape(experts * capacity, model_width)[slot_index]
        .reshape(tok_count, top_count, model_width)
        .astype(jnp.float32)
    )
    grad_normed_mid = jnp.sum(pair_grads, axis=1) + contract(grad_logits, router_full, "te,de->td")
    grad_gain_moe_w = jnp.sum(grad_normed_mid * unit_two, axis=0)
    grad_mid = grad_mid_out + norm_back(grad_normed_mid * gain_two, unit_two, inv_two)
    grad_branch = grad_mid.astype(jnp.bfloat16)
    grad_out_w = contract(mixed_heads, grad_branch, "tq,td->qd")
    grad_mixed = (
        contract(grad_branch, out_full, "td,qd->tq")
        .astype(jnp.bfloat16)
        .reshape(tok_count, kv_count, group_size, head_dim)
    )
    scores_again = contract(query_rot, key_rot, "tkgd,ukd->kgtu") * score_scale
    probs_back = jnp.exp(jnp.where(allowed, scores_again, masked_fill) - log_total)
    grad_value_rows = contract(
        probs_back.astype(jnp.bfloat16), grad_mixed, "kgtu,tkgd->ukd"
    ).astype(jnp.bfloat16)
    grad_probs = contract(grad_mixed, value_rows, "tkgd,ukd->kgtu")
    grad_scores = (
        probs_back * (grad_probs - jnp.sum(probs_back * grad_probs, axis=-1, keepdims=True))
    ).astype(jnp.bfloat16)
    grad_query_rot = contract(grad_scores, key_rot, "kgtu,ukd->tkgd") * score_scale
    grad_key_rot = contract(grad_scores, query_rot, "kgtu,tkgd->ukd") * score_scale
    grad_query_normed = rotate_back(grad_query_rot, cosine_query, sine_query)
    grad_key_normed = rotate_back(grad_key_rot, cosine_key, sine_key)
    grad_gain_q = jnp.sum(grad_query_normed * unit_query, axis=(0, 1, 2))
    grad_gain_k = jnp.sum(grad_key_normed * unit_key, axis=(0, 1))
    grad_query_raw = (
        norm_back(grad_query_normed * gain_query_f, unit_query, inv_query)
        .astype(jnp.bfloat16)
        .reshape(tok_count, head_count * head_dim)
    )
    grad_key_raw = (
        norm_back(grad_key_normed * gain_key_f, unit_key, inv_key)
        .astype(jnp.bfloat16)
        .reshape(tok_count, kv_count * head_dim)
    )
    grad_value_flat = grad_value_rows.reshape(tok_count, kv_count * head_dim)
    grad_query_w = contract(normed_in, grad_query_raw, "td,tq->dq")
    grad_key_w = contract(normed_in, grad_key_raw, "td,tq->dq")
    grad_value_w = contract(normed_in, grad_value_flat, "td,tq->dq")
    grad_normed_in = (
        contract(grad_query_raw, query_full, "tq,dq->td")
        + contract(grad_key_raw, key_full, "tq,dq->td")
        + contract(grad_value_flat, value_full, "tq,dq->td")
    )
    grad_gain_attn_w = jnp.sum(grad_normed_in * unit_one, axis=0)
    grad_resid_in = grad_mid + norm_back(grad_normed_in * gain_one, unit_one, inv_one)
    grad_input = jnp.zeros_like(grad_resid_in).at[local_order].set(grad_resid_in)
    grad_sums = (
        lax.psum_scatter(grad_query_w, ("dp", "ep"), scatter_dimension=0, tiled=True),
        lax.psum_scatter(grad_key_w, ("dp", "ep"), scatter_dimension=0, tiled=True),
        lax.psum_scatter(grad_value_w, ("dp", "ep"), scatter_dimension=0, tiled=True),
        lax.psum_scatter(grad_out_w, ("dp", "ep"), scatter_dimension=0, tiled=True),
        lax.psum_scatter(grad_router_w, ("dp", "ep"), scatter_dimension=0, tiled=True),
        lax.psum_scatter(grad_gain_attn_w, ("dp", "ep"), scatter_dimension=0, tiled=True),
        lax.psum_scatter(grad_gain_moe_w, ("dp", "ep"), scatter_dimension=0, tiled=True),
    )
    gain_sums = lax.psum((grad_gain_q, grad_gain_k), ("dp", "ep"))
    return (
        block_out,
        grad_input,
        grad_sums[0],
        grad_sums[1],
        grad_sums[2],
        grad_sums[3],
        grad_sums[4],
        grad_sums[5],
        grad_sums[6],
        gain_sums[0],
        gain_sums[1],
        grad_gate,
        grad_up,
        grad_down,
        clip_factor,
    )


def solution(mesh):
    placed = (
        P(("dp", "ep"), None),
        P(("dp", "ep"), None),
        P(("dp", "ep")),
        P(("dp", "ep"), None),
        P(("dp", "ep"), None),
        P(("dp", "ep"), None),
        P(("dp", "ep"), None),
        P(("dp", "ep"), None),
        P(("dp", "ep"), None),
        P(("dp", "ep"), None),
        P(("dp", "ep")),
        P(("dp", "ep")),
        P(),
        P(),
        P("ep", "dp", None),
        P("ep", "dp", None),
        P("ep", None, "dp"),
        P(),
    )
    return jax.shard_map(
        per_device,
        mesh=mesh,
        in_specs=placed,
        out_specs=(
            P(("dp", "ep"), None),
            P(("dp", "ep"), None),
            P(("dp", "ep"), None),
            P(("dp", "ep"), None),
            P(("dp", "ep"), None),
            P(("dp", "ep"), None),
            P(("dp", "ep"), None),
            P(("dp", "ep")),
            P(("dp", "ep")),
            P(),
            P(),
            P("ep", "dp", None),
            P("ep", "dp", None),
            P("ep", None, "dp"),
            P(),
        ),
        check_vma=False,
    )
```

profile of v0, /device:TPU:1, one launch (start us, length us, event | category | flops | bytes accessed | tf_op | source)
XLA Modules:
  0.0 2779.5 jit_solution(17452074020429287070)
XLA Ops:
  12.8 40.6 %all-reduce.5 = (bf16[2048]{0:T(1024)(128)(2,1)S(1)}, bf16[2048]{0:T(1024)(128)(2,1)S(1)}) all-reduce(bf16[2048]{0:T(1024)(128)(2,1)S(1)} %dynamic-update-slice, bf16[2048]{0:T(1024)(128)(2,1)S(1)} %dynamic-update-slice.1), channel_id=1, replica_groups=mesh['dp'=8,'ep'=4] {'dp','ep'}, use_global_device_ids=true, to_apply=%add | all-reduce | flops 4096 | bytes 16384
  72.4 55.3 %all-gather.9.cloned.1.call-done = bf16[2048,512]{1,0:T(8,128)(2,1)} async-done(((bf16[64,512]{1,0:T(8,128)(2,1)}), bf16[2048,512]{1,0:T(8,128)(2,1)}) %all-gather.9.cloned.1.call-update) | async-done | bytes 2097168 | tf_op jit(solution)/shard_map/all_gather | solution.py:96
  130.1 113.7 %all-gather.13.cloned.1.call-done = bf16[2048,4096]{1,0:T(8,128)(2,1)} async-done(((bf16[64,4096]{1,0:T(8,128)(2,1)}), bf16[2048,4096]{1,0:T(8,128)(2,1)}) %all-gather.13.cloned.1.call-update) | async-done | bytes 16777232 | tf_op jit(solution)/shard_map/all_gather | solution.py:94
  264.2 94.9 %all-gather.15.cloned.1.call-done = bf16[4096,2048]{1,0:T(8,128)(2,1)} async-done(((bf16[128,2048]{1,0:T(8,128)(2,1)}), bf16[4096,2048]{1,0:T(8,128)(2,1)}) %all-gather.15.cloned.1.call-update) | async-done | bytes 16777232 | tf_op jit(solution)/shard_map/all_gather | solution.py:97
  367.5 23.5 scatter_custom_fusion
  396.7 92.4 %all-gather = bf16[32,64,16]{1,2,0:T(8,128)(2,1)S(1)} all-gather(bf16[1,64,16]{1,2,0:T(8,128)(2,1)S(1)} %bitcast.241), channel_id=1, replica_groups=mesh['dp'=8,'ep'=4] {'dp','ep'}, dimensions={0}, use_global_device_ids=true | all-gather | bytes 67584 | tf_op jit(solution)/shard_map/all_gather | solution.py:98
  508.3 26.8 all-gather.17.cloned.1.call-done
  535.1 12.3 fusion.6
  547.3 164.1 %all-gather.19.cloned.1.call-done = bf16[4,2048,768]{2,1,0:T(8,128)(2,1)} async-done(((bf16[4,256,768]{2,1,0:T(8,128)(2,1)}), bf16[4,2048,768]{2,1,0:T(8,128)(2,1)}) %all-gather.19.cloned.1.call-update) | async-done | bytes 12582928 | tf_op jit(solution)/shard_map/all_gather | solution.py:104
  711.4 12.3 fusion.2
  723.7 164.1 %all-gather.21.cloned.1.call-done = bf16[4,768,2048]{2,1,0:T(8,128)(2,1)} async-done(((bf16[4,768,256]{2,1,0:T(8,128)(2,1)}), bf16[4,768,2048]{2,1,0:T(8,128)(2,1)}) %all-gather.21.cloned.1.call-update) | async-done | bytes 12582928 | tf_op jit(solution)/shard_map/all_gather | solution.py:105
  887.8 13.9 fusion.32
  920.3 58.5 %all-to-all-done.1 = bf16[4,4,80,2048]{3,2,1,0:T(8,128)(2,1)} async-done(((bf16[4,4,80,2048]{3,2,1,0:T(8,128)(2,1)}), bf16[4,4,80,2048]{3,2,1,0:T(8,128)(2,1)}, u32[]{:S(2)}, u32[]{:S(2)}) %all-to-all-start.1) | async-done | bytes 5242912 | tf_op jit(solution)/shard_map/all_to_all | solution.py:188
  978.8 12.0 gather_fusion.1
  998.2 12.5 bitcast_convert_fusion
  1010.7 12.4 bitcast_convert_fusion.2
  1023.2 11.9 bitcast_convert_fusion.1
  1035.1 13.4 fusion
  1048.5 16.4 fusion.15
  1076.6 62.6 %all-to-all-done.3 = bf16[4,4,80,2048]{3,2,1,0:T(8,128)(2,1)} async-done(((bf16[4,4,80,2048]{3,2,1,0:T(8,128)(2,1)}), bf16[4,4,80,2048]{3,2,1,0:T(8,128)(2,1)}, u32[]{:S(2)}, u32[]{:S(2)}) %all-to-all-start.3) | async-done | bytes 5242912 | tf_op jit(solution)/shard_map/all_to_all | solution.py:237
  1139.3 13.2 gather_fusion.3
  1159.6 12.9 fusion.55
  1188.7 13.7 fusion.78
  1208.2 13.5 fusion.105
  1222.5 40.5 %pmax.7 = f32[32]{0:T(128)S(1)} all-reduce(f32[32]{0:T(128)S(1)} %reshape.514), channel_id=1, replica_groups=mesh['dp'=8,'ep'=4] {'dp','ep'}, use_global_device_ids=true, to_apply=%region_46.47 | all-reduce | flops 32 | bytes 256 | tf_op jit(solution)/shard_map/pmax | solution.py:160
  1279.6 43.4 %all-reduce.4 = (f32[2048]{0:T(1024)S(1)}, f32[2048]{0:T(1024)S(1)}, f32[128]{0:T(128)}, f32[128]{0:T(128)}) all-reduce(f32[2048]{0:T(1024)S(1)} %get-tuple-element.23, f32[2048]{0:T(1024)S(1)} %get-tuple-element.19, f32[128]{0:T(128)S(1)} %get-tuple-element.15, ...), channel_id=7, replica_groups=mesh['dp'=8,'ep'=4] {'dp','ep'}, use_global_device_ids=true, to_apply=%region_35.36.clone | all-reduce | flops 4352 | bytes 34816
  1346.0 206.6 %reduce-scatter.19.cloned.1.call-done = bf16[4,256,768]{2,1,0:T(8,128)(2,1)} async-done(((bf16[4,2048,768]{2,1,0:T(8,128)(2,1)}), bf16[4,256,768]{2,1,0:T(8,128)(2,1)}) %reduce-scatter.19.cloned.1.call-update) | async-done | bytes 1572880 | tf_op jit(solution)/shard_map/reduce_scatter | solution.py:243
  1555.9 206.8 %reduce-scatter.21.cloned.1.call-done = bf16[4,256,768]{2,1,0:T(8,128)(2,1)} async-done(((bf16[4,2048,768]{2,1,0:T(8,128)(2,1)}), bf16[4,256,768]{2,1,0:T(8,128)(2,1)}) %reduce-scatter.21.cloned.1.call-update) | async-done | bytes 1572880 | tf_op jit(solution)/shard_map/reduce_scatter | solution.py:246
  1766.0 136.2 %reduce-scatter.15.cloned.1.call-done = f32[64,512]{1,0:T(8,128)} async-done(((f32[2048,512]{1,0:T(8,128)}), f32[64,512]{1,0:T(8,128)}) %reduce-scatter.15.cloned.1.call-update) | async-done | bytes 131088 | tf_op jit(solution)/shard_map/reduce_scatter | solution.py:314
  1902.2 141.5 %reduce-scatter.13.cloned.1.call-done = f32[64,512]{1,0:T(8,128)} async-done(((f32[2048,512]{1,0:T(8,128)}), f32[64,512]{1,0:T(8,128)}) %reduce-scatter.13.cloned.1.call-update) | async-done | bytes 131088 | tf_op jit(solution)/shard_map/reduce_scatter | solution.py:313
  2043.7 364.0 %reduce-scatter.17.cloned.1.call-done = f32[128,2048]{1,0:T(8,128)} async-done(((f32[4096,2048]{1,0:T(8,128)}), f32[128,2048]{1,0:T(8,128)}) %reduce-scatter.17.cloned.1.call-update) | async-done | bytes 1048592 | tf_op jit(solution)/shard_map/reduce_scatter | solution.py:315
  2407.7 364.8 %reduce-scatter.11.cloned.1.call-done = f32[64,4096]{1,0:T(8,128)} async-done(((f32[2048,4096]{1,0:T(8,128)}), f32[64,4096]{1,0:T(8,128)}) %reduce-scatter.11.cloned.1.call-update) | async-done | bytes 1048592 | tf_op jit(solution)/shard_map/reduce_scatter | solution.py:312
  (276 shorter events, 193.4 us)
Async XLA Ops:
  7.3 62.5 %all-gather.11.cloned.1.call-start = ((), (), s32[]{:S(2)}) async-start(), calls=%async_computation.13 | async-start | bytes 2162688 | tf_op jit(solution)/shard_map/all_gather | solution.py:95
  8.0 119.7 %all-gather.9.cloned.1.call-start = ((), (), s32[]{:S(2)}) async-start(), calls=%async_computation.12 | async-start | bytes 2162688 | tf_op jit(solution)/shard_map/all_gather | solution.py:96
  8.8 235.1 %all-gather.13.cloned.1.call-start = ((), (), s32[]{:S(2)}) async-start(), calls=%async_computation.14 | async-start | bytes 17301504 | tf_op jit(solution)/shard_map/all_gather | solution.py:94
  9.5 349.6 %all-gather.15.cloned.1.call-start = ((), (), s32[]{:S(2)}) async-start(), calls=%async_computation.15 | async-start | bytes 17301504 | tf_op jit(solution)/shard_map/all_gather | solution.py:97
  10.1 525.0 %all-gather.17.cloned.1.call-start = ((), (), s32[]{:S(2)}) async-start(), calls=%async_computation.16 | async-start | bytes 14155776 | tf_op jit(solution)/shard_map/all_gather | solution.py:103
  10.7 700.8 %all-gather.19.cloned.1.call-start = ((), (), s32[]{:S(2)}) async-start(), calls=%async_computation.17 | async-start | bytes 14155776 | tf_op jit(solution)/shard_map/all_gather | solution.py:104
  11.2 876.5 %all-gather.21.cloned.1.call-start = ((), (), s32[]{:S(2)}) async-start(), calls=%async_computation.18 | async-start | bytes 14155776 | tf_op jit(solution)/shard_map/all_gather | solution.py:105
  53.5 190.4 %copy-start.25 = (f32[2048]{0:T(1024)}, f32[2048]{0:T(1024)S(1)}, u32[]{:S(2)}) copy-start(f32[2048]{0:T(1024)S(1)} %convert_element_type.159) | copy-start | bytes 24580
  53.5 206.3 %copy-start.45 = (f32[128]{0:T(128)}, f32[128]{0:T(128)S(1)}, u32[]{:S(2)}) copy-start(f32[128]{0:T(128)S(1)} %convert_element_type.166) | copy-start | bytes 1540
  60.3 298.8 %copy-start.2 = (bf16[128,2048]{1,0:T(8,128)(2,1)}, bf16[128,2048]{1,0:T(8,128)(2,1)S(1)}, u32[]{:S(2)}) copy-start(bf16[128,2048]{1,0:T(8,128)(2,1)S(1)} %gather_fusion) | copy-start | bytes 1572868
  61.9 182.0 %copy-start.40 = (f32[128]{0:T(128)}, f32[128]{0:T(128)S(1)}, u32[]{:S(2)}) copy-start(f32[128]{0:T(128)S(1)} %add_rsqrt_fusion.3) | copy-start | bytes 1540
  62.0 201.4 %copy-start.35 = (pred[128,128]{0,1:T(8,128)(4,1)}, pred[128,128]{0,1:T(8,128)(4,1)S(1)}, u32[]{:S(2)}) copy-start(pred[128,128]{0,1:T(8,128)(4,1)S(1)} %get-tuple-element.54) | copy-start | bytes 49156
  72.1 180.0 %copy-start.20 = (f32[128,4,128]{0,2,1:T(8,128)}, f32[128,4,128]{0,2,1:T(8,128)S(1)}, u32[]{:S(2)}) copy-start(f32[128,4,128]{0,2,1:T(8,128)S(1)} %copy.200) | copy-start | bytes 786436
  129.9 133.6 %copy-start.31 = (bf16[128,4,128]{2,1,0:T(4,128)(2,1)}, bf16[128,4,128]{2,1,0:T(4,128)(2,1)S(1)}, u32[]{:S(2)}) copy-start(bf16[128,4,128]{2,1,0:T(4,128)(2,1)S(1)} %reshape.499) | copy-start | bytes 393220
  129.9 122.2 %copy-start.38 = (f32[128,4]{0,1:T(4,128)}, f32[128,4]{0,1:T(4,128)S(1)}, u32[]{:S(2)}) copy-start(f32[128,4]{0,1:T(4,128)S(1)} %add_rsqrt_fusion.1) | copy-start | bytes 6148
  130.1 130.3 %copy-start.27 = (bf16[128,4,128,1]{0,2,3,1:T(8,128)(2,1)}, bf16[128,4,128,1]{0,2,3,1:T(8,128)(2,1)S(1)}, u32[]{:S(2)}) copy-start(bf16[128,4,128,1]{0,2,3,1:T(8,128)(2,1)S(1)} %fusion.82) | copy-start | bytes 393220
  264.2 103.1 %copy-start.18 = (bf16[4,128,8,128]{3,1,2,0:T(8,128)(2,1)}, bf16[4,128,8,128]{3,1,2,0:T(8,128)(2,1)S(1)}, u32[]{:S(2)}) copy-start(bf16[4,128,8,128]{3,1,2,0:T(8,128)(2,1)S(1)} %convolution_convert_fusion.1) | copy-start | bytes 3145732
  367.3 790.8 %copy-start.9 = (f32[128,2048]{1,0:T(8,128)}, f32[128,2048]{1,0:T(8,128)S(1)}, u32[]{:S(2)}) copy-start(f32[128,2048]{1,0:T(8,128)S(1)} %get-tuple-element.59) | copy-start | bytes 3145732
  391.0 98.3 %copy-start.6 = (bf16[128,2048]{1,0:T(8,128)(2,1)S(1)}, bf16[128,2048]{1,0:T(8,128)(2,1)}, u32[]{:S(2)}) copy-start(bf16[128,2048]{1,0:T(8,128)(2,1)} %param.19) | copy-start | bytes 1572868
  391.0 111.9 %all-to-all-start = ((bf16[4,4,80,2048]{3,2,1,0:T(8,128)(2,1)}), bf16[4,4,80,2048]{3,2,1,0:T(8,128)(2,1)}, u32[]{:S(2)}, u32[]{:S(2)}) async-start(bf16[4,4,80,2048]{3,2,1,0:T(8,128)(2,1)} %bitcast.218), calls=%async_computation | async-start | bytes 10485760 | tf_op jit(solution)/shard_map/all_to_all | solution.py:183
  502.8 384.9 %all-to-all-start.2 = ((bf16[4,4,80,2048]{3,2,1,0:T(8,128)(2,1)}), bf16[4,4,80,2048]{3,2,1,0:T(8,128)(2,1)}, u32[]{:S(2)}, u32[]{:S(2)}) async-start(bf16[4,4,80,2048]{3,2,1,0:T(8,128)(2,1)} %bitcast.219), calls=%async_computation.2 | async-start | bytes 10485760 | tf_op jit(solution)/shard_map/all_to_all | solution.py:225
  913.8 65.0 %all-to-all-start.1 = ((bf16[4,4,80,2048]{3,2,1,0:T(8,128)(2,1)}), bf16[4,4,80,2048]{3,2,1,0:T(8,128)(2,1)}, u32[]{:S(2)}, u32[]{:S(2)}) async-start(bf16[4,4,80,2048]{3,2,1,0:T(8,128)(2,1)} %copy.216), calls=%async_computation.1 | async-start | bytes 10485760 | tf_op jit(solution)/shard_map/all_to_all | solution.py:188
  920.3 410.1 %reduce-scatter.25.cloned.1.call-start = ((), (), s32[]{:S(2)}) async-start(), calls=%async_computation.26 | async-start | bytes 1081344
  998.1 344.5 %reduce-scatter.23.cloned.1.call-start = ((), (), s32[]{:S(2)}) async-start(), calls=%async_computation.25 | async-start | bytes 14155776 | tf_op jit(solution)/shard_map/reduce_scatter | solution.py:249
  1010.6 541.9 %reduce-scatter.19.cloned.1.call-start = ((), (), s32[]{:S(2)}) async-start(), calls=%async_computation.23 | async-start | bytes 14155776 | tf_op jit(solution)/shard_map/reduce_scatter | solution.py:243
  1023.1 739.6 %reduce-scatter.21.cloned.1.call-start = ((), (), s32[]{:S(2)}) async-start(), calls=%async_computation.24 | async-start | bytes 14155776 | tf_op jit(solution)/shard_map/reduce_scatter | solution.py:246
  1070.7 68.6 %all-to-all-start.3 = ((bf16[4,4,80,2048]{3,2,1,0:T(8,128)(2,1)}), bf16[4,4,80,2048]{3,2,1,0:T(8,128)(2,1)}, u32[]{:S(2)}, u32[]{:S(2)}) async-start(bf16[4,4,80,2048]{3,2,1,0:T(8,128)(2,1)} %copy.219), calls=%async_computation.3 | async-start | bytes 10485760 | tf_op jit(solution)/shard_map/all_to_all | solution.py:237
  1076.6 825.6 %reduce-scatter.15.cloned.1.call-start = ((), (), s32[]{:S(2)}) async-start(), calls=%async_computation.21 | async-start | bytes 4325376 | tf_op jit(solution)/shard_map/reduce_scatter | solution.py:314
  1184.7 859.1 %reduce-scatter.13.cloned.1.call-start = ((), (), s32[]{:S(2)}) async-start(), calls=%async_computation.20 | async-start | bytes 4325376 | tf_op jit(solution)/shard_map/reduce_scatter | solution.py:313
  1188.7 1219.0 %reduce-scatter.17.cloned.1.call-start = ((), (), s32[]{:S(2)}) async-start(), calls=%async_computation.22 | async-start | bytes 34603008 | tf_op jit(solution)/shard_map/reduce_scatter | solution.py:315
  1202.5 1570.0 %reduce-scatter.11.cloned.1.call-start = ((), (), s32[]{:S(2)}) async-start(), calls=%async_computation.19 | async-start | bytes 34603008 | tf_op jit(solution)/shard_map/reduce_scatter | solution.py:312
  1342.6 1430.0 %copy-start.1 = (bf16[128,2048]{1,0:T(8,128)(2,1)S(1)}, bf16[128,2048]{1,0:T(8,128)(2,1)}, u32[]{:S(2)}) copy-start(bf16[128,2048]{1,0:T(8,128)(2,1)} %param.18) | copy-start | bytes 1572868
  (43 other events, 619.8 us)
Sparse Core Ops, SparseCore 0:
  10.9 58.8 all-gather.10
  72.6 55.0 all-gather.8
  130.6 113.1 all-gather.12
  246.5 112.5 all-gather.14
  361.2 173.8 all-gather.16
  537.1 174.2 all-gather.18
  713.5 174.2 all-gather.20
  998.2 130.1 reduce-scatter.24
  1132.0 210.4 reduce-scatter.22
  1346.0 206.4 reduce-scatter.18
  1556.1 206.5 reduce-scatter.20
  1765.4 136.7 reduce-scatter.14
  1905.1 138.6 reduce-scatter.12
  2046.5 361.1 reduce-scatter.16
  2410.4 362.0 reduce-scatter.10
where the time goes:
time: 2790 us; the launch traced here: 2780 us
  waiting for transfers between devices  2180 us (78%)
  blocking collectives  217 us (8%)
  matrix products  205 us (7%)
  local copies, waits for them, and re-layouts  77.1 us (3%)
  other arithmetic  57.8 us (2%)
    reduce_scatter x1, waiting for transfers between devices, per_device(): lax.psum_scatter(grad_query_w, ('dp', 'ep'), scatter_dimension=0, tiled=T...  365 us
    reduce_scatter x1, waiting for transfers between devices, per_device(): lax.psum_scatter(grad_out_w, ('dp', 'ep'), scatter_dimension=0, tiled=True)  364 us
    reduce_scatter x1, waiting for transfers between devices, per_device(): lax.psum_scatter(grad_up_w.astype(jnp.bfloat16), 'dp', scatter_dimension=...  207 us
    reduce_scatter x1, waiting for transfers between devices, per_device(): lax.psum_scatter(grad_gate_w.astype(jnp.bfloat16), 'dp', scatter_dimensio...  207 us
    dot_general x24, matrix products, contract(): jnp.einsum(pattern, left_side, right_side, preferred_element_type=jnp.flo...  183 us
    all_gather x1, waiting for transfers between devices, per_device(): lax.all_gather(w_up, 'dp', axis=1, tiled=True)  164 us
    all_gather x1, waiting for transfers between devices, per_device(): lax.all_gather(w_down, 'dp', axis=2, tiled=True)  164 us
    reduce_scatter x1, waiting for transfers between devices, per_device(): lax.psum_scatter(grad_key_w, ('dp', 'ep'), scatter_dimension=0, tiled=True)  142 us
  transfers between devices with their start and end apart: 19, of which 16 were waited for; matrix products, arithmetic and copies ran while one was open for 10% of the time, Pallas kernels for 0%

commit v1 on v0

--- a/solution.py
+++ b/solution.py
@@ -1,6 +1,10 @@
+import functools
+
 import jax
 import jax.numpy as jnp
 from jax import lax
+from jax.experimental import pallas as pl
+from jax.experimental.pallas import tpu as pltpu
 from jax.sharding import PartitionSpec as P
 
 epsilon = 1e-06
@@ -337,6 +341,610 @@
     )
 
 
+MESH = pl.DeviceIdType.MESH
+
+
+def place():
+    dp = lax.axis_index("dp")
+    ep = lax.axis_index("ep")
+    z, y = dp // 2, dp % 2
+    x, c = ep // 2, ep % 2
+    first = (1 - c) * y + c * x
+    second = (1 - c) * x + c * y
+    return dp, ep, z, y, x, c, first, second
+
+
+def targets(dp, ep, z, y, x, c, nz):
+    up = (jnp.where(z < nz - 1, dp + 2, dp), ep)
+    down = (jnp.where(z > 0, dp - 2, dp), ep)
+    turn_y, turn_x = 1 - 2 * y, 2 - 4 * x
+    near = (dp + (1 - c) * turn_y, ep + c * turn_x)
+    far = (dp + c * turn_y, ep + (1 - c) * turn_x)
+    twin = (dp, ep + 1 - 2 * c)
+    return up, down, near, far, twin
+
+
+def slot(z, first, second, c):
+    return z * 8 + first * (4 - 2 * c) + second * (2 + 2 * c) + c
+
+
+def greet(nz, z, up, down, near, far, twin):
+    barrier = pltpu.get_barrier_semaphore()
+
+    @pl.when(z < nz - 1)
+    def _():
+        pl.semaphore_signal(barrier, inc=1, device_id=up, device_id_type=MESH)
+
+    @pl.when(z > 0)
+    def _():
+        pl.semaphore_signal(barrier, inc=1, device_id=down, device_id_type=MESH)
+
+    for other in (near, far, twin):
+        pl.semaphore_signal(barrier, inc=1, device_id=other, device_id_type=MESH)
+    peers = 3 + jnp.where(z < nz - 1, 1, 0) + jnp.where(z > 0, 1, 0)
+    pl.semaphore_wait(barrier, peers)
+
+
+def gather_kernel(nz, count, *refs):
+    ins = refs[:count]
+    outs = refs[count : 2 * count]
+    send_sem, recv_sem, own_sem = refs[2 * count :]
+    dp, ep, z, y, x, c, a, b = place()
+    up, down, near, far, twin = targets(dp, ep, z, y, x, c, nz)
+    ways = (up, down, near, far, twin)
+    greet(nz, z, up, down, near, far, twin)
+    mine = slot(z, a, b, c)
+    pending = []
+
+    def push(way, where, allowed=None, own=False):
+        for k in range(count):
+            copy = pltpu.make_async_remote_copy(
+                src_ref=ins[k] if own else outs[k].at[where],
+                dst_ref=outs[k].at[where],
+                send_sem=send_sem.at[k, way, where],
+                recv_sem=recv_sem.at[k, where],
+                device_id=ways[way],
+                device_id_type=MESH,
+            )
+            if allowed is None:
+                copy.start()
+            else:
+                pl.when(allowed)(copy.start)
+            pending.append((allowed, copy))
+
+    def arrive(where):
+        for k in range(count):
+            pltpu.make_async_remote_copy(
+                src_ref=outs[k].at[where],
+                dst_ref=outs[k].at[where],
+                send_sem=send_sem.at[k, 0, where],
+                recv_sem=recv_sem.at[k, where],
+                device_id=twin,
+                device_id_type=MESH,
+            ).wait_recv()
+
+    own_copies = [pltpu.make_async_copy(ins[k], outs[k].at[mine], own_sem.at[k]) for k in range(count)]
+    push(0, mine, z < nz - 1, True)
+    push(1, mine, z > 0, True)
+    push(2, mine, None, True)
+    push(3, mine, None, True)
+    push(4, mine, None, True)
+    for copy in own_copies:
+        copy.start()
+
+    def along(step):
+        if step == 0:
+            yield None, z
+        else:
+            yield z >= step, jnp.maximum(z - step, 0)
+            yield z + step < nz, jnp.minimum(z + step, nz - 1)
+
+    def on(allowed, action):
+        if allowed is None:
+            action()
+        else:
+            pl.when(allowed)(action)
+
+    for turn in range(1, nz + 2):
+        if turn < nz:
+            for index, (allowed, zz) in enumerate(along(turn)):
+                where = slot(zz, a, b, c)
+                on(allowed, functools.partial(arrive, where))
+                if index == 0:
+                    push(0, where, allowed & (z < nz - 1))
+                else:
+                    push(1, where, allowed & (z > 0))
+                for way in (2, 3, 4):
+                    push(way, where, allowed)
+        if turn - 1 < nz:
+            for allowed, zz in along(turn - 1):
+                where = slot(zz, 1 - a, b, c)
+                on(allowed, functools.partial(arrive, where))
+                for way in (3, 4):
+                    push(way, where, allowed)
+            for allowed, zz in along(turn - 1):
+                where = slot(zz, a, 1 - b, c)
+                on(allowed, functools.partial(arrive, where))
+                push(4, where, allowed)
+        if turn >= 2:
+            for allowed, zz in along(turn - 2):
+                where = slot(zz, 1 - a, 1 - b, c)
+                on(allowed, functools.partial(arrive, where))
+                push(4, where, allowed)
+    for zz in range(nz):
+        for aa in range(2):
+            for bb in range(2):
+                arrive(slot(zz, aa, bb, 1 - c))
+    for allowed, copy in pending:
+        on(allowed, copy.wait_send)
+    for copy in own_copies:
+        copy.wait()
+
+
+def gather_rows(arrays, devices, ident):
+    count = len(arrays)
+    nz = devices // 8
+    return pl.pallas_call(
+        functools.partial(gather_kernel, nz, count),
+        out_shape=tuple(jax.ShapeDtypeStruct((devices,) + v.shape, v.dtype) for v in arrays),
+        in_specs=[pl.BlockSpec(memory_space=pltpu.VMEM)] * count,
+        out_specs=tuple(pl.BlockSpec(memory_space=pl.ANY) for v in arrays),
+        scratch_shapes=[
+            pltpu.SemaphoreType.DMA((count, 5, devices)),
+            pltpu.SemaphoreType.DMA((count, devices)),
+            pltpu.SemaphoreType.DMA((count,)),
+        ],
+        compiler_params=pltpu.CompilerParams(collective_id=ident, has_side_effects=True),
+        name="gather_rows_%d" % ident,
+    )(*arrays)
+
+
+def scatter_kernel(nz, left_ref, right_ref, out_ref, sent, got, from_far, from_near, rising, falling,
+                   twin_send, twin_recv, far_send, far_recv, near_send, near_recv, line_send, up_recv, down_recv):
+    dp, ep, z, y, x, c, a, b = place()
+    up, down, near, far, twin = targets(dp, ep, z, y, x, c, nz)
+    greet(nz, z, up, down, near, far, twin)
+    per = 4 * nz
+
+    def zed(step):
+        if nz == 4:
+            far_one = jnp.where(z < 2, 3, 0)
+            second = jnp.where(z < 2, 2 - 2 * z, 7 - 2 * z)
+            third = 1 + z % 2
+            return jnp.where(step == 0, far_one, jnp.where(step == 1, second, jnp.where(step == 2, third, z)))
+        return (z + 1 + step) % nz
+
+    def term(where):
+        return jnp.dot(left_ref[where], right_ref[...], preferred_element_type=jnp.float32)
+
+    def order(index, aa, bb, cc):
+        part = index // nz
+        flip_b = 1 - part // 2
+        flip_a = 1 - part % 2
+        return slot(zed(index % nz), aa + flip_a * (1 - 2 * aa), bb + flip_b * (1 - 2 * bb), cc)
+
+    def twin_copy(index):
+        return pltpu.make_async_remote_copy(
+            src_ref=sent.at[index], dst_ref=got.at[index], send_sem=twin_send.at[index],
+            recv_sem=twin_recv.at[index], device_id=twin, device_id_type=MESH)
+
+    def far_copy(index):
+        return pltpu.make_async_remote_copy(
+            src_ref=got.at[index], dst_ref=from_far.at[index], send_sem=far_send.at[index],
+            recv_sem=far_recv.at[index], device_id=far, device_id_type=MESH)
+
+    def near_copy(index):
+        return pltpu.make_async_remote_copy(
+            src_ref=got.at[2 * nz + index], dst_ref=from_near.at[index], send_sem=near_send.at[index],
+            recv_sem=near_recv.at[index], device_id=near, device_id_type=MESH)
+
+    def up_copy(index, zz):
+        return pltpu.make_async_remote_copy(
+            src_ref=got.at[3 * nz + index], dst_ref=rising.at[zz], send_sem=line_send.at[index],
+            recv_sem=up_recv.at[zz], device_id=up, device_id_type=MESH)
+
+    def down_copy(index, zz):
+        return pltpu.make_async_remote_copy(
+            src_ref=got.at[3 * nz + index], dst_ref=falling.at[zz], send_sem=line_send.at[index],
+            recv_sem=down_recv.at[zz], device_id=down, device_id_type=MESH)
+
+    def give(index):
+        sent[index] = term(order(index, b, a, 1 - c)).astype(sent.dtype)
+        twin_copy(index).start()
+
+    def taken(index):
+        value = term(order(index, a, b, c))
+        twin_copy(index).wait_recv()
+        return value + got[index].astype(jnp.float32)
+
+    def far_step(step, carry):
+        give(2 * step)
+        give(2 * step + 1)
+        got[step] = taken(step).astype(got.dtype)
+        far_copy(step).start()
+        return carry
+
+    lax.fori_loop(0, 2 * nz, far_step, 0)
+
+    def near_step(step, carry):
+        value = taken(2 * nz + step)
+        far_copy(step).wait_recv()
+        value = value + from_far[step].astype(jnp.float32)
+        got[2 * nz + step] = value.astype(got.dtype)
+        near_copy(step).start()
+        return carry
+
+    lax.fori_loop(0, nz, near_step, 0)
+
+    def line_step(step, carry):
+        zz = zed(step)
+        value = taken(3 * nz + step)
+        far_copy(nz + step).wait_recv()
+        near_copy(step).wait_recv()
+        out_ref[...] = value + from_far[nz + step].astype(jnp.float32) + from_near[step].astype(jnp.float32)
+
+        @pl.when((zz >= z) & (z > 0))
+        def _():
+            up_copy(step, zz).wait_recv()
+            out_ref[...] += rising[zz].astype(jnp.float32)
+
+        @pl.when((zz <= z) & (z < nz - 1))
+        def _():
+            down_copy(step, zz).wait_recv()
+            out_ref[...] += falling[zz].astype(jnp.float32)
+
+        @pl.when(zz > z)
+        def _():
+            got[3 * nz + step] = out_ref[...].astype(got.dtype)
+            up_copy(step, zz).start()
+
+        @pl.when(zz < z)
+        def _():
+            got[3 * nz + step] = out_ref[...].astype(got.dtype)
+            down_copy(step, zz).start()
+
+        return carry
+
+    lax.fori_loop(0, nz, line_step, 0)
+
+    def finish(step, carry):
+        twin_copy(step).wait_send()
+        return carry
+
+    lax.fori_loop(0, per, finish, 0)
+
+    def finish_far(step, carry):
+        far_copy(step).wait_send()
+        return carry
+
+    lax.fori_loop(0, 2 * nz, finish_far, 0)
+
+    def finish_near(step, carry):
+        near_copy(step).wait_send()
+
+        @pl.when(step < nz - 1)
+        def _():
+            up_copy(step, 0).wait_send()
+
+        return carry
+
+    lax.fori_loop(0, nz, finish_near, 0)
+
+
+def scatter_sum(left, right, devices, ident):
+    nz = devices // 8
+    rows = left.shape[0] // devices
+    depth, wide = right.shape
+    block = (rows, wide)
+    low = jnp.bfloat16
+    dma = pltpu.SemaphoreType.DMA
+    return pl.pallas_call(
+        functools.partial(scatter_kernel, nz),
+        out_shape=jax.ShapeDtypeStruct(block, jnp.float32),
+        in_specs=[pl.BlockSpec(memory_space=pltpu.VMEM)] * 2,
+        out_specs=pl.BlockSpec(memory_space=pltpu.VMEM),
+        scratch_shapes=[
+            pltpu.VMEM((4 * nz,) + block, low),
+            pltpu.VMEM((4 * nz,) + block, low),
+            pltpu.VMEM((2 * nz,) + block, low),
+            pltpu.VMEM((nz,) + block, low),
+            pltpu.VMEM((nz,) + block, low),
+            pltpu.VMEM((nz,) + block, low),
+            dma((4 * nz,)), dma((4 * nz,)), dma((2 * nz,)), dma((2 * nz,)),
+            dma((nz,)), dma((nz,)), dma((nz,)), dma((nz,)), dma((nz,)),
+        ],
+        compiler_params=pltpu.CompilerParams(
+            collective_id=ident, has_side_effects=True, vmem_limit_bytes=58 * 2**20),
+        name="scatter_sum_%d" % ident,
+    )(left.reshape(devices, rows, depth), right)
+
+
+def whole_rows(mesh):
+    return mesh.shape["ep"] == 4 and mesh.shape["dp"] % 2 == 0 and mesh.shape["dp"] <= 8
+
+
+def exact_dot(left_side, right_side):
+    return jnp.dot(
+        left_side, right_side, precision=lax.Precision.HIGHEST, preferred_element_type=jnp.float32
+    )
+
+
+def block_layout(lens, tok_count):
+    ends = [lens[:, :1]]
+    for at in range(1, lens.shape[1]):
+        ends.append(ends[-1] + lens[:, at : at + 1])
+    row_index = lax.broadcasted_iota(jnp.int32, (lens.shape[0], tok_count), 1)
+    segment = jnp.zeros_like(row_index)
+    first_row = jnp.zeros_like(row_index)
+    for end in ends:
+        passed = row_index >= end
+        segment = segment + passed.astype(jnp.int32)
+        first_row = jnp.where(passed, end, first_row)
+    return (segment, row_index - first_row, segment < lens.shape[1])
+
+
+def by_experts(
+    hidden_in,
+    cotangent,
+    deal_order,
+    seq_lengths,
+    expert_ids,
+    w_query,
+    w_key,
+    w_value,
+    w_out,
+    w_router,
+    gain_attn,
+    gain_moe,
+    gain_query,
+    gain_key,
+    w_gate,
+    w_up,
+    w_down,
+    clip_threshold,
+):
+    f32, low = jnp.float32, jnp.bfloat16
+    everyone = ("dp", "ep")
+    dp_count, ep_count = lax.axis_size("dp"), lax.axis_size("ep")
+    devices = dp_count * ep_count
+    dp, ep = lax.axis_index("dp"), lax.axis_index("ep")
+    me = dp * ep_count + ep
+    tok_count, width = hidden_in.shape
+    all_count = devices * tok_count
+    head_dim = gain_query.shape[0]
+    half_dim = head_dim // 2
+    rows_own = w_query.shape[0]
+    head_count = w_query.shape[1] // head_dim
+    kv_count = w_key.shape[1] // head_dim
+    group_size = head_count // kv_count
+    experts = w_router.shape[1]
+    exp_local, wide_own, hidden = w_gate.shape
+    parts = dp_count // exp_local
+    piece = hidden // parts
+    score_scale = head_dim ** (-0.5)
+
+    gain_col = gain_attn.astype(f32)[:, None]
+    heads_in = (w_query.astype(f32) * gain_col).astype(low).reshape(rows_own, head_count, head_dim)
+    keys_in = (w_key.astype(f32) * gain_col).astype(low).reshape(rows_own, kv_count, head_dim)
+    values_in = (w_value.astype(f32) * gain_col).astype(low).reshape(rows_own, kv_count, head_dim)
+    sent_heads = jnp.concatenate(
+        [heads_in, jnp.repeat(keys_in, group_size, axis=1), jnp.repeat(values_in, group_size, axis=1)],
+        axis=2,
+    ).transpose(1, 0, 2)
+    w_heads = lax.all_to_all(sent_heads, everyone, 0, 0, tiled=True).reshape(width, 3 * head_dim)
+
+    def by_part(weights):
+        return weights.reshape(exp_local, wide_own, parts, piece).transpose(0, 2, 1, 3)
+
+    sent_rise = jnp.concatenate([by_part(w_gate), by_part(w_up)], axis=3).reshape(
+        dp_count, wide_own, 2 * piece
+    )
+    w_rise = lax.all_to_all(sent_rise, "dp", 0, 0, tiled=True).reshape(width, 2 * piece)
+    w_fall = lax.all_to_all(w_down.reshape(dp_count, piece, wide_own), "dp", 0, 0, tiled=True)
+    w_fall = w_fall.transpose(1, 0, 2).reshape(piece, width)
+
+    local_order = deal_order % tok_count
+    deal = (local_order[:, None] == jnp.arange(tok_count, dtype=jnp.int32)[None, :]).astype(low)
+    resid_in = jnp.dot(deal, hidden_in, preferred_element_type=f32)
+    own_segment, own_position, own_valid = block_layout(seq_lengths, tok_count)
+    valid_col = own_valid[0].astype(f32)[:, None]
+    grad_mid_out = jnp.dot(deal, cotangent, preferred_element_type=f32) * valid_col
+    inv_one = rms_scale(resid_in)
+    unit_one = resid_in * inv_one
+    lens_row = jnp.pad(seq_lengths.astype(f32), ((0, 0), (0, 128 - seq_lengths.shape[1])))
+    gain_row = jnp.pad(gain_moe.astype(f32)[None, :], ((0, 0), (0, 128 - rows_own)))
+    router_rows = w_router.astype(f32).reshape(-1, 128)
+    note_one = jnp.concatenate([lens_row, gain_row, router_rows], axis=0)
+    note_one = jnp.pad(note_one, ((0, -note_one.shape[0] % 8), (0, 0)))
+    unit_all, grad_all, notes = gather_rows(
+        (unit_one.astype(low), grad_mid_out.astype(low), note_one), devices, 1
+    )
+    lens_all = notes[:, 0, : seq_lengths.shape[1]].astype(jnp.int32)
+    gain_two = notes[:, 1, :rows_own].reshape(1, width)
+    router_full = notes[:, 2 : 2 + router_rows.shape[0]].reshape(width, experts)
+
+    segment, position, valid_row = block_layout(lens_all, tok_count)
+    step_down = lax.broadcasted_iota(jnp.int32, (1, tok_count, tok_count), 1)
+    step_across = lax.broadcasted_iota(jnp.int32, (1, tok_count, tok_count), 2)
+    allowed = (segment[:, :, None] == segment[:, None, :]) & (step_across <= step_down)
+    cosine_rows, sine_rows = rotary_tables(jnp.arange(tok_count, dtype=jnp.int32), head_dim)
+    place_hot = (position.reshape(-1)[:, None] == jnp.arange(tok_count)[None, :]).astype(f32)
+    cosine_all = exact_dot(place_hot, cosine_rows).reshape(devices, tok_count, head_dim)
+    sine_all = exact_dot(place_hot, sine_rows).reshape(devices, tok_count, head_dim)
+    flat_unit = unit_all.reshape(all_count, width)
+    projected = jnp.dot(flat_unit, w_heads, preferred_element_type=f32).reshape(
+        devices, tok_count, 3 * head_dim
+    )
+    query_raw = projected[..., :head_dim]
+    key_raw = projected[..., head_dim : 2 * head_dim]
+    value_rows = projected[..., 2 * head_dim :].astype(low)
+    gain_query_f = gain_query.astype(f32)
+    gain_key_f = gain_key.astype(f32)
+    inv_query = rms_scale(query_raw)
+    unit_query = query_raw * inv_query
+    query_rot = rotate(unit_query * gain_query_f, cosine_all, sine_all).astype(low)
+    inv_key = rms_scale(key_raw)
+    unit_key = key_raw * inv_key
+    key_rot = rotate(unit_key * gain_key_f, cosine_all, sine_all).astype(low)
+    scores = contract(query_rot, key_rot, "btd,bud->btu") * score_scale
+    masked = jnp.where(allowed, scores, masked_fill)
+    row_top = jnp.max(masked, axis=-1, keepdims=True)
+    exponent = jnp.exp(masked - row_top)
+    probs = exponent / jnp.sum(exponent, axis=-1, keepdims=True)
+    probs_low = probs.astype(low)
+    mixed = contract(probs_low, value_rows, "btu,bud->btd").astype(low).reshape(all_count, head_dim)
+    largest_own = jnp.max(jnp.where(valid_row[:, :, None], row_top, masked_fill))
+    resid_mid = resid_in + scatter_sum(mixed, w_out, devices, 2)
+
+    inv_two = rms_scale(resid_mid)
+    unit_two = resid_mid * inv_two
+    normed_mid = (unit_two * gain_two).astype(low)
+    logits = jnp.dot(normed_mid, router_full.astype(low), preferred_element_type=f32)
+    choose = (expert_ids[:, :, None] == jnp.arange(experts, dtype=jnp.int32)[None, None, :]).any(axis=1)
+    picked = jnp.where(choose, logits, masked_fill)
+    gate_power = jnp.where(choose, jnp.exp(picked - jnp.max(picked, axis=1, keepdims=True)), 0.0)
+    route = gate_power / jnp.sum(gate_power, axis=1, keepdims=True)
+    note_two = jnp.concatenate([route.T, jnp.full((8, tok_count), largest_own, f32)], axis=0)
+    normed_all, notes = gather_rows((normed_mid, note_two), devices, 3)
+    clip_factor = jnp.sqrt(clip_threshold / jnp.maximum(notes[:, experts, 0], clip_threshold))
+
+    mine = ep * exp_local + dp // parts
+    weight = lax.dynamic_slice_in_dim(notes, mine, 1, axis=1).reshape(all_count, 1)
+    flat_mid = normed_all.reshape(all_count, width)
+    flat_grad = grad_all.reshape(all_count, width)
+    risen = jnp.dot(flat_mid, w_rise, preferred_element_type=f32)
+    gate_part, up_part = risen[:, :piece], risen[:, piece:]
+    grad_plain = contract(flat_grad, w_fall, "td,fd->tf")
+    sigmoid_gate = jax.nn.sigmoid(gate_part)
+    silu_gate = gate_part * sigmoid_gate
+    hidden_mid = silu_gate * up_part
+    grad_route = jnp.sum(hidden_mid * grad_plain, axis=1, keepdims=True)
+    weighted_mid = (hidden_mid * weight).astype(low)
+    grad_hidden = grad_plain * weight
+    grad_gate_part = (
+        grad_hidden * up_part * sigmoid_gate * (1.0 + gate_part * (1.0 - sigmoid_gate))
+    ).astype(low)
+    grad_up_part = (grad_hidden * silu_gate).astype(low)
+    route_high = grad_route.astype(low)
+    route_rest = (grad_route - route_high.astype(f32)).astype(low)
+    both = jnp.concatenate([grad_gate_part, grad_up_part], axis=1)
+    lane = lax.broadcasted_iota(jnp.int32, (1, 128), 1)
+    tail = jnp.where(lane == 0, route_high, jnp.where(lane == 1, route_rest, jnp.zeros((), low)))
+    left = jnp.concatenate([both, tail], axis=1)
+    spot = lax.broadcasted_iota(jnp.int32, (128, 128), 0)
+    across = lax.broadcasted_iota(jnp.int32, (128, 128), 1)
+    spread = ((spot < 2) & (across == mine)).astype(low)
+    right = jnp.concatenate(
+        [
+            jnp.concatenate([w_rise.T, jnp.zeros((2 * piece, 128), low)], axis=1),
+            jnp.concatenate([jnp.zeros((128, width), low), spread], axis=1),
+        ],
+        axis=0,
+    )
+    summed = scatter_sum(left, right, devices, 4)
+    grad_rise_w = contract(flat_mid, both, "td,tf->df").astype(low)
+    grad_fall_w = contract(weighted_mid, flat_grad, "tf,td->fd").astype(low)
+    back_rise = lax.all_to_all(
+        grad_rise_w.reshape(dp_count, wide_own, 2 * piece), "dp", 0, 0, tiled=True
+    )
+    back_fall = lax.all_to_all(
+        grad_fall_w.reshape(piece, dp_count, wide_own).transpose(1, 0, 2), "dp", 0, 0, tiled=True
+    )
+    resid_out = resid_mid + scatter_sum(weighted_mid, w_fall, devices, 5)
+    undeal = (jnp.arange(tok_count, dtype=jnp.int32)[:, None] == local_order[None, :]).astype(low)
+    block_out = jnp.dot(
+        undeal, (resid_out * valid_col).astype(low), preferred_element_type=f32
+    ).astype(low)
+
+    def from_part(grads):
+        grads = grads.reshape(exp_local, parts, wide_own, piece).transpose(0, 2, 1, 3)
+        return grads.reshape(exp_local, wide_own, hidden).astype(f32)
+
+    grad_gate = from_part(back_rise[..., :piece])
+    grad_up = from_part(back_rise[..., piece:])
+    grad_down = back_fall.reshape(exp_local, hidden, wide_own).astype(f32)
+
+    grad_gates = summed[:, width : width + experts]
+    mean_term = jnp.sum(route * grad_gates, axis=1, keepdims=True)
+    grad_logits = (route * (grad_gates - mean_term)).astype(low)
+    grad_normed_mid = summed[:, :width] + contract(grad_logits, router_full.astype(low), "te,de->td")
+    gain_part = jnp.sum(grad_normed_mid * unit_two, axis=0)
+    grad_mid = grad_mid_out + norm_back(grad_normed_mid * gain_two, unit_two, inv_two)
+    grad_branch = grad_mid.astype(low)
+    note_three = jnp.concatenate([grad_logits.T.astype(f32), gain_part.reshape(-1, 128)], axis=0)
+    branch_all, notes = gather_rows((grad_branch, note_three), devices, 6)
+    logits_all = notes[:, :experts].astype(low)
+    normed_own = lax.dynamic_slice_in_dim(normed_all, me * rows_own, rows_own, axis=2)
+    grad_router = contract(normed_own, logits_all, "btd,bet->de")
+    gain_sum = jnp.sum(notes[:, experts:], axis=0).reshape(-1)
+    grad_gain_moe = lax.dynamic_slice_in_dim(gain_sum, me * rows_own, rows_own)
+
+    flat_branch = branch_all.reshape(all_count, width)
+    grad_out = contract(mixed, flat_branch, "tq,td->qd")
+    grad_mixed = (
+        contract(flat_branch, w_out, "td,qd->tq").astype(low).reshape(devices, tok_count, head_dim)
+    )
+    grad_value = contract(probs_low, grad_mixed, "btu,btd->bud").astype(low)
+    grad_probs = contract(grad_mixed, value_rows, "btd,bud->btu")
+    grad_scores = (
+        probs * (grad_probs - jnp.sum(probs * grad_probs, axis=-1, keepdims=True))
+    ).astype(low)
+    grad_query_rot = contract(grad_scores, key_rot, "btu,bud->btd") * score_scale
+    grad_key_rot = contract(grad_scores, query_rot, "btu,btd->bud") * score_scale
+    grad_query_normed = rotate_back(grad_query_rot, cosine_all, sine_all)
+    grad_key_normed = rotate_back(grad_key_rot, cosine_all, sine_all)
+    gain_pair = jnp.stack(
+        [
+            jnp.sum(grad_query_normed * unit_query, axis=(0, 1)),
+            jnp.sum(grad_key_normed * unit_key, axis=(0, 1)),
+        ]
+    )
+    grad_query_raw = norm_back(grad_query_normed * gain_query_f, unit_query, inv_query).astype(low)
+    grad_key_raw = norm_back(grad_key_normed * gain_key_f, unit_key, inv_key).astype(low)
+    grad_heads = jnp.concatenate([grad_query_raw, grad_key_raw, grad_value], axis=2).reshape(
+        all_count, 3 * head_dim
+    )
+    grad_heads_w = contract(flat_unit, grad_heads, "td,tq->dq").astype(low)
+    back_heads = lax.all_to_all(
+        grad_heads_w.reshape(devices, rows_own, 3 * head_dim), everyone, 0, 0, tiled=True
+    ).astype(f32)
+    grad_unit_one = scatter_sum(grad_heads, w_heads.T, devices, 7)
+    (gain_pairs,) = gather_rows((jnp.pad(gain_pair, ((0, 6), (0, 0))),), devices, 8)
+    gain_pair = jnp.sum(gain_pairs, axis=0)
+    plain_query = back_heads[..., :head_dim].transpose(1, 0, 2).reshape(rows_own, -1)
+
+    def of_group(grads):
+        grads = jnp.sum(grads.reshape(kv_count, group_size, rows_own, head_dim), axis=1)
+        return grads.transpose(1, 0, 2).reshape(rows_own, -1)
+
+    plain_key = of_group(back_heads[..., head_dim : 2 * head_dim])
+    plain_value = of_group(back_heads[..., 2 * head_dim :])
+    grad_gain_attn = (
+        jnp.sum(plain_query * w_query.astype(f32), axis=1)
+        + jnp.sum(plain_key * w_key.astype(f32), axis=1)
+        + jnp.sum(plain_value * w_value.astype(f32), axis=1)
+    )
+    grad_resid_in = grad_mid + norm_back(grad_unit_one, unit_one, inv_one)
+    grad_input = exact_dot(undeal.astype(f32), grad_resid_in)
+    return (
+        block_out,
+        grad_input,
+        plain_query * gain_col,
+        plain_key * gain_col,
+        plain_value * gain_col,
+        grad_out,
+        grad_router,
+        grad_gain_attn,
+        grad_gain_moe,
+        gain_pair[0],
+        gain_pair[1],
+        grad_gate,
+        grad_up,
+        grad_down,
+        clip_factor,
+    )
+
+
 def solution(mesh):
     placed = (
         P(("dp", "ep"), None),
@@ -359,7 +967,7 @@
         P(),
     )
     return jax.shard_map(
-        per_device,
+        per_device if not whole_rows(mesh) else by_experts,
         mesh=mesh,
         in_specs=placed,
         out_specs=(

time: 2790 us -> 1080 us (0.39)
  waiting for transfers between devices: 2180 us -> 34.2 us
  Pallas kernels: 0 us -> 734 us
  blocking collectives: 217 us -> 0 us
  matrix products: 205 us -> 142 us
    reduce_scatter x7 -> x0, waiting for transfers between devices: 1430 us -> none  [the longest x1 365 us: per_device(): lax.psum_scatter(grad_query_w, ('dp', 'ep'), scatter_dimension=0, tiled=T...]
    pallas_call x0 -> x8, Pallas kernels: none -> 734 us  [the longest x4 392 us: scatter_sum(): pl.pallas_call(functools.partial(scatter_kernel, nz), out_shape=jax.Shape...]
    all_gather x7 -> x0, waiting for transfers between devices: 627 us -> none  [the longest x1 164 us: per_device(): lax.all_gather(w_up, 'dp', axis=1, tiled=True)]
    all_gather x1 -> x0, blocking collectives: 92.4 us -> none  [per_device(): lax.all_gather(w_router, ('dp', 'ep'), axis=0, tiled=True)]
    all_to_all x4 -> x6, waiting for transfers between devices: 121 us -> 34.2 us  [the longest x1 17.8 us: by_experts(): lax.all_to_all(sent_heads, everyone, 0, 0, tiled=True)]
    unnamed x2 -> x0, blocking collectives: 84 us -> none
    dot_general x24 -> x14, matrix products: 183 us -> 99.1 us  [contract(): jnp.einsum(pattern, left_side, right_side, preferred_element_type=jnp.flo...]
    pmax x1 -> x0, blocking collectives: 40.5 us -> none  [per_device(): largest = lax.pmax(largest_local, ('dp', 'ep'))]
  transfers between devices with their start and end apart: 19 -> 6, of which waited for: 16 -> 2; matrix products, arithmetic and copies ran while one was open for 10% -> 16% of each run, Pallas kernels for 0% -> 69%
where the time goes in v1:
time: 1080 us; the launch traced here: 1070 us
  Pallas kernels  734 us (68%)
  matrix products  142 us (13%)
  other arithmetic  64.3 us (6%)
  local copies, waits for them, and re-layouts  49.8 us (5%)
  starting transfers between devices  38.4 us (4%)
  waiting for transfers between devices  34.2 us (3%)
    pallas_call x4, Pallas kernels, scatter_sum(): pl.pallas_call(functools.partial(scatter_kernel, nz), out_shape=jax.Shape...  392 us
    pallas_call x4, Pallas kernels, gather_rows(): pl.pallas_call(functools.partial(gather_kernel, nz, count), out_shape=tup...  343 us
    dot_general x14, matrix products, contract(): jnp.einsum(pattern, left_side, right_side, preferred_element_type=jnp.flo...  99.1 us
  transfers between devices with their start and end apart: 6, of which 2 were waited for; matrix products, arithmetic and copies ran while one was open for 16% of the time, Pallas kernels for 69%

profile of v1, /device:TPU:1, one launch (start us, length us, event | category | flops | bytes accessed | tf_op | source)
XLA Modules:
  0.0 1067.2 jit_solution(11203008333286735523)
XLA Ops:
  0.7 6.5 all-to-all-start.2
  18.1 164.0 %gather_rows_1.1 = (bf16[32,128,2048]{2,1,0:T(8,128)(2,1)}, bf16[32,128,2048]{2,1,0:T(8,128)(2,1)}, f32[32,16,128]{2,1,0:T(8,128)}) custom-call(bf16[128,2048]{1,0:T(8,128)(2,1)} %multiply_convert_fusion.8.refs_0_, bf16[128,2048]{1,0:T(8,128)(2,1)} %get-tuple-element.91.refs_1_, f32[16,128]{1,0:T(8,128)} %pad.26.refs_2_), custom_call_target="tpu_custom_call" | custom-call | tf_op jit(solution)/shard_map/gather_rows_1/pallas_call | solution.py:487
  185.2 11.8 %all-to-all-start = ((bf16[32,64,384]{2,1,0:T(8,128)(2,1)}), bf16[32,64,384]{2,1,0:T(8,128)(2,1)S(1)}, u32[]{:S(2)}, u32[]{:S(2)}) async-start(bf16[32,64,384]{2,1,0:T(8,128)(2,1)} %copy.203), calls=%async_computation | async-start | bytes 3145728 | tf_op jit(solution)/shard_map/all_to_all | solution.py:734
  203.9 3.8 pad_maximum_fusion.1
  215.9 17.8 %all-to-all-done = bf16[32,64,384]{2,1,0:T(8,128)(2,1)S(1)} async-done(((bf16[32,64,384]{2,1,0:T(8,128)(2,1)}), bf16[32,64,384]{2,1,0:T(8,128)(2,1)S(1)}, u32[]{:S(2)}, u32[]{:S(2)}) %all-to-all-start) | async-done | bytes 1572896 | tf_op jit(solution)/shard_map/all_to_all | solution.py:734
  233.6 4.7 all-to-all-start.1
  238.3 11.5 %fusion.77 = f32[32,128,384]{2,1,0:T(8,128)S(1)} fusion(bf16[32,128,2048]{2,1,0:T(8,128)(2,1)} %get-tuple-element.23, bf16[2048,384,1]{1,0,2:T(8,128)(2,1)S(1)} %bitcast.173), kind=kOutput, calls=%fused_computation.212 | convolution fusion | flops 6442450944 | bytes 24641536 | tf_op jit(solution)/shard_map/dot_general | solution.py:775
  258.1 6.7 fusion.13
  271.4 99.4 %scatter_sum_2.1 = f32[128,2048]{1,0:T(8,128)} custom-call(bf16[32,128,128]{2,1,0:T(8,128)(2,1)} %convolution_convert_fusion.4.left_ref, bf16[128,2048]{1,0:T(8,128)(2,1)} %right_ref.1), custom_call_target="tpu_custom_call" | custom-call | tf_op jit(solution)/shard_map/scatter_sum_2/pallas_call | solution.py:641
  374.7 79.7 %gather_rows_3.1 = (bf16[32,128,2048]{2,1,0:T(8,128)(2,1)}, f32[32,24,128]{2,1,0:T(8,128)}) custom-call(bf16[128,2048]{1,0:T(8,128)(2,1)} %copy-done.22, f32[24,128]{1,0:T(8,128)} %concatenate.56.refs_1_), custom_call_target="tpu_custom_call" | custom-call | tf_op jit(solution)/shard_map/gather_rows_3/pallas_call | solution.py:487
  457.6 19.5 %fusion.78 = f32[4096,768]{1,0:T(8,128)} fusion(bf16[4096,2048]{1,0:T(8,128)(2,1)} %bitcast.190, bf16[2048,768]{0,1:T(8,128)(2,1)S(1)} %bitcast.171), kind=kOutput, calls=%fused_computation.213 | convolution fusion | flops 12884901888 | bytes 32505856 | tf_op jit(solution)/shard_map/dot_general | solution.py:815
  477.1 20.0 %multiply_convert_fusion.1 = (bf16[4096,384]{1,0:T(8,128)(2,1)}, bf16[4096,384]{1,0:T(8,128)(2,1)}, f32[4096]{0:T(1024)S(1)}, bf16[4096,384]{1,0:T(8,128)(2,1)}) fusion(f32[4096,768]{1,0:T(8,128)} %fusion.78, f32[4096]{0:T(1024)S(1)} %bitcast.193, bf16[4096,2048]{1,0:T(8,128)(2,1)} %bitcast.198, bf16[384,2048]{1,0:T(8,128)(2,1)S(1)} %bitcast.178), kind=kOutput, calls=%fused_computation.9 | convolution fusion | flops 6472331264 | bytes 40402944 | tf_op jit(solution)/shard_map/td,fd->tf/dot_general | solution.py:42
  497.1 11.3 %convolution_convert_fusion.1 = bf16[384,2048]{1,0:T(8,128)(2,1)S(1)} fusion(bf16[4096,384]{1,0:T(8,128)(2,1)} %get-tuple-element.54, bf16[4096,2048]{1,0:T(8,128)(2,1)} %bitcast.199), kind=kOutput, calls=%fused_computation.22 | convolution fusion | flops 6443237376 | bytes 21495808 | tf_op jit(solution)/shard_map/tf,td->fd/dot_general | solution.py:42
  509.7 5.2 all-to-all-start.5
  514.9 4.3 fusion.6.right_ref
  521.9 3.5 pad_maximum_fusion
  525.4 91.9 %scatter_sum_4.1 = f32[128,2176]{1,0:T(8,128)} custom-call(bf16[32,128,896]{2,1,0:T(8,128)(2,1)} %bitcast.163, bf16[896,2176]{1,0:T(8,128)(2,1)} %fusion.6.right_ref), custom_call_target="tpu_custom_call" | custom-call | tf_op jit(solution)/shard_map/scatter_sum_4/pallas_call | solution.py:641
  623.8 82.5 %gather_rows_6.1 = (bf16[32,128,2048]{2,1,0:T(8,128)(2,1)}, f32[32,32,128]{2,1,0:T(8,128)}) custom-call(bf16[128,2048]{1,0:T(8,128)(2,1)} %get-tuple-element.45.refs_0_, f32[32,128]{1,0:T(8,128)} %pad_maximum_fusion.6.refs_1_), custom_call_target="tpu_custom_call" | custom-call | tf_op jit(solution)/shard_map/gather_rows_6/pallas_call | solution.py:487
  706.3 8.6 convolution_convert_fusion
  724.7 3.7 multiply_reduce_fusion.2
  735.5 13.4 %bitcast_convert_fusion = bf16[2048,384]{1,0:T(8,128)(2,1)} fusion(bf16[32,128,2048]{2,1,0:T(8,128)(2,1)} %get-tuple-element.23, bf16[32,128,128]{2,1,0:T(8,128)(2,1)S(1)} %convolution_convert_fusion.3, bf16[32,128,128]{2,1,0:T(8,128)(2,1)S(1)} %get-tuple-element.56, bf16[32,128,128]{2,1,0:T(8,128)(2,1)S(1)} %get-tuple-element.55), kind=kOutput, calls=%fused_computation.19 | convolution fusion | flops 6452674560 | bytes 21495808 | tf_op jit(solution)/shard_map/td,tq->dq/dot_general | solution.py:42
  748.9 5.6 all-to-all-start.3
  754.5 20.1 %fusion.7 = bf16[2048,768]{1,0:T(8,128)(2,1)} fusion(bf16[4096,2048]{1,0:T(8,128)(2,1)} %bitcast.191, bf16[4096,384]{1,0:T(8,128)(2,1)} %get-tuple-element.52, bf16[4096,384]{1,0:T(8,128)(2,1)} %get-tuple-element.51), kind=kOutput, calls=%fused_computation.16 | convolution fusion | flops 12899057664 | bytes 26214400 | tf_op jit(solution)/shard_map/td,tf->df/dot_general | solution.py:42
  774.6 16.4 %all-to-all-done.3 = bf16[32,64,384]{2,1,0:T(8,128)(2,1)S(1)} async-done(((bf16[32,64,384]{2,1,0:T(8,128)(2,1)}), bf16[32,64,384]{2,1,0:T(8,128)(2,1)S(1)}, u32[]{:S(2)}, u32[]{:S(2)}) %all-to-all-start.3) | async-done | bytes 1572896 | tf_op jit(solution)/shard_map/all_to_all | solution.py:908
  792.1 4.6 all-to-all-start.4
  800.1 110.0 %scatter_sum_5.1 = f32[128,2048]{1,0:T(8,128)} custom-call(bf16[32,128,384]{2,1,0:T(8,128)(2,1)} %bitcast.185, bf16[384,2048]{1,0:T(8,128)(2,1)} %bitcast.177), custom_call_target="tpu_custom_call" | custom-call | tf_op jit(solution)/shard_map/scatter_sum_5/pallas_call | solution.py:641
  910.7 16.5 %gather_rows_8.1 = f32[32,8,128]{2,1,0:T(8,128)} custom-call(f32[8,128]{1,0:T(8,128)} %select_maximum_fusion.1.refs_0_), custom_call_target="tpu_custom_call" | custom-call | tf_op jit(solution)/shard_map/gather_rows_8/pallas_call | solution.py:487
  932.1 90.5 %scatter_sum_7.1 = f32[128,2048]{1,0:T(8,128)} custom-call(bf16[32,128,384]{2,1,0:T(8,128)(2,1)} %pad_maximum_fusion.2.left_ref, bf16[384,2048]{1,0:T(8,128)(2,1)} %bitcast.179), custom_call_target="tpu_custom_call" | custom-call | tf_op jit(solution)/shard_map/scatter_sum_7/pallas_call | solution.py:641
  1030.4 9.2 convolution_bitcast_fusion
  1039.6 3.5 bitcast_convert_fusion.1
  1052.5 5.7 reshape.532
  1061.5 5.6 reshape.533
  (245 shorter events, 106.0 us)
Async XLA Ops:
  0.6 14.9 %copy-start = (bf16[128,2048]{1,0:T(8,128)(2,1)S(1)}, bf16[128,2048]{1,0:T(8,128)(2,1)}, u32[]{:S(2)}) copy-start(bf16[128,2048]{1,0:T(8,128)(2,1)} %param.19) | copy-start | bytes 1572868
  0.7 6.6 copy-start.55
  0.7 6.6 copy-start.42
  0.7 6.6 copy-start.40
  0.7 6.7 copy-start.35
  0.7 7.0 copy-start.48
  0.7 7.1 copy-start.53
  0.7 183.3 %all-to-all-start.2 = ((bf16[8,384,256]{2,1,0:T(8,128)(2,1)}), bf16[8,384,256]{2,1,0:T(8,128)(2,1)S(1)}, u32[]{:S(2)}, u32[]{:S(2)}) async-start(bf16[8,384,256]{2,1,0:T(8,128)(2,1)} %bitcast.187), calls=%async_computation.2 | async-start | bytes 3145728 | tf_op jit(solution)/shard_map/all_to_all | solution.py:743
  15.5 355.2 %copy-start.3 = (f32[128,2048]{1,0:T(8,128)}, f32[128,2048]{1,0:T(8,128)S(1)}, u32[]{:S(2)}) copy-start(f32[128,2048]{1,0:T(8,128)S(1)} %get-tuple-element.90) | copy-start | bytes 3145732
  18.0 180.0 %copy-start.58 = (bf16[128]{0:T(256)(128)(2,1)S(1)}, bf16[128]{0:T(256)(128)(2,1)}, u32[]{:S(2)}) copy-start(bf16[128]{0:T(256)(128)(2,1)} %param.30) | copy-start | bytes 772
  18.1 180.0 %copy-start.59 = (bf16[128]{0:T(256)(128)(2,1)S(1)}, bf16[128]{0:T(256)(128)(2,1)}, u32[]{:S(2)}) copy-start(bf16[128]{0:T(256)(128)(2,1)} %param.31) | copy-start | bytes 772
  185.2 48.5 %all-to-all-start = ((bf16[32,64,384]{2,1,0:T(8,128)(2,1)}), bf16[32,64,384]{2,1,0:T(8,128)(2,1)S(1)}, u32[]{:S(2)}, u32[]{:S(2)}) async-start(bf16[32,64,384]{2,1,0:T(8,128)(2,1)} %copy.203), calls=%async_computation | async-start | bytes 3145728 | tf_op jit(solution)/shard_map/all_to_all | solution.py:734
  208.0 6.4 copy-start.17
  233.6 221.6 %all-to-all-start.1 = ((bf16[8,256,768]{1,2,0:T(8,128)(2,1)}), bf16[8,256,768]{1,2,0:T(8,128)(2,1)}, u32[]{:S(2)}, u32[]{:S(2)}) async-start(bf16[8,256,768]{1,2,0:T(8,128)(2,1)} %bitcast.168), calls=%async_computation.1 | async-start | bytes 6291456 | tf_op jit(solution)/shard_map/all_to_all | solution.py:742
  249.9 19.2 %copy-start.2 = (f32[32,128,384]{2,1,0:T(8,128)}, f32[32,128,384]{2,1,0:T(8,128)S(1)}, u32[]{:S(2)}) copy-start(f32[32,128,384]{2,1,0:T(8,128)S(1)} %fusion.77) | copy-start | bytes 18874372
  372.2 246.1 %copy-start.5 = (f32[128,2048]{1,0:T(8,128)}, f32[128,2048]{1,0:T(8,128)S(1)}, u32[]{:S(2)}) copy-start(f32[128,2048]{1,0:T(8,128)S(1)} %get-tuple-element.50) | copy-start | bytes 3145732
  457.6 19.5 %copy-start.10 = (bf16[8,96,8,256]{3,2,0,1:T(8,128)(2,1)}, bf16[8,96,8,256]{3,2,0,1:T(8,128)(2,1)S(1)}, u32[]{:S(2)}) copy-start(bf16[8,96,8,256]{3,2,0,1:T(8,128)(2,1)S(1)} %copy.246) | copy-start | bytes 9437188
  457.6 19.5 %copy-start.18 = (bf16[8,48,8,256]{3,2,0,1:T(8,128)(2,1)S(1)}, bf16[8,48,8,256]{3,2,0,1:T(8,128)(2,1)}, u32[]{:S(2)}) copy-start(bf16[8,48,8,256]{3,2,0,1:T(8,128)(2,1)} %copy.247) | copy-start | bytes 4718596
  509.7 239.2 %all-to-all-start.5 = ((bf16[8,384,256]{2,1,0:T(8,128)(2,1)}), bf16[8,384,256]{2,1,0:T(8,128)(2,1)}, u32[]{:S(2)}, u32[]{:S(2)}) async-start(bf16[8,384,256]{2,1,0:T(8,128)(2,1)} %bitcast.176), calls=%async_computation.5 | async-start | bytes 3145728 | tf_op jit(solution)/shard_map/all_to_all | solution.py:850
  514.9 7.0 copy-start.32
  514.9 7.0 copy-start.33
  620.6 85.6 %copy-start.38 = (bf16[128,2048]{1,0:T(8,128)(2,1)S(1)}, bf16[128,2048]{1,0:T(8,128)(2,1)}, u32[]{:S(2)}) copy-start(bf16[128,2048]{1,0:T(8,128)(2,1)} %right_ref.1) | copy-start | bytes 1572868
  620.6 94.3 %slice-start = ((s8[6291456]{0:T(1024)(128)(4,1)}), s8[2097152]{0:T(1024)(128)(4,1)S(1)}, s32[]{:S(2)}) async-start(s8[6291456]{0:T(1024)(128)(4,1)} %bitcast.161), calls=%async_computation.6 | async-start | bytes 4194304
  706.3 8.6 slice-start.1
  706.3 8.6 copy-start.13
  748.9 42.1 %all-to-all-start.3 = ((bf16[32,64,384]{2,1,0:T(8,128)(2,1)}), bf16[32,64,384]{2,1,0:T(8,128)(2,1)S(1)}, u32[]{:S(2)}, u32[]{:S(2)}) async-start(bf16[32,64,384]{2,1,0:T(8,128)(2,1)} %bitcast.188), calls=%async_computation.3 | async-start | bytes 3145728 | tf_op jit(solution)/shard_map/all_to_all | solution.py:908
  792.1 254.9 %all-to-all-start.4 = ((bf16[8,256,768]{2,1,0:T(8,128)(2,1)}), bf16[8,256,768]{2,1,0:T(8,128)(2,1)}, u32[]{:S(2)}, u32[]{:S(2)}) async-start(bf16[8,256,768]{2,1,0:T(8,128)(2,1)} %bitcast.184), calls=%async_computation.4 | async-start | bytes 6291456 | tf_op jit(solution)/shard_map/all_to_all | solution.py:847
  800.1 128.0 %copy-start.39 = (f32[32,32,128]{2,1,0:T(8,128)S(1)}, f32[32,32,128]{2,1,0:T(8,128)}, u32[]{:S(2)}) copy-start(f32[32,32,128]{2,1,0:T(8,128)} %get-tuple-element.28) | copy-start | bytes 1572868
  800.1 128.7 %copy-start.29 = (bf16[32,128,128]{2,1,0:T(8,128)(2,1)S(1)}, bf16[32,128,128]{2,1,0:T(8,128)(2,1)}, u32[]{:S(2)}) copy-start(bf16[32,128,128]{2,1,0:T(8,128)(2,1)} %copy-done.28) | copy-start | bytes 3145732
  800.1 128.7 %copy-start.31 = (bf16[32,128,128]{2,1,0:T(8,128)(2,1)S(1)}, bf16[32,128,128]{2,1,0:T(8,128)(2,1)}, u32[]{:S(2)}) copy-start(bf16[32,128,128]{2,1,0:T(8,128)(2,1)} %copy-done.30) | copy-start | bytes 3145732
  932.1 93.0 %copy-start.4 = (f32[128,2048]{1,0:T(8,128)S(1)}, f32[128,2048]{1,0:T(8,128)}, u32[]{:S(2)}) copy-start(f32[128,2048]{1,0:T(8,128)} %copy-done.3) | copy-start | bytes 3145732
  932.1 93.0 %copy-start.50 = (f32[128]{0:T(128)S(1)}, f32[128]{0:T(128)}, u32[]{:S(2)}) copy-start(f32[128]{0:T(128)} %copy-done.49) | copy-start | bytes 1540
  (38 other events, 104.0 us)

commit v2 on v1

--- a/solution.py
+++ b/solution.py
@@ -368,8 +368,23 @@
     return z * 8 + first * (4 - 2 * c) + second * (2 + 2 * c) + c
 
 
-def greet(nz, z, up, down, near, far, twin):
+def greet(nz, z, dp, ep, ways, everyone):
     barrier = pltpu.get_barrier_semaphore()
+    if everyone:
+        total = nz * 8
+        me = dp * 4 + ep
+
+        def hello(step, carry):
+            other = (me + step) % total
+            pl.semaphore_signal(
+                barrier, inc=1, device_id=(other // 4, other % 4), device_id_type=MESH
+            )
+            return carry
+
+        lax.fori_loop(1, total, hello, 0)
+        pl.semaphore_wait(barrier, total - 1)
+        return
+    up, down, near, far, twin = ways
 
     @pl.when(z < nz - 1)
     def _():
@@ -385,14 +400,107 @@
     pl.semaphore_wait(barrier, peers)
 
 
-def gather_kernel(nz, count, *refs):
+class Riders:
+    def __init__(self, kinds, nz, dp, ep, refs):
+        count = len(kinds)
+        self.kinds, self.dp, self.ep = kinds, dp, ep
+        self.ins, self.outs = refs[:count], refs[count : 2 * count]
+        self.send, self.recv, self.own = refs[2 * count :] if count else (None, None, None)
+        self.sizes = [2 * nz if kind == "dp" else 8 * nz for kind in kinds]
+        self.at = [dp if kind == "dp" else dp * 4 + ep for kind in kinds]
+        self.steps = [(r, k) for r in range(count) for k in range(1, self.sizes[r])]
+        self.steps.sort(key=lambda step: step[1] / self.sizes[step[0]])
+
+    def device(self, r, other):
+        if self.kinds[r] == "dp":
+            return (other, self.ep)
+        return (other // 4, other % 4)
+
+    def copy(self, r, step):
+        other = (self.at[r] + step) % self.sizes[r]
+        return pltpu.make_async_remote_copy(
+            src_ref=self.ins[r] if self.kinds[r] == "same" else self.ins[r].at[other],
+            dst_ref=self.outs[r].at[self.at[r]],
+            send_sem=self.send.at[r, step],
+            recv_sem=self.recv.at[r, self.at[r]],
+            device_id=self.device(r, other),
+            device_id_type=MESH,
+        )
+
+    def arrival(self, r, step):
+        other = (self.at[r] + step) % self.sizes[r]
+        return pltpu.make_async_remote_copy(
+            src_ref=self.outs[r].at[other],
+            dst_ref=self.outs[r].at[other],
+            send_sem=self.send.at[r, step],
+            recv_sem=self.recv.at[r, other],
+            device_id=self.device(r, other),
+            device_id_type=MESH,
+        )
+
+    def own_copy(self, r):
+        here = self.ins[r] if self.kinds[r] == "same" else self.ins[r].at[self.at[r]]
+        return pltpu.make_async_copy(here, self.outs[r].at[self.at[r]], self.own.at[r])
+
+    def begin(self):
+        for r in range(len(self.kinds)):
+            self.own_copy(r).start()
+
+    def some(self, share, shares):
+        total = len(self.steps)
+        for r, k in self.steps[total * share // shares : total * (share + 1) // shares]:
+            self.copy(r, k).start()
+
+    def looped(self, step, steps):
+        for r in range(len(self.kinds)):
+            per = -(-(self.sizes[r] - 1) // steps)
+            for k in range(per):
+                piece = 1 + step * per + k
+
+                @pl.when(piece < self.sizes[r])
+                def _():
+                    self.copy(r, piece).start()
+
+    def finish(self):
+        for r in range(len(self.kinds)):
+
+            def settle(step, carry):
+                self.arrival(r, step).wait_recv()
+                self.copy(r, step).wait_send()
+                return carry
+
+            lax.fori_loop(1, self.sizes[r], settle, 0)
+            self.own_copy(r).wait()
+
+
+def rider_shapes(riders, devices):
+    kinds = tuple(kind for kind, _ in riders)
+    arrays = tuple(array for _, array in riders)
+    outs = tuple(
+        jax.ShapeDtypeStruct(((devices,) + v.shape) if kind == "same" else v.shape, v.dtype)
+        for kind, v in riders
+    )
+    dma = pltpu.SemaphoreType.DMA
+    count = len(riders)
+    sems = [dma((count, devices)), dma((count, devices)), dma((count,))] if count else []
+    return kinds, arrays, outs, sems
+
+
+def gather_kernel(nz, count, kinds, *refs):
+    extra = len(kinds)
     ins = refs[:count]
-    outs = refs[count : 2 * count]
-    send_sem, recv_sem, own_sem = refs[2 * count :]
+    outs = refs[count + extra : 2 * count + extra]
+    send_sem, recv_sem, own_sem = refs[2 * (count + extra) : 2 * (count + extra) + 3]
     dp, ep, z, y, x, c, a, b = place()
-    up, down, near, far, twin = targets(dp, ep, z, y, x, c, nz)
-    ways = (up, down, near, far, twin)
-    greet(nz, z, up, down, near, far, twin)
+    ways = targets(dp, ep, z, y, x, c, nz)
+    twin = ways[4]
+    riders = Riders(
+        kinds, nz, dp, ep,
+        refs[count : count + extra]
+        + refs[2 * count + extra : 2 * (count + extra)]
+        + refs[2 * (count + extra) + 3 :],
+    )
+    greet(nz, z, dp, ep, ways, extra > 0)
     mine = slot(z, a, b, c)
     pending = []
 
@@ -431,6 +539,7 @@
     push(4, mine, None, True)
     for copy in own_copies:
         copy.start()
+    riders.begin()
 
     def along(step):
         if step == 0:
@@ -446,6 +555,8 @@
             pl.when(allowed)(action)
 
     for turn in range(1, nz + 2):
+        if turn <= nz:
+            riders.some(turn - 1, nz)
         if turn < nz:
             for index, (allowed, zz) in enumerate(along(turn)):
                 where = slot(zz, a, b, c)
@@ -479,31 +590,47 @@
         on(allowed, copy.wait_send)
     for copy in own_copies:
         copy.wait()
-
-
-def gather_rows(arrays, devices, ident):
+    riders.finish()
+
+
+def gather_rows(arrays, devices, ident, riders=()):
     count = len(arrays)
     nz = devices // 8
+    kinds, ridden, rider_outs, rider_sems = rider_shapes(riders, devices)
     return pl.pallas_call(
-        functools.partial(gather_kernel, nz, count),
-        out_shape=tuple(jax.ShapeDtypeStruct((devices,) + v.shape, v.dtype) for v in arrays),
-        in_specs=[pl.BlockSpec(memory_space=pltpu.VMEM)] * count,
-        out_specs=tuple(pl.BlockSpec(memory_space=pl.ANY) for v in arrays),
+        functools.partial(gather_kernel, nz, count, kinds),
+        out_shape=tuple(jax.ShapeDtypeStruct((devices,) + v.shape, v.dtype) for v in arrays)
+        + rider_outs,
+        in_specs=[pl.BlockSpec(memory_space=pltpu.VMEM)] * (count + len(riders)),
+        out_specs=tuple(pl.BlockSpec(memory_space=pl.ANY) for v in arrays + ridden),
         scratch_shapes=[
             pltpu.SemaphoreType.DMA((count, 5, devices)),
             pltpu.SemaphoreType.DMA((count, devices)),
             pltpu.SemaphoreType.DMA((count,)),
-        ],
+        ]
+        + rider_sems,
         compiler_params=pltpu.CompilerParams(collective_id=ident, has_side_effects=True),
         name="gather_rows_%d" % ident,
-    )(*arrays)
-
-
-def scatter_kernel(nz, left_ref, right_ref, out_ref, sent, got, from_far, from_near, rising, falling,
-                   twin_send, twin_recv, far_send, far_recv, near_send, near_recv, line_send, up_recv, down_recv):
+    )(*arrays, *ridden)
+
+
+def scatter_kernel(nz, turned, beside, kinds, *refs):
+    extra = len(kinds)
+    left_ref, right_ref = refs[:2]
+    beside_ref = refs[2] if beside else None
+    refs = refs[2 + beside :]
+    out_ref = refs[extra]
+    sent, got, from_far, from_near, rising, falling = refs[2 * extra + 1 : 2 * extra + 7]
+    (twin_send, twin_recv, far_send, far_recv, near_send, near_recv, line_send, up_recv,
+     down_recv) = refs[2 * extra + 7 : 2 * extra + 16]
     dp, ep, z, y, x, c, a, b = place()
-    up, down, near, far, twin = targets(dp, ep, z, y, x, c, nz)
-    greet(nz, z, up, down, near, far, twin)
+    ways = targets(dp, ep, z, y, x, c, nz)
+    up, down, near, far, twin = ways
+    riders = Riders(
+        kinds, nz, dp, ep, refs[:extra] + refs[extra + 1 : 2 * extra + 1] + refs[2 * extra + 16 :]
+    )
+    greet(nz, z, dp, ep, ways, extra > 0)
+    riders.begin()
     per = 4 * nz
 
     def zed(step):
@@ -515,7 +642,13 @@
         return (z + 1 + step) % nz
 
     def term(where):
-        return jnp.dot(left_ref[where], right_ref[...], preferred_element_type=jnp.float32)
+        sides = (((1,), (1 if turned else 0,)), ((), ()))
+        value = lax.dot_general(
+            left_ref[where], right_ref[...], sides, preferred_element_type=jnp.float32
+        )
+        if beside:
+            value = jnp.concatenate([value, beside_ref[where].astype(jnp.float32)], axis=1)
+        return value
 
     def order(index, aa, bb, cc):
         part = index // nz
@@ -562,6 +695,7 @@
         give(2 * step + 1)
         got[step] = taken(step).astype(got.dtype)
         far_copy(step).start()
+        riders.looped(step, 2 * nz)
         return carry
 
     lax.fori_loop(0, 2 * nz, far_step, 0)
@@ -629,20 +763,25 @@
         return carry
 
     lax.fori_loop(0, nz, finish_near, 0)
-
-
-def scatter_sum(left, right, devices, ident):
+    riders.finish()
+
+
+def scatter_sum(left, right, devices, ident, turned=False, beside=None, riders=()):
     nz = devices // 8
     rows = left.shape[0] // devices
-    depth, wide = right.shape
+    depth, wide = right.shape[::-1] if turned else right.shape
+    held = () if beside is None else (beside.reshape(devices, rows, -1),)
+    wide = wide + sum(v.shape[2] for v in held)
+    kinds, ridden, rider_outs, rider_sems = rider_shapes(riders, devices)
     block = (rows, wide)
     low = jnp.bfloat16
     dma = pltpu.SemaphoreType.DMA
-    return pl.pallas_call(
-        functools.partial(scatter_kernel, nz),
-        out_shape=jax.ShapeDtypeStruct(block, jnp.float32),
-        in_specs=[pl.BlockSpec(memory_space=pltpu.VMEM)] * 2,
-        out_specs=pl.BlockSpec(memory_space=pltpu.VMEM),
+    result = pl.pallas_call(
+        functools.partial(scatter_kernel, nz, turned, len(held), kinds),
+        out_shape=(jax.ShapeDtypeStruct(block, jnp.float32),) + rider_outs,
+        in_specs=[pl.BlockSpec(memory_space=pltpu.VMEM)] * (2 + len(held) + len(riders)),
+        out_specs=(pl.BlockSpec(memory_space=pltpu.VMEM),)
+        + (pl.BlockSpec(memory_space=pl.ANY),) * len(riders),
         scratch_shapes=[
             pltpu.VMEM((4 * nz,) + block, low),
             pltpu.VMEM((4 * nz,) + block, low),
@@ -652,11 +791,13 @@
             pltpu.VMEM((nz,) + block, low),
             dma((4 * nz,)), dma((4 * nz,)), dma((2 * nz,)), dma((2 * nz,)),
             dma((nz,)), dma((nz,)), dma((nz,)), dma((nz,)), dma((nz,)),
-        ],
+        ]
+        + rider_sems,
         compiler_params=pltpu.CompilerParams(
             collective_id=ident, has_side_effects=True, vmem_limit_bytes=58 * 2**20),
         name="scatter_sum_%d" % ident,
-    )(left.reshape(devices, rows, depth), right)
+    )(left.reshape(devices, rows, depth), right, *held, *ridden)
+    return result if riders else result[0]
 
 
 def whole_rows(mesh):
@@ -680,7 +821,7 @@
         passed = row_index >= end
         segment = segment + passed.astype(jnp.int32)
         first_row = jnp.where(passed, end, first_row)
-    return (segment, row_index - first_row, segment < lens.shape[1])
+    return (segment, row_index - first_row)
 
 
 def by_experts(
@@ -704,13 +845,13 @@
     clip_threshold,
 ):
     f32, low = jnp.float32, jnp.bfloat16
-    everyone = ("dp", "ep")
     dp_count, ep_count = lax.axis_size("dp"), lax.axis_size("ep")
     devices = dp_count * ep_count
     dp, ep = lax.axis_index("dp"), lax.axis_index("ep")
     me = dp * ep_count + ep
     tok_count, width = hidden_in.shape
-    all_count = devices * tok_count
+    row_count = tok_count * 7 // 8
+    all_count = devices * row_count
     head_dim = gain_query.shape[0]
     half_dim = head_dim // 2
     rows_own = w_query.shape[0]
@@ -731,24 +872,15 @@
         [heads_in, jnp.repeat(keys_in, group_size, axis=1), jnp.repeat(values_in, group_size, axis=1)],
         axis=2,
     ).transpose(1, 0, 2)
-    w_heads = lax.all_to_all(sent_heads, everyone, 0, 0, tiled=True).reshape(width, 3 * head_dim)
-
     def by_part(weights):
-        return weights.reshape(exp_local, wide_own, parts, piece).transpose(0, 2, 1, 3)
-
-    sent_rise = jnp.concatenate([by_part(w_gate), by_part(w_up)], axis=3).reshape(
-        dp_count, wide_own, 2 * piece
-    )
-    w_rise = lax.all_to_all(sent_rise, "dp", 0, 0, tiled=True).reshape(width, 2 * piece)
-    w_fall = lax.all_to_all(w_down.reshape(dp_count, piece, wide_own), "dp", 0, 0, tiled=True)
-    w_fall = w_fall.transpose(1, 0, 2).reshape(piece, width)
+        weights = weights.reshape(exp_local, wide_own, parts, piece).transpose(0, 2, 1, 3)
+        return weights.reshape(dp_count, wide_own, piece)
 
     local_order = deal_order % tok_count
     deal = (local_order[:, None] == jnp.arange(tok_count, dtype=jnp.int32)[None, :]).astype(low)
+    deal = deal[:row_count]
     resid_in = jnp.dot(deal, hidden_in, preferred_element_type=f32)
-    own_segment, own_position, own_valid = block_layout(seq_lengths, tok_count)
-    valid_col = own_valid[0].astype(f32)[:, None]
-    grad_mid_out = jnp.dot(deal, cotangent, preferred_element_type=f32) * valid_col
+    grad_mid_out = jnp.dot(deal, cotangent, preferred_element_type=f32)
     inv_one = rms_scale(resid_in)
     unit_one = resid_in * inv_one
     lens_row = jnp.pad(seq_lengths.astype(f32), ((0, 0), (0, 128 - seq_lengths.shape[1])))
@@ -756,24 +888,32 @@
     router_rows = w_router.astype(f32).reshape(-1, 128)
     note_one = jnp.concatenate([lens_row, gain_row, router_rows], axis=0)
     note_one = jnp.pad(note_one, ((0, -note_one.shape[0] % 8), (0, 0)))
-    unit_all, grad_all, notes = gather_rows(
-        (unit_one.astype(low), grad_mid_out.astype(low), note_one), devices, 1
+    unit_all, notes, w_heads, w_fall = gather_rows(
+        (unit_one.astype(low), note_one),
+        devices,
+        1,
+        (("all", sent_heads), ("dp", w_down.reshape(dp_count, piece, wide_own))),
+    )
+    w_heads = w_heads.reshape(width, 3 * head_dim)
+    w_fall = w_fall.transpose(1, 0, 2).reshape(piece, width)
+    grad_all, w_rise_up = gather_rows(
+        (grad_mid_out.astype(low),), devices, 9, (("dp", by_part(w_up)),)
     )
     lens_all = notes[:, 0, : seq_lengths.shape[1]].astype(jnp.int32)
     gain_two = notes[:, 1, :rows_own].reshape(1, width)
     router_full = notes[:, 2 : 2 + router_rows.shape[0]].reshape(width, experts)
 
-    segment, position, valid_row = block_layout(lens_all, tok_count)
-    step_down = lax.broadcasted_iota(jnp.int32, (1, tok_count, tok_count), 1)
-    step_across = lax.broadcasted_iota(jnp.int32, (1, tok_count, tok_count), 2)
+    segment, position = block_layout(lens_all, row_count)
+    step_down = lax.broadcasted_iota(jnp.int32, (1, row_count, row_count), 1)
+    step_across = lax.broadcasted_iota(jnp.int32, (1, row_count, row_count), 2)
     allowed = (segment[:, :, None] == segment[:, None, :]) & (step_across <= step_down)
     cosine_rows, sine_rows = rotary_tables(jnp.arange(tok_count, dtype=jnp.int32), head_dim)
     place_hot = (position.reshape(-1)[:, None] == jnp.arange(tok_count)[None, :]).astype(f32)
-    cosine_all = exact_dot(place_hot, cosine_rows).reshape(devices, tok_count, head_dim)
-    sine_all = exact_dot(place_hot, sine_rows).reshape(devices, tok_count, head_dim)
+    cosine_all = exact_dot(place_hot, cosine_rows).reshape(devices, row_count, head_dim)
+    sine_all = exact_dot(place_hot, sine_rows).reshape(devices, row_count, head_dim)
     flat_unit = unit_all.reshape(all_count, width)
     projected = jnp.dot(flat_unit, w_heads, preferred_element_type=f32).reshape(
-        devices, tok_count, 3 * head_dim
+        devices, row_count, 3 * head_dim
     )
     query_raw = projected[..., :head_dim]
     key_raw = projected[..., head_dim : 2 * head_dim]
@@ -793,23 +933,28 @@
     probs = exponent / jnp.sum(exponent, axis=-1, keepdims=True)
     probs_low = probs.astype(low)
     mixed = contract(probs_low, value_rows, "btu,bud->btd").astype(low).reshape(all_count, head_dim)
-    largest_own = jnp.max(jnp.where(valid_row[:, :, None], row_top, masked_fill))
-    resid_mid = resid_in + scatter_sum(mixed, w_out, devices, 2)
+    largest_own = jnp.max(row_top)
+    branch, w_rise_gate = scatter_sum(
+        mixed, w_out, devices, 2, riders=(("dp", by_part(w_gate)),)
+    )
+    resid_mid = resid_in + branch
+    w_rise = jnp.concatenate([w_rise_gate, w_rise_up], axis=2).reshape(width, 2 * piece)
 
     inv_two = rms_scale(resid_mid)
     unit_two = resid_mid * inv_two
     normed_mid = (unit_two * gain_two).astype(low)
     logits = jnp.dot(normed_mid, router_full.astype(low), preferred_element_type=f32)
-    choose = (expert_ids[:, :, None] == jnp.arange(experts, dtype=jnp.int32)[None, None, :]).any(axis=1)
+    choose = (expert_ids[:row_count, :, None] == jnp.arange(experts, dtype=jnp.int32)[None, None, :]).any(axis=1)
     picked = jnp.where(choose, logits, masked_fill)
     gate_power = jnp.where(choose, jnp.exp(picked - jnp.max(picked, axis=1, keepdims=True)), 0.0)
     route = gate_power / jnp.sum(gate_power, axis=1, keepdims=True)
-    note_two = jnp.concatenate([route.T, jnp.full((8, tok_count), largest_own, f32)], axis=0)
+    note_two = jnp.concatenate([route.T, jnp.full((8, row_count), largest_own, f32)], axis=0)
+    note_two = jnp.pad(note_two, ((0, 0), (0, 128 - row_count)))
     normed_all, notes = gather_rows((normed_mid, note_two), devices, 3)
     clip_factor = jnp.sqrt(clip_threshold / jnp.maximum(notes[:, experts, 0], clip_threshold))
 
     mine = ep * exp_local + dp // parts
-    weight = lax.dynamic_slice_in_dim(notes, mine, 1, axis=1).reshape(all_count, 1)
+    weight = lax.dynamic_slice_in_dim(notes, mine, 1, axis=1)[..., :row_count].reshape(all_count, 1)
     flat_mid = normed_all.reshape(all_count, width)
     flat_grad = grad_all.reshape(all_count, width)
     risen = jnp.dot(flat_mid, w_rise, preferred_element_type=f32)
@@ -825,44 +970,15 @@
         grad_hidden * up_part * sigmoid_gate * (1.0 + gate_part * (1.0 - sigmoid_gate))
     ).astype(low)
     grad_up_part = (grad_hidden * silu_gate).astype(low)
-    route_high = grad_route.astype(low)
-    route_rest = (grad_route - route_high.astype(f32)).astype(low)
     both = jnp.concatenate([grad_gate_part, grad_up_part], axis=1)
     lane = lax.broadcasted_iota(jnp.int32, (1, 128), 1)
-    tail = jnp.where(lane == 0, route_high, jnp.where(lane == 1, route_rest, jnp.zeros((), low)))
-    left = jnp.concatenate([both, tail], axis=1)
-    spot = lax.broadcasted_iota(jnp.int32, (128, 128), 0)
-    across = lax.broadcasted_iota(jnp.int32, (128, 128), 1)
-    spread = ((spot < 2) & (across == mine)).astype(low)
-    right = jnp.concatenate(
-        [
-            jnp.concatenate([w_rise.T, jnp.zeros((2 * piece, 128), low)], axis=1),
-            jnp.concatenate([jnp.zeros((128, width), low), spread], axis=1),
-        ],
-        axis=0,
-    )
-    summed = scatter_sum(left, right, devices, 4)
+    beside = jnp.where(lane == mine, grad_route, 0.0).astype(low)
+    summed = scatter_sum(both, w_rise, devices, 4, turned=True, beside=beside)
     grad_rise_w = contract(flat_mid, both, "td,tf->df").astype(low)
     grad_fall_w = contract(weighted_mid, flat_grad, "tf,td->fd").astype(low)
-    back_rise = lax.all_to_all(
-        grad_rise_w.reshape(dp_count, wide_own, 2 * piece), "dp", 0, 0, tiled=True
-    )
-    back_fall = lax.all_to_all(
-        grad_fall_w.reshape(piece, dp_count, wide_own).transpose(1, 0, 2), "dp", 0, 0, tiled=True
-    )
-    resid_out = resid_mid + scatter_sum(weighted_mid, w_fall, devices, 5)
-    undeal = (jnp.arange(tok_count, dtype=jnp.int32)[:, None] == local_order[None, :]).astype(low)
-    block_out = jnp.dot(
-        undeal, (resid_out * valid_col).astype(low), preferred_element_type=f32
-    ).astype(low)
-
     def from_part(grads):
         grads = grads.reshape(exp_local, parts, wide_own, piece).transpose(0, 2, 1, 3)
         return grads.reshape(exp_local, wide_own, hidden).astype(f32)
-
-    grad_gate = from_part(back_rise[..., :piece])
-    grad_up = from_part(back_rise[..., piece:])
-    grad_down = back_fall.reshape(exp_local, hidden, wide_own).astype(f32)
 
     grad_gates = summed[:, width : width + experts]
     mean_term = jnp.sum(route * grad_gates, axis=1, keepdims=True)
@@ -871,9 +987,20 @@
     gain_part = jnp.sum(grad_normed_mid * unit_two, axis=0)
     grad_mid = grad_mid_out + norm_back(grad_normed_mid * gain_two, unit_two, inv_two)
     grad_branch = grad_mid.astype(low)
-    note_three = jnp.concatenate([grad_logits.T.astype(f32), gain_part.reshape(-1, 128)], axis=0)
-    branch_all, notes = gather_rows((grad_branch, note_three), devices, 6)
-    logits_all = notes[:, :experts].astype(low)
+    note_three = jnp.concatenate(
+        [
+            jnp.pad(grad_logits.T.astype(f32), ((0, 0), (0, 128 - row_count))),
+            gain_part.reshape(-1, 128),
+        ],
+        axis=0,
+    )
+    branch_all, notes, back_gate = gather_rows(
+        (grad_branch, note_three),
+        devices,
+        6,
+        (("dp", grad_rise_w[:, :piece].reshape(dp_count, wide_own, piece)),),
+    )
+    logits_all = notes[:, :experts, :row_count].astype(low)
     normed_own = lax.dynamic_slice_in_dim(normed_all, me * rows_own, rows_own, axis=2)
     grad_router = contract(normed_own, logits_all, "btd,bet->de")
     gain_sum = jnp.sum(notes[:, experts:], axis=0).reshape(-1)
@@ -882,7 +1009,7 @@
     flat_branch = branch_all.reshape(all_count, width)
     grad_out = contract(mixed, flat_branch, "tq,td->qd")
     grad_mixed = (
-        contract(flat_branch, w_out, "td,qd->tq").astype(low).reshape(devices, tok_count, head_dim)
+        contract(flat_branch, w_out, "td,qd->tq").astype(low).reshape(devices, row_count, head_dim)
     )
     grad_value = contract(probs_low, grad_mixed, "btu,btd->bud").astype(low)
     grad_probs = contract(grad_mixed, value_rows, "btd,bud->btu")
@@ -905,11 +1032,33 @@
         all_count, 3 * head_dim
     )
     grad_heads_w = contract(flat_unit, grad_heads, "td,tq->dq").astype(low)
-    back_heads = lax.all_to_all(
-        grad_heads_w.reshape(devices, rows_own, 3 * head_dim), everyone, 0, 0, tiled=True
-    ).astype(f32)
-    grad_unit_one = scatter_sum(grad_heads, w_heads.T, devices, 7)
-    (gain_pairs,) = gather_rows((jnp.pad(gain_pair, ((0, 6), (0, 0))),), devices, 8)
+    moe_rows, back_up = scatter_sum(
+        weighted_mid,
+        w_fall,
+        devices,
+        5,
+        riders=(("dp", grad_rise_w[:, piece:].reshape(dp_count, wide_own, piece)),),
+    )
+    resid_out = resid_mid + moe_rows
+    undeal = (jnp.arange(tok_count, dtype=jnp.int32)[:, None] == local_order[None, :]).astype(low)
+    undeal = undeal[:, :row_count]
+    block_out = jnp.dot(undeal, resid_out.astype(low), preferred_element_type=f32).astype(low)
+    grad_unit_one, back_heads, back_fall, gain_pairs = scatter_sum(
+        grad_heads,
+        w_heads,
+        devices,
+        7,
+        turned=True,
+        riders=(
+            ("all", grad_heads_w.reshape(devices, rows_own, 3 * head_dim)),
+            ("dp", grad_fall_w.reshape(piece, dp_count, wide_own).transpose(1, 0, 2)),
+            ("same", jnp.pad(gain_pair, ((0, 6), (0, 0)))),
+        ),
+    )
+    back_heads = back_heads.astype(f32)
+    grad_gate = from_part(back_gate)
+    grad_up = from_part(back_up)
+    grad_down = back_fall.reshape(exp_local, hidden, wide_own).astype(f32)
     gain_pair = jnp.sum(gain_pairs, axis=0)
     plain_query = back_heads[..., :head_dim].transpose(1, 0, 2).reshape(rows_own, -1)
 

time: 1080 us -> 1000 us (0.926)
  Pallas kernels: 734 us -> 782 us
  starting transfers between devices: 38.4 us -> 0 us
  waiting for transfers between devices: 34.2 us -> 0 us
  local copies, waits for them, and re-layouts: 49.8 us -> 32.1 us
  other arithmetic: 64.3 us -> 48.6 us
  matrix products: 142 us -> 127 us
    pallas_call x8, Pallas kernels: 734 us -> 782 us  [the longest x4 397 us: gather_rows(): pl.pallas_call(functools.partial(gather_kernel, nz, count, kinds), out_sh...]
    all_to_all x6 -> x0, starting transfers between devices: 38.4 us -> none  [the longest x1 11.8 us: by_experts(): lax.all_to_all(sent_heads, everyone, 0, 0, tiled=True)]
    all_to_all x6 -> x0, waiting for transfers between devices: 34.2 us -> none  [the longest x1 17.8 us: by_experts(): lax.all_to_all(sent_heads, everyone, 0, 0, tiled=True)]
    convert_element_type x4 -> x2, local copies, waits for them, and re-layouts: 17.8 us -> 3.88 us  [from_part(): return grads.reshape(exp_local, wide_own, hidden).astype(f32)]
    dot_general x14, matrix products: 99.1 us -> 87.9 us  [contract(): jnp.einsum(pattern, left_side, right_side, preferred_element_type=jnp.flo...]
  transfers between devices with their start and end apart: 6 -> 0, of which waited for: 2 -> 0; matrix products, arithmetic and copies ran while one was open for 16% -> 0% of each run, Pallas kernels for 69% -> 0%
where the time goes in v2:
time: 1000 us; the launch traced here: 992 us
  Pallas kernels  782 us (78%)
  matrix products  127 us (13%)
  other arithmetic  48.6 us (5%)
  local copies, waits for them, and re-layouts  32.1 us (3%)
    pallas_call x4, Pallas kernels, gather_rows(): pl.pallas_call(functools.partial(gather_kernel, nz, count, kinds), out_sh...  397 us
    pallas_call x4, Pallas kernels, scatter_sum(): pl.pallas_call(functools.partial(scatter_kernel, nz, turned, len(held), k...  385 us
    dot_general x14, matrix products, contract(): jnp.einsum(pattern, left_side, right_side, preferred_element_type=jnp.flo...  87.9 us

profile of v2, /device:TPU:1, one launch (start us, length us, event | category | flops | bytes accessed | tf_op | source)
XLA Modules:
  0.0 991.6 jit_solution(16193907710421736788)
XLA Ops:
  16.4 92.6 %gather_rows_9.1 = (bf16[32,112,2048]{2,1,0:T(8,128)(2,1)}, bf16[8,256,384]{2,1,0:T(8,128)(2,1)}) custom-call(bf16[112,2048]{1,0:T(8,128)(2,1)} %get-tuple-element.118.refs_0_, bf16[8,256,384]{2,1,0:T(8,128)(2,1)} %bitcast.166), custom_call_target="tpu_custom_call" | custom-call | tf_op jit(solution)/shard_map/gather_rows_9/pallas_call | solution.py:600
  109.0 132.3 %gather_rows_1.1 = (bf16[32,112,2048]{2,1,0:T(8,128)(2,1)}, f32[32,16,128]{2,1,0:T(8,128)}, bf16[32,64,384]{2,1,0:T(8,128)(2,1)}, bf16[8,384,256]{2,1,0:T(8,128)(2,1)}) custom-call(bf16[112,2048]{1,0:T(8,128)(2,1)} %multiply_convert_fusion.7.refs_0_, f32[16,128]{1,0:T(8,128)} %pad.34.refs_1_, bf16[32,64,384]{2,1,0:T(8,128)(2,1)} %maximum_bitcast_fusion.refs_2_, ...), custom_call_target="tpu_custom_call" | custom-call | tf_op jit(solution)/shard_map/gather_rows_1/pallas_call | solution.py:600
  241.3 2.8 copy.149
  250.7 11.9 %fusion.66 = f32[32,112,384]{2,1,0:T(8,128)S(1)} fusion(bf16[32,112,2048]{2,1,0:T(8,128)(2,1)} %get-tuple-element.35, bf16[2048,384,1]{1,0,2:T(8,128)(2,1)S(1)} %bitcast.177), kind=kOutput, calls=%fused_computation.198 | convolution fusion | flops 5637144576 | bytes 21757952 | tf_op jit(solution)/shard_map/dot_general | solution.py:915
  270.6 3.1 convolution_convert_fusion.5.refs_0_
  273.7 94.8 %scatter_sum_2.1 = (f32[112,2048]{1,0:T(8,128)}, bf16[8,256,384]{2,1,0:T(8,128)(2,1)}) custom-call(bf16[32,112,128]{2,1,0:T(8,128)(2,1)} %convolution_convert_fusion.5.refs_0_, bf16[128,2048]{1,0:T(8,128)(2,1)} %refs_1_.1, bf16[8,256,384]{2,1,0:T(8,128)(2,1)} %bitcast.161), custom_call_target="tpu_custom_call" | custom-call | tf_op jit(solution)/shard_map/scatter_sum_2/pallas_call | solution.py:779
  372.0 1.9 pad_maximum_fusion.1
  373.9 74.4 %gather_rows_3.1 = (bf16[32,112,2048]{2,1,0:T(8,128)(2,1)}, f32[32,24,128]{2,1,0:T(8,128)}) custom-call(bf16[112,2048]{1,0:T(8,128)(2,1)} %copy-done.11, f32[24,128]{1,0:T(8,128)} %pad_select_fusion.refs_1_), custom_call_target="tpu_custom_call" | custom-call | tf_op jit(solution)/shard_map/gather_rows_3/pallas_call | solution.py:600
  451.2 18.5 %fusion.67 = f32[3584,768]{1,0:T(8,128)} fusion(bf16[3584,2048]{1,0:T(8,128)(2,1)} %bitcast.184, bf16[2048,768]{1,0:T(8,128)(2,1)} %bitcast.159), kind=kOutput, calls=%fused_computation.199 | convolution fusion | flops 11274289152 | bytes 28835840 | tf_op jit(solution)/shard_map/dot_general | solution.py:960
  469.7 18.1 %multiply_convert_fusion.1 = (bf16[3584,384]{1,0:T(8,128)(2,1)}, bf16[3584,384]{1,0:T(8,128)(2,1)}, bf16[3584]{0:T(1024)(128)(2,1)S(1)}, bf16[3584,384]{1,0:T(8,128)(2,1)S(1)}) fusion(f32[3584,768]{1,0:T(8,128)} %fusion.67, f32[3584]{0:T(1024)S(1)} %mul.381, bf16[3584,2048]{1,0:T(8,128)(2,1)} %bitcast.197, bf16[384,2048]{1,0:T(8,128)(2,1)S(1)} %bitcast.165), kind=kOutput, calls=%fused_computation.4 | convolution fusion | flops 5663289856 | bytes 35542016 | tf_op jit(solution)/shard_map/td,fd->tf/dot_general | solution.py:42
  487.8 11.6 %convolution_convert_fusion.2 = bf16[384,2048]{1,0:T(8,128)(2,1)} fusion(bf16[3584,384]{1,0:T(8,128)(2,1)S(1)} %get-tuple-element.74, bf16[3584,2048]{1,0:T(8,128)(2,1)} %bitcast.198), kind=kOutput, calls=%fused_computation.15 | convolution fusion | flops 5637931008 | bytes 19005440 | tf_op jit(solution)/shard_map/tf,td->fd/dot_general | solution.py:42
  499.5 2.6 copy.133
  502.1 2.6 copy.134
  506.1 18.0 %convolution_convert_fusion.1 = bf16[2048,768]{1,0:T(8,128)(2,1)} fusion(bf16[3584,2048]{1,0:T(8,128)(2,1)} %bitcast.185, bf16[3584,384]{1,0:T(8,128)(2,1)} %get-tuple-element.72, bf16[3584,384]{1,0:T(8,128)(2,1)} %get-tuple-element.71), kind=kOutput, calls=%fused_computation.10 | convolution fusion | flops 11286872064 | bytes 23330816 | tf_op jit(solution)/shard_map/td,tf->df/dot_general | solution.py:42
  524.2 2.8 pad_maximum_fusion
  527.0 78.5 %scatter_sum_4.1 = f32[112,2176]{1,0:T(8,128)} custom-call(bf16[32,112,768]{2,1,0:T(8,128)(2,1)} %bitcast.154, bf16[2048,768]{1,0:T(8,128)(2,1)} %bitcast.160, bf16[32,112,128]{2,1,0:T(8,128)(2,1)} %select_convert_fusion.refs_2_), custom_call_target="tpu_custom_call" | custom-call | tf_op jit(solution)/shard_map/scatter_sum_4/pallas_call | solution.py:779
  605.5 3.9 fusion.58
  609.4 96.0 %scatter_sum_5.1 = (f32[112,2048]{1,0:T(8,128)}, bf16[8,256,384]{2,1,0:T(8,128)(2,1)}) custom-call(bf16[32,112,384]{2,1,0:T(8,128)(2,1)} %bitcast.171, bf16[384,2048]{1,0:T(8,128)(2,1)} %bitcast.164, bf16[8,256,384]{2,1,0:T(8,128)(2,1)} %bitcast.168), custom_call_target="tpu_custom_call" | custom-call | tf_op jit(solution)/shard_map/scatter_sum_5/pallas_call | solution.py:779
  705.4 2.4 convolution_convert_fusion.3
  711.2 1.9 copy.154
  713.1 97.5 %gather_rows_6.1 = (bf16[32,112,2048]{2,1,0:T(8,128)(2,1)}, f32[32,32,128]{2,1,0:T(8,128)}, bf16[8,256,384]{2,1,0:T(8,128)(2,1)}) custom-call(bf16[112,2048]{1,0:T(8,128)(2,1)} %get-tuple-element.67.refs_0_, f32[32,128]{1,0:T(8,128)} %pad_maximum_fusion.8.refs_1_, bf16[8,256,384]{2,1,0:T(8,128)(2,1)} %bitcast.167), custom_call_target="tpu_custom_call" | custom-call | tf_op jit(solution)/shard_map/gather_rows_6/pallas_call | solution.py:600
  810.6 2.3 convolution_bitcast_fusion.1
  814.5 8.4 convolution_bitcast_fusion
  824.3 5.1 convolution_convert_fusion
  829.4 4.0 convolution_convert_fusion.4
  833.4 2.4 multiply_reduce_fusion.5
  838.6 1.9 copy.153
  844.9 3.7 multiply_reduce_fusion.2
  849.2 2.2 multiply_convert_fusion.4
  851.5 12.0 %bitcast_convert_fusion = bf16[2048,384]{1,0:T(8,128)(2,1)} fusion(bf16[32,112,2048]{2,1,0:T(8,128)(2,1)} %get-tuple-element.35, bf16[32,112,128]{2,1,0:T(8,128)(2,1)S(1)} %copy-done.35, bf16[32,112,128]{2,1,0:T(8,128)(2,1)S(1)} %get-tuple-element.76, bf16[32,112,128]{2,1,0:T(8,128)(2,1)S(1)} %get-tuple-element.75), kind=kOutput, calls=%fused_computation.14 | convolution fusion | flops 5646188544 | bytes 19005440 | tf_op jit(solution)/shard_map/td,tq->dq/dot_general | solution.py:42
  865.3 115.6 %scatter_sum_7.1 = (f32[112,2048]{1,0:T(8,128)}, bf16[32,64,384]{2,1,0:T(8,128)(2,1)}, bf16[8,384,256]{2,1,0:T(8,128)(2,1)}, f32[32,8,128]{2,1,0:T(8,128)}) custom-call(bf16[32,112,384]{2,1,0:T(8,128)(2,1)} %pad_maximum_fusion.2.refs_0_, bf16[2048,384]{1,0:T(8,128)(2,1)} %bitcast.176, bf16[32,64,384]{2,1,0:T(8,128)(2,1)} %bitcast.181, ...), custom_call_target="tpu_custom_call" | custom-call | tf_op jit(solution)/shard_map/scatter_sum_7/pallas_call | solution.py:779
  989.2 1.9 bitcast_convert_fusion.1
  (202 shorter events, 61.8 us)
Async XLA Ops:
  0.6 10.7 %copy-start = (bf16[128,2048]{1,0:T(8,128)(2,1)S(1)}, bf16[128,2048]{1,0:T(8,128)(2,1)}, u32[]{:S(2)}) copy-start(bf16[128,2048]{1,0:T(8,128)(2,1)} %param.19) | copy-start | bytes 1572868
  0.7 7.7 copy-start.23
  1.5 8.5 copy-start.41
  10.4 2.3 copy-start.26
  10.4 2.5 copy-start.43
  248.1 2.7 copy-start.28
  249.4 17.0 %copy-start.6 = (f32[3584,128]{1,0:T(8,128)}, f32[3584,128]{1,0:T(8,128)S(1)}, u32[]{:S(2)}) copy-start(f32[3584,128]{1,0:T(8,128)S(1)} %fusion.6) | copy-start | bytes 5505028
  250.7 15.6 %copy-start.4 = (f32[3584,128]{1,0:T(8,128)}, f32[3584,128]{1,0:T(8,128)S(1)}, u32[]{:S(2)}) copy-start(f32[3584,128]{1,0:T(8,128)S(1)} %fusion.7) | copy-start | bytes 5505028
  262.6 2.5 copy-start.2
  368.6 3.4 copy-start.34
  370.3 3.7 copy-start.11
  372.0 78.6 %copy-start.45 = (f32[32]{0:T(128)S(1)}, f32[32]{0:T(128)}, u32[]{:S(2)}) copy-start(f32[32]{0:T(128)} %param.35) | copy-start | bytes 388
  451.2 18.5 %copy-start.9 = (bf16[8,48,8,256]{3,2,0,1:T(8,128)(2,1)S(1)}, bf16[8,48,8,256]{3,2,0,1:T(8,128)(2,1)}, u32[]{:S(2)}) copy-start(bf16[8,48,8,256]{3,2,0,1:T(8,128)(2,1)} %copy.149) | copy-start | bytes 4718596
  487.8 11.6 %copy-start.20 = (bf16[3584,384]{1,0:T(8,128)(2,1)}, bf16[3584,384]{1,0:T(8,128)(2,1)S(1)}, u32[]{:S(2)}) copy-start(bf16[3584,384]{1,0:T(8,128)(2,1)S(1)} %get-tuple-element.74) | copy-start | bytes 8257540
  506.1 18.0 %copy-start.21 = (bf16[3584,384]{1,0:T(8,128)(2,1)S(1)}, bf16[3584,384]{1,0:T(8,128)(2,1)}, u32[]{:S(2)}) copy-start(bf16[3584,384]{1,0:T(8,128)(2,1)} %get-tuple-element.71) | copy-start | bytes 8257540
  506.1 18.0 %copy-start.22 = (bf16[3584,384]{1,0:T(8,128)(2,1)S(1)}, bf16[3584,384]{1,0:T(8,128)(2,1)}, u32[]{:S(2)}) copy-start(bf16[3584,384]{1,0:T(8,128)(2,1)} %get-tuple-element.72) | copy-start | bytes 8257540
  705.4 2.4 slice-start.2
  705.4 2.5 copy-start.12
  713.1 101.4 %copy-start.10 = (bf16[32,112,128]{2,1,0:T(8,128)(2,1)S(1)}, bf16[32,112,128]{2,1,0:T(8,128)(2,1)}, u32[]{:S(2)}) copy-start(bf16[32,112,128]{2,1,0:T(8,128)(2,1)} %convolution_convert_fusion.5.refs_0_) | copy-start | bytes 2752516
  814.5 9.7 copy-start.3
  814.5 9.8 copy-start.37
  829.4 4.0 copy-start.8
  838.6 2.1 copy-start.7
  838.6 2.9 copy-start.19
  841.5 2.2 slice-start
  842.1 2.1 slice-start.1
  842.7 2.1 copy-start.5
  849.2 2.3 copy-start.35
  865.3 115.6 %copy-start.44 = (f32[112]{0:T(128)S(1)}, f32[112]{0:T(128)}, u32[]{:S(2)}) copy-start(f32[112]{0:T(128)} %copy-done.43) | copy-start | bytes 1348
  982.6 2.4 copy-start.33
  986.5 2.7 copy-start.30
  988.7 2.5 copy-start.1
  (17 other events, 25.3 us)

commit v3 on v2

--- a/solution.py
+++ b/solution.py
@@ -384,106 +384,166 @@
         lax.fori_loop(1, total, hello, 0)
         pl.semaphore_wait(barrier, total - 1)
         return
-    up, down, near, far, twin = ways
-
-    @pl.when(z < nz - 1)
-    def _():
-        pl.semaphore_signal(barrier, inc=1, device_id=up, device_id_type=MESH)
-
-    @pl.when(z > 0)
-    def _():
-        pl.semaphore_signal(barrier, inc=1, device_id=down, device_id_type=MESH)
-
-    for other in (near, far, twin):
+    for step in range(1, nz):
+        other = ((z + step) % nz) * 2 + dp % 2
+        pl.semaphore_signal(barrier, inc=1, device_id=(other, ep), device_id_type=MESH)
+    for other in ways[2:]:
         pl.semaphore_signal(barrier, inc=1, device_id=other, device_id_type=MESH)
-    peers = 3 + jnp.where(z < nz - 1, 1, 0) + jnp.where(z > 0, 1, 0)
-    pl.semaphore_wait(barrier, peers)
+    pl.semaphore_wait(barrier, nz + 2)
 
 
 class Riders:
-    def __init__(self, kinds, nz, dp, ep, refs):
+    def __init__(self, kinds, nz, spot, refs):
         count = len(kinds)
-        self.kinds, self.dp, self.ep = kinds, dp, ep
+        self.kinds, self.nz = kinds, nz
+        self.dp, self.ep, self.z, self.y = spot
+        self.me = self.dp * 4 + self.ep
+        self.over_y = (self.dp + 1 - 2 * self.y, self.ep)
         self.ins, self.outs = refs[:count], refs[count : 2 * count]
-        self.send, self.recv, self.own = refs[2 * count :] if count else (None, None, None)
-        self.sizes = [2 * nz if kind == "dp" else 8 * nz for kind in kinds]
-        self.at = [dp if kind == "dp" else dp * 4 + ep for kind in kinds]
-        self.steps = [(r, k) for r in range(count) for k in range(1, self.sizes[r])]
-        self.steps.sort(key=lambda step: step[1] / self.sizes[step[0]])
-
-    def device(self, r, other):
-        if self.kinds[r] == "dp":
-            return (other, self.ep)
-        return (other // 4, other % 4)
+        self.send, self.onward, self.recv, self.own = refs[2 * count :] if count else (None,) * 4
+        self.spans = []
+        for kind in kinds:
+            if kind in ("all", "same"):
+                self.spans.append((1, 8 * nz))
+            else:
+                self.spans.append((1 if kind in ("line", "cube") else 0, nz))
+        self.steps = [(r, k) for r in range(count) for k in range(*self.spans[r])]
+        self.steps.sort(key=lambda step: step[1] / self.spans[step[0]][1])
+        self.cubes = [r for r in range(count) if kinds[r] == "cube"]
+
+    def remote(self, source, target, send, recv, device):
+        return pltpu.make_async_remote_copy(
+            src_ref=source, dst_ref=target, send_sem=send, recv_sem=recv,
+            device_id=device, device_id_type=MESH)
 
     def copy(self, r, step):
-        other = (self.at[r] + step) % self.sizes[r]
-        return pltpu.make_async_remote_copy(
-            src_ref=self.ins[r] if self.kinds[r] == "same" else self.ins[r].at[other],
-            dst_ref=self.outs[r].at[self.at[r]],
-            send_sem=self.send.at[r, step],
-            recv_sem=self.recv.at[r, self.at[r]],
-            device_id=self.device(r, other),
-            device_id_type=MESH,
-        )
+        kind, source, target = self.kinds[r], self.ins[r], self.outs[r]
+        if kind in ("all", "same"):
+            other = (self.me + step) % (8 * self.nz)
+            source = source if kind == "same" else source.at[other]
+            target, key, device = target.at[self.me], self.me, (other // 4, other % 4)
+        elif kind in ("line", "cube"):
+            other = (self.z + step) % self.nz
+            source, key, device = source.at[other], self.z, (other * 2 + self.y, self.ep)
+            target = target.at[self.z] if kind == "line" else target.at[self.z, self.y]
+        else:
+            source = source.at[step, 1 - self.y] if kind == "half" else source.at[step]
+            target, key, device = target.at[step], step, self.over_y
+        return self.remote(source, target, self.send.at[r, step], self.recv.at[r, key], device)
 
     def arrival(self, r, step):
-        other = (self.at[r] + step) % self.sizes[r]
-        return pltpu.make_async_remote_copy(
-            src_ref=self.outs[r].at[other],
-            dst_ref=self.outs[r].at[other],
-            send_sem=self.send.at[r, step],
-            recv_sem=self.recv.at[r, other],
-            device_id=self.device(r, other),
-            device_id_type=MESH,
-        )
+        kind, target = self.kinds[r], self.outs[r]
+        if kind in ("all", "same"):
+            key = (self.me + step) % (8 * self.nz)
+            target = target.at[key]
+        elif kind in ("line", "cube"):
+            key = (self.z + self.nz - step) % self.nz
+            target = target.at[key] if kind == "line" else target.at[key, self.y]
+        else:
+            key, target = step, target.at[step]
+        return self.remote(target, target, self.send.at[r, step], self.recv.at[r, key], self.over_y)
+
+    def passing(self, r, step, first=False):
+        key = (self.z + self.nz - step) % self.nz
+        target = self.outs[r].at[key, self.y]
+        source = self.ins[r].at[key] if first else target
+        return self.remote(
+            source, target, self.onward.at[r, step], self.recv.at[r, self.nz + key], self.over_y)
+
+    def passed(self, r, step):
+        key = (self.z + self.nz - step) % self.nz
+        target = self.outs[r].at[key, 1 - self.y]
+        return self.remote(
+            target, target, self.onward.at[r, step], self.recv.at[r, self.nz + key], self.over_y)
 
     def own_copy(self, r):
-        here = self.ins[r] if self.kinds[r] == "same" else self.ins[r].at[self.at[r]]
-        return pltpu.make_async_copy(here, self.outs[r].at[self.at[r]], self.own.at[r])
+        kind, source, target = self.kinds[r], self.ins[r], self.outs[r]
+        if kind in ("all", "same"):
+            source = source if kind == "same" else source.at[self.me]
+            target = target.at[self.me]
+        else:
+            source = source.at[self.z]
+            target = target.at[self.z] if kind == "line" else target.at[self.z, self.y]
+        return pltpu.make_async_copy(source, target, self.own.at[r])
 
     def begin(self):
-        for r in range(len(self.kinds)):
-            self.own_copy(r).start()
+        for r, kind in enumerate(self.kinds):
+            if kind not in ("half", "across"):
+                self.own_copy(r).start()
+            if kind == "cube":
+                self.passing(r, 0, True).start()
 
     def some(self, share, shares):
         total = len(self.steps)
         for r, k in self.steps[total * share // shares : total * (share + 1) // shares]:
             self.copy(r, k).start()
 
+    def onwards(self, step):
+        for r in self.cubes:
+            self.arrival(r, step).wait_recv()
+            self.passing(r, step).start()
+
     def looped(self, step, steps):
         for r in range(len(self.kinds)):
-            per = -(-(self.sizes[r] - 1) // steps)
+            first, last = self.spans[r]
+            per = -(-(last - first) // steps)
             for k in range(per):
-                piece = 1 + step * per + k
-
-                @pl.when(piece < self.sizes[r])
+                piece = first + step * per + k
+
+                @pl.when(piece < last)
                 def _():
                     self.copy(r, piece).start()
 
     def finish(self):
-        for r in range(len(self.kinds)):
+        for r, kind in enumerate(self.kinds):
 
             def settle(step, carry):
-                self.arrival(r, step).wait_recv()
+                if kind != "cube":
+                    self.arrival(r, step).wait_recv()
                 self.copy(r, step).wait_send()
                 return carry
 
-            lax.fori_loop(1, self.sizes[r], settle, 0)
-            self.own_copy(r).wait()
+            lax.fori_loop(*self.spans[r], settle, 0)
+            if kind == "cube":
+
+                def settle_y(step, carry):
+                    self.passed(r, step).wait_recv()
+                    self.passing(r, step).wait_send()
+                    return carry
+
+                lax.fori_loop(0, self.nz, settle_y, 0)
+            if kind not in ("half", "across"):
+                self.own_copy(r).wait()
 
 
 def rider_shapes(riders, devices):
     kinds = tuple(kind for kind, _ in riders)
     arrays = tuple(array for _, array in riders)
-    outs = tuple(
-        jax.ShapeDtypeStruct(((devices,) + v.shape) if kind == "same" else v.shape, v.dtype)
-        for kind, v in riders
-    )
+    outs = []
+    for kind, v in riders:
+        shape = v.shape
+        if kind == "same":
+            shape = (devices,) + shape
+        elif kind == "cube":
+            shape = shape[:1] + (2,) + shape[1:]
+        elif kind == "half":
+            shape = shape[:1] + shape[2:]
+        outs.append(jax.ShapeDtypeStruct(shape, v.dtype))
     dma = pltpu.SemaphoreType.DMA
     count = len(riders)
-    sems = [dma((count, devices)), dma((count, devices)), dma((count,))] if count else []
-    return kinds, arrays, outs, sems
+    sems = [dma((count, devices))] * 3 + [dma((count,))] if count else []
+    return kinds, arrays, tuple(outs), sems
+
+
+def rider_specs(kinds):
+    return [
+        pl.BlockSpec(memory_space=pl.ANY if kind in ("half", "across") else pltpu.VMEM)
+        for kind in kinds
+    ]
+
+
+def wide_greeting(kinds):
+    return "all" in kinds or "same" in kinds
 
 
 def gather_kernel(nz, count, kinds, *refs):
@@ -495,12 +555,12 @@
     ways = targets(dp, ep, z, y, x, c, nz)
     twin = ways[4]
     riders = Riders(
-        kinds, nz, dp, ep,
+        kinds, nz, (dp, ep, z, y),
         refs[count : count + extra]
         + refs[2 * count + extra : 2 * (count + extra)]
         + refs[2 * (count + extra) + 3 :],
     )
-    greet(nz, z, dp, ep, ways, extra > 0)
+    greet(nz, z, dp, ep, ways, wide_greeting(kinds))
     mine = slot(z, a, b, c)
     pending = []
 
@@ -601,7 +661,7 @@
         functools.partial(gather_kernel, nz, count, kinds),
         out_shape=tuple(jax.ShapeDtypeStruct((devices,) + v.shape, v.dtype) for v in arrays)
         + rider_outs,
-        in_specs=[pl.BlockSpec(memory_space=pltpu.VMEM)] * (count + len(riders)),
+        in_specs=[pl.BlockSpec(memory_space=pltpu.VMEM)] * count + rider_specs(kinds),
         out_specs=tuple(pl.BlockSpec(memory_space=pl.ANY) for v in arrays + ridden),
         scratch_shapes=[
             pltpu.SemaphoreType.DMA((count, 5, devices)),
@@ -614,11 +674,10 @@
     )(*arrays, *ridden)
 
 
-def scatter_kernel(nz, turned, beside, kinds, *refs):
+def scatter_kernel(nz, turned, kinds, *refs):
     extra = len(kinds)
     left_ref, right_ref = refs[:2]
-    beside_ref = refs[2] if beside else None
-    refs = refs[2 + beside :]
+    refs = refs[2:]
     out_ref = refs[extra]
     sent, got, from_far, from_near, rising, falling = refs[2 * extra + 1 : 2 * extra + 7]
     (twin_send, twin_recv, far_send, far_recv, near_send, near_recv, line_send, up_recv,
@@ -627,9 +686,10 @@
     ways = targets(dp, ep, z, y, x, c, nz)
     up, down, near, far, twin = ways
     riders = Riders(
-        kinds, nz, dp, ep, refs[:extra] + refs[extra + 1 : 2 * extra + 1] + refs[2 * extra + 16 :]
-    )
-    greet(nz, z, dp, ep, ways, extra > 0)
+        kinds, nz, (dp, ep, z, y),
+        refs[:extra] + refs[extra + 1 : 2 * extra + 1] + refs[2 * extra + 16 :]
+    )
+    greet(nz, z, dp, ep, ways, wide_greeting(kinds))
     riders.begin()
     per = 4 * nz
 
@@ -643,12 +703,9 @@
 
     def term(where):
         sides = (((1,), (1 if turned else 0,)), ((), ()))
-        value = lax.dot_general(
+        return lax.dot_general(
             left_ref[where], right_ref[...], sides, preferred_element_type=jnp.float32
         )
-        if beside:
-            value = jnp.concatenate([value, beside_ref[where].astype(jnp.float32)], axis=1)
-        return value
 
     def order(index, aa, bb, cc):
         part = index // nz
@@ -766,20 +823,18 @@
     riders.finish()
 
 
-def scatter_sum(left, right, devices, ident, turned=False, beside=None, riders=()):
+def scatter_sum(left, right, devices, ident, turned=False, riders=()):
     nz = devices // 8
     rows = left.shape[0] // devices
     depth, wide = right.shape[::-1] if turned else right.shape
-    held = () if beside is None else (beside.reshape(devices, rows, -1),)
-    wide = wide + sum(v.shape[2] for v in held)
     kinds, ridden, rider_outs, rider_sems = rider_shapes(riders, devices)
     block = (rows, wide)
     low = jnp.bfloat16
     dma = pltpu.SemaphoreType.DMA
     result = pl.pallas_call(
-        functools.partial(scatter_kernel, nz, turned, len(held), kinds),
+        functools.partial(scatter_kernel, nz, turned, kinds),
         out_shape=(jax.ShapeDtypeStruct(block, jnp.float32),) + rider_outs,
-        in_specs=[pl.BlockSpec(memory_space=pltpu.VMEM)] * (2 + len(held) + len(riders)),
+        in_specs=[pl.BlockSpec(memory_space=pltpu.VMEM)] * 2 + rider_specs(kinds),
         out_specs=(pl.BlockSpec(memory_space=pltpu.VMEM),)
         + (pl.BlockSpec(memory_space=pl.ANY),) * len(riders),
         scratch_shapes=[
@@ -796,7 +851,297 @@
         compiler_params=pltpu.CompilerParams(
             collective_id=ident, has_side_effects=True, vmem_limit_bytes=58 * 2**20),
         name="scatter_sum_%d" % ident,
-    )(left.reshape(devices, rows, depth), right, *held, *ridden)
+    )(left.reshape(devices, rows, depth), right, *ridden)
+    return result if riders else result[0]
+
+
+def slab_gather_kernel(nz, count, kinds, *refs):
+    extra = len(kinds)
+    ins = refs[:count]
+    outs = refs[count + extra : 2 * count + extra]
+    send_sem, recv_sem, own_sem = refs[2 * (count + extra) : 2 * (count + extra) + 3]
+    dp, ep, z, y, x, c, _, _ = place()
+    ways = targets(dp, ep, z, y, x, c, nz)
+    side = (dp, ep + 2 - 4 * x)
+    ways = (ways[0], ways[1], side, ways[4])
+    riders = Riders(
+        kinds, nz, (dp, ep, z, y),
+        refs[count : count + extra]
+        + refs[2 * count + extra : 2 * (count + extra)]
+        + refs[2 * (count + extra) + 3 :],
+    )
+    greet(nz, z, dp, ep, (None, None, riders.over_y, side, ways[3]), False)
+    mine = z * 4 + ep
+    pending = []
+
+    def push(way, where, allowed=None, own=False):
+        for k in range(count):
+            copy = pltpu.make_async_remote_copy(
+                src_ref=ins[k] if own else outs[k].at[where],
+                dst_ref=outs[k].at[where],
+                send_sem=send_sem.at[k, way, where],
+                recv_sem=recv_sem.at[k, where],
+                device_id=ways[way],
+                device_id_type=MESH,
+            )
+            on(allowed, copy.start)
+            pending.append((allowed, copy))
+
+    def arrive(where):
+        for k in range(count):
+            pltpu.make_async_remote_copy(
+                src_ref=outs[k].at[where],
+                dst_ref=outs[k].at[where],
+                send_sem=send_sem.at[k, 0, where],
+                recv_sem=recv_sem.at[k, where],
+                device_id=side,
+                device_id_type=MESH,
+            ).wait_recv()
+
+    def on(allowed, action):
+        if allowed is None:
+            action()
+        else:
+            pl.when(allowed)(action)
+
+    own_copies = [pltpu.make_async_copy(ins[k], outs[k].at[mine], own_sem.at[k]) for k in range(count)]
+    push(0, mine, z < nz - 1, True)
+    push(1, mine, z > 0, True)
+    push(2, mine, None, True)
+    push(3, mine, None, True)
+    for copy in own_copies:
+        copy.start()
+    riders.begin()
+    riders.some(0, 1)
+
+    def along(step):
+        if step == 0:
+            yield None, z
+        else:
+            yield z >= step, jnp.maximum(z - step, 0)
+            yield z + step < nz, jnp.minimum(z + step, nz - 1)
+
+    for turn in range(1, nz + 1):
+        if turn < nz:
+            for index, (allowed, zz) in enumerate(along(turn)):
+                where = zz * 4 + ep
+                on(allowed, functools.partial(arrive, where))
+                if index == 0:
+                    push(0, where, allowed & (z < nz - 1))
+                else:
+                    push(1, where, allowed & (z > 0))
+                push(2, where, allowed)
+                push(3, where, allowed)
+        for allowed, zz in along(turn - 1):
+            where = zz * 4 + ep + 2 - 4 * x
+            on(allowed, functools.partial(arrive, where))
+            push(3, where, allowed)
+        if turn >= 2:
+            riders.onwards(turn - 1)
+    for where in range(4 * nz):
+        pl.when(where % 2 != c)(functools.partial(arrive, where))
+    for allowed, copy in pending:
+        on(allowed, copy.wait_send)
+    for copy in own_copies:
+        copy.wait()
+    riders.finish()
+
+
+def slab_gather(arrays, devices, ident, riders=()):
+    count = len(arrays)
+    nz = devices // 8
+    kinds, ridden, rider_outs, rider_sems = rider_shapes(riders, devices)
+    return pl.pallas_call(
+        functools.partial(slab_gather_kernel, nz, count, kinds),
+        out_shape=tuple(jax.ShapeDtypeStruct((4 * nz,) + v.shape, v.dtype) for v in arrays)
+        + rider_outs,
+        in_specs=[pl.BlockSpec(memory_space=pltpu.VMEM)] * count + rider_specs(kinds),
+        out_specs=tuple(pl.BlockSpec(memory_space=pl.ANY) for v in arrays + ridden),
+        scratch_shapes=[
+            pltpu.SemaphoreType.DMA((count, 4, 4 * nz)),
+            pltpu.SemaphoreType.DMA((count, 4 * nz)),
+            pltpu.SemaphoreType.DMA((count,)),
+        ]
+        + rider_sems,
+        compiler_params=pltpu.CompilerParams(collective_id=ident, has_side_effects=True),
+        name="slab_gather_%d" % ident,
+    )(*arrays, *ridden)
+
+
+def slab_scatter_kernel(nz, pairs, turned, beside, kinds, *refs):
+    extra = len(kinds)
+    lefts, rights = refs[:pairs], refs[pairs : 2 * pairs]
+    beside_ref = refs[2 * pairs] if beside else None
+    refs = refs[2 * pairs + beside :]
+    out_ref = refs[extra]
+    sent, got, from_side, rising, falling = refs[2 * extra + 1 : 2 * extra + 6]
+    (twin_send, twin_recv, side_send, side_recv, line_send, up_recv,
+     down_recv) = refs[2 * extra + 6 : 2 * extra + 13]
+    dp, ep, z, y, x, c, _, _ = place()
+    up, down, _, _, twin = targets(dp, ep, z, y, x, c, nz)
+    side = (dp, ep + 2 - 4 * x)
+    riders = Riders(
+        kinds, nz, (dp, ep, z, y),
+        refs[:extra] + refs[extra + 1 : 2 * extra + 1] + refs[2 * extra + 13 :],
+    )
+    greet(nz, z, dp, ep, (None, None, riders.over_y, side, twin), False)
+    riders.begin()
+    plain = rights[0].shape[0 if turned else 1]
+    span = 512 if plain % 512 == 0 else plain
+
+    def zed(step):
+        if nz == 4:
+            far_one = jnp.where(z < 2, 3, 0)
+            second = jnp.where(z < 2, 2 - 2 * z, 7 - 2 * z)
+            third = 1 + z % 2
+            return jnp.where(step == 0, far_one, jnp.where(step == 1, second, jnp.where(step == 2, third, z)))
+        return (z + 1 + step) % nz
+
+    def order(index, cc):
+        flip = 1 - index // nz
+        return zed(index % nz) * 4 + (x + flip * (1 - 2 * x)) * 2 + cc
+
+    def combine(target, where, added):
+        def fill(chunk, carry):
+            at = pl.ds(pl.multiple_of(chunk * span, span), span)
+            total = None
+            for left_ref, right_ref in zip(lefts, rights):
+                value = lax.dot_general(
+                    left_ref[where],
+                    right_ref[at, :] if turned else right_ref[:, at],
+                    (((1,), (1 if turned else 0,)), ((), ())),
+                    preferred_element_type=jnp.float32,
+                )
+                total = value if total is None else total + value
+            for ref in added:
+                total = total + ref[:, at].astype(jnp.float32)
+            target[:, at] = total.astype(target.dtype)
+            return carry
+
+        lax.fori_loop(0, plain // span, fill, 0)
+        if beside:
+            at = pl.ds(plain, beside_ref.shape[2])
+            total = beside_ref[where].astype(jnp.float32)
+            for ref in added:
+                total = total + ref[:, at].astype(jnp.float32)
+            target[:, at] = total.astype(target.dtype)
+
+    def twin_copy(index):
+        return pltpu.make_async_remote_copy(
+            src_ref=sent.at[index], dst_ref=got.at[index], send_sem=twin_send.at[index],
+            recv_sem=twin_recv.at[index], device_id=twin, device_id_type=MESH)
+
+    def side_copy(index):
+        return pltpu.make_async_remote_copy(
+            src_ref=got.at[index], dst_ref=from_side.at[index], send_sem=side_send.at[index],
+            recv_sem=side_recv.at[index], device_id=side, device_id_type=MESH)
+
+    def up_copy(index, zz):
+        return pltpu.make_async_remote_copy(
+            src_ref=got.at[nz + index], dst_ref=rising.at[zz], send_sem=line_send.at[index],
+            recv_sem=up_recv.at[zz], device_id=up, device_id_type=MESH)
+
+    def down_copy(index, zz):
+        return pltpu.make_async_remote_copy(
+            src_ref=got.at[nz + index], dst_ref=falling.at[zz], send_sem=line_send.at[index],
+            recv_sem=down_recv.at[zz], device_id=down, device_id_type=MESH)
+
+    def give(index, carry):
+        combine(sent.at[index], order(index, 1 - c), ())
+        twin_copy(index).start()
+        return carry
+
+    def side_step(step, carry):
+        lax.fori_loop(2 * step, 2 * step + 2, give, 0)
+        twin_copy(step).wait_recv()
+        combine(got.at[step], order(step, c), (got.at[step],))
+        side_copy(step).start()
+        riders.looped(step, nz)
+        return carry
+
+    lax.fori_loop(0, nz, side_step, 0)
+
+    def line_step(step, carry):
+        zz = zed(step)
+        twin_copy(nz + step).wait_recv()
+        side_copy(step).wait_recv()
+        combine(out_ref, order(nz + step, c), (got.at[nz + step], from_side.at[step]))
+
+        @pl.when((zz >= z) & (z > 0))
+        def _():
+            up_copy(step, zz).wait_recv()
+            out_ref[...] += rising[zz].astype(jnp.float32)
+
+        @pl.when((zz <= z) & (z < nz - 1))
+        def _():
+            down_copy(step, zz).wait_recv()
+            out_ref[...] += falling[zz].astype(jnp.float32)
+
+        @pl.when(zz > z)
+        def _():
+            got[nz + step] = out_ref[...].astype(got.dtype)
+            up_copy(step, zz).start()
+
+        @pl.when(zz < z)
+        def _():
+            got[nz + step] = out_ref[...].astype(got.dtype)
+            down_copy(step, zz).start()
+
+        return carry
+
+    lax.fori_loop(0, nz, line_step, 0)
+
+    def finish(step, carry):
+        twin_copy(step).wait_send()
+        return carry
+
+    lax.fori_loop(0, 2 * nz, finish, 0)
+
+    def finish_side(step, carry):
+        side_copy(step).wait_send()
+
+        @pl.when(step < nz - 1)
+        def _():
+            up_copy(step, 0).wait_send()
+
+        return carry
+
+    lax.fori_loop(0, nz, finish_side, 0)
+    riders.finish()
+
+
+def slab_scatter(lefts, rights, devices, ident, turned=False, beside=None, riders=()):
+    nz = devices // 8
+    blocks = 4 * nz
+    rows = lefts[0].shape[0] // blocks
+    wide = rights[0].shape[0 if turned else 1]
+    held = () if beside is None else (beside.reshape(blocks, rows, -1),)
+    wide = wide + sum(v.shape[2] for v in held)
+    kinds, ridden, rider_outs, rider_sems = rider_shapes(riders, devices)
+    block = (rows, wide)
+    low = jnp.bfloat16
+    dma = pltpu.SemaphoreType.DMA
+    pairs = len(lefts)
+    result = pl.pallas_call(
+        functools.partial(slab_scatter_kernel, nz, pairs, turned, len(held), kinds),
+        out_shape=(jax.ShapeDtypeStruct(block, jnp.float32),) + rider_outs,
+        in_specs=[pl.BlockSpec(memory_space=pltpu.VMEM)] * (2 * pairs + len(held))
+        + rider_specs(kinds),
+        out_specs=(pl.BlockSpec(memory_space=pltpu.VMEM),)
+        + (pl.BlockSpec(memory_space=pl.ANY),) * len(riders),
+        scratch_shapes=[
+            pltpu.VMEM((2 * nz,) + block, low),
+            pltpu.VMEM((2 * nz,) + block, low),
+            pltpu.VMEM((nz,) + block, low),
+            pltpu.VMEM((nz,) + block, low),
+            pltpu.VMEM((nz,) + block, low),
+            dma((2 * nz,)), dma((2 * nz,)), dma((nz,)), dma((nz,)), dma((nz,)), dma((nz,)), dma((nz,)),
+        ]
+        + rider_sems,
+        compiler_params=pltpu.CompilerParams(
+            collective_id=ident, has_side_effects=True, vmem_limit_bytes=58 * 2**20),
+        name="slab_scatter_%d" % ident,
+    )(*(v.reshape(blocks, rows, -1) for v in lefts), *rights, *held, *ridden)
     return result if riders else result[0]
 
 
@@ -860,8 +1205,9 @@
     group_size = head_count // kv_count
     experts = w_router.shape[1]
     exp_local, wide_own, hidden = w_gate.shape
-    parts = dp_count // exp_local
-    piece = hidden // parts
+    lines = dp_count // 2
+    slab = lines * ep_count
+    z, y = dp // 2, dp % 2
     score_scale = head_dim ** (-0.5)
 
     gain_col = gain_attn.astype(f32)[:, None]
@@ -872,9 +1218,6 @@
         [heads_in, jnp.repeat(keys_in, group_size, axis=1), jnp.repeat(values_in, group_size, axis=1)],
         axis=2,
     ).transpose(1, 0, 2)
-    def by_part(weights):
-        weights = weights.reshape(exp_local, wide_own, parts, piece).transpose(0, 2, 1, 3)
-        return weights.reshape(dp_count, wide_own, piece)
 
     local_order = deal_order % tok_count
     deal = (local_order[:, None] == jnp.arange(tok_count, dtype=jnp.int32)[None, :]).astype(low)
@@ -888,17 +1231,14 @@
     router_rows = w_router.astype(f32).reshape(-1, 128)
     note_one = jnp.concatenate([lens_row, gain_row, router_rows], axis=0)
     note_one = jnp.pad(note_one, ((0, -note_one.shape[0] % 8), (0, 0)))
-    unit_all, notes, w_heads, w_fall = gather_rows(
-        (unit_one.astype(low), note_one),
-        devices,
-        1,
-        (("all", sent_heads), ("dp", w_down.reshape(dp_count, piece, wide_own))),
+    unit_all, notes, w_heads = gather_rows(
+        (unit_one.astype(low), note_one), devices, 1, (("all", sent_heads),)
     )
     w_heads = w_heads.reshape(width, 3 * head_dim)
-    w_fall = w_fall.transpose(1, 0, 2).reshape(piece, width)
-    grad_all, w_rise_up = gather_rows(
-        (grad_mid_out.astype(low),), devices, 9, (("dp", by_part(w_up)),)
-    )
+    grad_all, w_rise_up = slab_gather(
+        (grad_mid_out.astype(low),), devices, 9, (("cube", w_up),)
+    )
+    w_rise_up = w_rise_up.reshape(width, hidden)
     lens_all = notes[:, 0, : seq_lengths.shape[1]].astype(jnp.int32)
     gain_two = notes[:, 1, :rows_own].reshape(1, width)
     router_full = notes[:, 2 : 2 + router_rows.shape[0]].reshape(width, experts)
@@ -934,11 +1274,8 @@
     probs_low = probs.astype(low)
     mixed = contract(probs_low, value_rows, "btu,bud->btd").astype(low).reshape(all_count, head_dim)
     largest_own = jnp.max(row_top)
-    branch, w_rise_gate = scatter_sum(
-        mixed, w_out, devices, 2, riders=(("dp", by_part(w_gate)),)
-    )
+    branch, fall_own = scatter_sum(mixed, w_out, devices, 2, riders=(("line", w_down),))
     resid_mid = resid_in + branch
-    w_rise = jnp.concatenate([w_rise_gate, w_rise_up], axis=2).reshape(width, 2 * piece)
 
     inv_two = rms_scale(resid_mid)
     unit_two = resid_mid * inv_two
@@ -948,17 +1285,23 @@
     picked = jnp.where(choose, logits, masked_fill)
     gate_power = jnp.where(choose, jnp.exp(picked - jnp.max(picked, axis=1, keepdims=True)), 0.0)
     route = gate_power / jnp.sum(gate_power, axis=1, keepdims=True)
-    note_two = jnp.concatenate([route.T, jnp.full((8, row_count), largest_own, f32)], axis=0)
-    note_two = jnp.pad(note_two, ((0, 0), (0, 128 - row_count)))
-    normed_all, notes = gather_rows((normed_mid, note_two), devices, 3)
-    clip_factor = jnp.sqrt(clip_threshold / jnp.maximum(notes[:, experts, 0], clip_threshold))
-
-    mine = ep * exp_local + dp // parts
-    weight = lax.dynamic_slice_in_dim(notes, mine, 1, axis=1)[..., :row_count].reshape(all_count, 1)
-    flat_mid = normed_all.reshape(all_count, width)
-    flat_grad = grad_all.reshape(all_count, width)
-    risen = jnp.dot(flat_mid, w_rise, preferred_element_type=f32)
-    gate_part, up_part = risen[:, :piece], risen[:, piece:]
+    note_two = jnp.pad(route.T, ((0, 0), (0, 128 - row_count)))
+    normed_all, notes, w_rise_gate, fall_other = slab_gather(
+        (normed_mid, note_two), devices, 3, (("cube", w_gate), ("across", fall_own))
+    )
+    w_rise_gate = w_rise_gate.reshape(width, hidden)
+    w_fall = jnp.where(
+        y == 0, jnp.stack([fall_own, fall_other], axis=1), jnp.stack([fall_other, fall_own], axis=1)
+    )
+    w_fall = w_fall.transpose(2, 0, 1, 3).reshape(hidden, width)
+
+    mine = ep * exp_local + z
+    slab_rows = slab * row_count
+    weight = lax.dynamic_slice_in_dim(notes, mine, 1, axis=1)[..., :row_count].reshape(slab_rows, 1)
+    flat_mid = normed_all.reshape(slab_rows, width)
+    flat_grad = grad_all.reshape(slab_rows, width)
+    gate_part = jnp.dot(flat_mid, w_rise_gate, preferred_element_type=f32)
+    up_part = jnp.dot(flat_mid, w_rise_up, preferred_element_type=f32)
     grad_plain = contract(flat_grad, w_fall, "td,fd->tf")
     sigmoid_gate = jax.nn.sigmoid(gate_part)
     silu_gate = gate_part * sigmoid_gate
@@ -970,15 +1313,28 @@
         grad_hidden * up_part * sigmoid_gate * (1.0 + gate_part * (1.0 - sigmoid_gate))
     ).astype(low)
     grad_up_part = (grad_hidden * silu_gate).astype(low)
-    both = jnp.concatenate([grad_gate_part, grad_up_part], axis=1)
     lane = lax.broadcasted_iota(jnp.int32, (1, 128), 1)
     beside = jnp.where(lane == mine, grad_route, 0.0).astype(low)
-    summed = scatter_sum(both, w_rise, devices, 4, turned=True, beside=beside)
-    grad_rise_w = contract(flat_mid, both, "td,tf->df").astype(low)
-    grad_fall_w = contract(weighted_mid, flat_grad, "tf,td->fd").astype(low)
-    def from_part(grads):
-        grads = grads.reshape(exp_local, parts, wide_own, piece).transpose(0, 2, 1, 3)
-        return grads.reshape(exp_local, wide_own, hidden).astype(f32)
+
+    def for_each_y(grads):
+        return grads.astype(low).reshape(lines, 2, wide_own, hidden)
+
+    gate_halves = for_each_y(contract(flat_mid, grad_gate_part, "td,tf->df"))
+    up_halves = for_each_y(contract(flat_mid, grad_up_part, "td,tf->df"))
+    fall_halves = for_each_y(contract(flat_grad, weighted_mid, "td,tf->df"))
+    summed, gate_come, up_come = slab_scatter(
+        (grad_gate_part, grad_up_part),
+        (w_rise_gate, w_rise_up),
+        devices,
+        4,
+        turned=True,
+        beside=beside,
+        riders=(("half", gate_halves), ("half", up_halves)),
+    )
+
+    def add_halves(halves, come):
+        kept = lax.dynamic_index_in_dim(halves, y, axis=1, keepdims=False)
+        return (kept.astype(f32) + come.astype(f32)).astype(low)
 
     grad_gates = summed[:, width : width + experts]
     mean_term = jnp.sum(route * grad_gates, axis=1, keepdims=True)
@@ -987,23 +1343,19 @@
     gain_part = jnp.sum(grad_normed_mid * unit_two, axis=0)
     grad_mid = grad_mid_out + norm_back(grad_normed_mid * gain_two, unit_two, inv_two)
     grad_branch = grad_mid.astype(low)
+    router_part = contract(normed_mid, grad_logits, "td,te->de").reshape(devices, -1, 128)
     note_three = jnp.concatenate(
         [
-            jnp.pad(grad_logits.T.astype(f32), ((0, 0), (0, 128 - row_count))),
             gain_part.reshape(-1, 128),
+            jnp.full((8, 128), largest_own, f32),
         ],
         axis=0,
     )
-    branch_all, notes, back_gate = gather_rows(
-        (grad_branch, note_three),
-        devices,
-        6,
-        (("dp", grad_rise_w[:, :piece].reshape(dp_count, wide_own, piece)),),
-    )
-    logits_all = notes[:, :experts, :row_count].astype(low)
-    normed_own = lax.dynamic_slice_in_dim(normed_all, me * rows_own, rows_own, axis=2)
-    grad_router = contract(normed_own, logits_all, "btd,bet->de")
-    gain_sum = jnp.sum(notes[:, experts:], axis=0).reshape(-1)
+    branch_all, notes, back_up = gather_rows(
+        (grad_branch, note_three), devices, 6, (("line", add_halves(up_halves, up_come)),)
+    )
+    clip_factor = jnp.sqrt(clip_threshold / jnp.maximum(notes[:, -1, 0], clip_threshold))
+    gain_sum = jnp.sum(notes[:, :-8], axis=0).reshape(-1)
     grad_gain_moe = lax.dynamic_slice_in_dim(gain_sum, me * rows_own, rows_own)
 
     flat_branch = branch_all.reshape(all_count, width)
@@ -1032,18 +1384,18 @@
         all_count, 3 * head_dim
     )
     grad_heads_w = contract(flat_unit, grad_heads, "td,tq->dq").astype(low)
-    moe_rows, back_up = scatter_sum(
-        weighted_mid,
-        w_fall,
+    moe_rows, back_gate, fall_come = slab_scatter(
+        (weighted_mid,),
+        (w_fall,),
         devices,
         5,
-        riders=(("dp", grad_rise_w[:, piece:].reshape(dp_count, wide_own, piece)),),
+        riders=(("line", add_halves(gate_halves, gate_come)), ("half", fall_halves)),
     )
     resid_out = resid_mid + moe_rows
     undeal = (jnp.arange(tok_count, dtype=jnp.int32)[:, None] == local_order[None, :]).astype(low)
     undeal = undeal[:, :row_count]
     block_out = jnp.dot(undeal, resid_out.astype(low), preferred_element_type=f32).astype(low)
-    grad_unit_one, back_heads, back_fall, gain_pairs = scatter_sum(
+    grad_unit_one, back_heads, back_fall, gain_pairs, router_parts = scatter_sum(
         grad_heads,
         w_heads,
         devices,
@@ -1051,14 +1403,16 @@
         turned=True,
         riders=(
             ("all", grad_heads_w.reshape(devices, rows_own, 3 * head_dim)),
-            ("dp", grad_fall_w.reshape(piece, dp_count, wide_own).transpose(1, 0, 2)),
+            ("line", add_halves(fall_halves, fall_come)),
             ("same", jnp.pad(gain_pair, ((0, 6), (0, 0)))),
+            ("all", router_part),
         ),
     )
     back_heads = back_heads.astype(f32)
-    grad_gate = from_part(back_gate)
-    grad_up = from_part(back_up)
-    grad_down = back_fall.reshape(exp_local, hidden, wide_own).astype(f32)
+    grad_gate = back_gate.astype(f32)
+    grad_up = back_up.astype(f32)
+    grad_down = back_fall.transpose(0, 2, 1).astype(f32)
+    grad_router = jnp.sum(router_parts, axis=0).reshape(rows_own, experts)
     gain_pair = jnp.sum(gain_pairs, axis=0)
     plain_query = back_heads[..., :head_dim].transpose(1, 0, 2).reshape(rows_own, -1)
 

time: 1000 us -> 961 us (0.961)
  Pallas kernels: 782 us -> 731 us
    pallas_call x4 -> x2, Pallas kernels: 397 us -> 185 us  [gather_rows(): pl.pallas_call(functools.partial(gather_kernel, nz, count, kinds), out_sh...]
    pallas_call x4 -> x6, Pallas kernels: 385 us -> 545 us  [the longest x2 204 us: scatter_sum(): pl.pallas_call(functools.partial(scatter_kernel, nz, turned, kinds), out_...]
    convert_element_type x2 -> x6, other arithmetic: 1.95 us -> 13.5 us  [the longest x3 7.69 us: add_halves(): return (kept.astype(f32) + come.astype(f32)).astype(low)]
    dot_general x1 -> x2, matrix products: 18.5 us -> 20.4 us  [the longest x1 10.7 us: by_experts(): gate_part = jnp.dot(flat_mid, w_rise_gate, preferred_element_type=f32)]
    dot_general x14 -> x15, matrix products: 87.9 us -> 88.9 us  [contract(): jnp.einsum(pattern, left_side, right_side, preferred_element_type=jnp.flo...]
where the time goes in v3:
time: 961 us; the launch traced here: 951 us
  Pallas kernels  731 us (76%)
  matrix products  129 us (13%)
  other arithmetic  55.7 us (6%)
  local copies, waits for them, and re-layouts  33.4 us (3%)
    pallas_call x2, Pallas kernels, scatter_sum(): pl.pallas_call(functools.partial(scatter_kernel, nz, turned, kinds), out_...  204 us
    pallas_call x2, Pallas kernels, gather_rows(): pl.pallas_call(functools.partial(gather_kernel, nz, count, kinds), out_sh...  185 us
    pallas_call x2, Pallas kernels, slab_gather(): pl.pallas_call(functools.partial(slab_gather_kernel, nz, count, kinds), o...  181 us
    pallas_call x2, Pallas kernels, slab_scatter(): pl.pallas_call(functools.partial(slab_scatter_kernel, nz, pairs, turned,...  160 us
    dot_general x15, matrix products, contract(): jnp.einsum(pattern, left_side, right_side, preferred_element_type=jnp.flo...  88.9 us

profile of v3, /device:TPU:1, one launch (start us, length us, event | category | flops | bytes accessed | tf_op | source)
XLA Modules:
  0.0 950.6 jit_solution(16935719642633206454)
XLA Ops:
  13.0 89.8 %slab_gather_9.1 = (bf16[16,112,2048]{2,1,0:T(8,128)(2,1)}, bf16[4,2,256,768]{3,2,1,0:T(8,128)(2,1)}) custom-call(bf16[112,2048]{1,0:T(8,128)(2,1)} %get-tuple-element.210.refs_0_, bf16[4,256,768]{2,1,0:T(8,128)(2,1)} %refs_1_.3), custom_call_target="tpu_custom_call" | custom-call | tf_op jit(solution)/shard_map/slab_gather_9/pallas_call | solution.py:954
  102.8 96.5 %gather_rows_1.1 = (bf16[32,112,2048]{2,1,0:T(8,128)(2,1)}, f32[32,16,128]{2,1,0:T(8,128)}, bf16[32,64,384]{2,1,0:T(8,128)(2,1)}) custom-call(bf16[112,2048]{1,0:T(8,128)(2,1)} %multiply_convert_fusion.7.refs_0_, f32[16,128]{1,0:T(8,128)} %pad.27.refs_1_, bf16[32,64,384]{2,1,0:T(8,128)(2,1)} %maximum_bitcast_fusion.refs_2_), custom_call_target="tpu_custom_call" | custom-call | tf_op jit(solution)/shard_map/gather_rows_1/pallas_call | solution.py:660
  206.0 11.9 %fusion.66 = f32[32,112,384]{2,1,0:T(8,128)S(1)} fusion(bf16[32,112,2048]{2,1,0:T(8,128)(2,1)} %get-tuple-element.41, bf16[2048,384,1]{1,0,2:T(8,128)(2,1)S(1)} %bitcast.177), kind=kOutput, calls=%fused_computation.190 | convolution fusion | flops 5637144576 | bytes 21757952 | tf_op jit(solution)/shard_map/dot_general | solution.py:1255
  226.0 4.3 convolution_convert_fusion.6.refs_0_
  230.4 90.4 %scatter_sum_2.1 = (f32[112,2048]{1,0:T(8,128)}, bf16[4,768,256]{2,1,0:T(8,128)(2,1)}) custom-call(bf16[32,112,128]{2,1,0:T(8,128)(2,1)} %convolution_convert_fusion.6.refs_0_, bf16[128,2048]{1,0:T(8,128)(2,1)} %refs_1_.2, bf16[4,768,256]{2,1,0:T(8,128)(2,1)} %refs_2_.2), custom_call_target="tpu_custom_call" | custom-call | tf_op jit(solution)/shard_map/scatter_sum_2/pallas_call | solution.py:834
  323.7 91.3 %slab_gather_3.1 = (bf16[16,112,2048]{2,1,0:T(8,128)(2,1)}, f32[16,16,128]{2,1,0:T(8,128)}, bf16[4,2,256,768]{3,2,1,0:T(8,128)(2,1)}, bf16[4,768,256]{2,1,0:T(8,128)(2,1)}) custom-call(bf16[112,2048]{1,0:T(8,128)(2,1)} %copy-done.12, f32[16,128]{1,0:T(8,128)} %pad.28.refs_1_, bf16[4,256,768]{2,1,0:T(8,128)(2,1)} %refs_2_.3, ...), custom_call_target="tpu_custom_call" | custom-call | tf_op jit(solution)/shard_map/slab_gather_3/pallas_call | solution.py:954
  415.9 3.4 fusion.2
  419.3 4.9 copy.137
  424.2 6.5 reshape.434.refs_1_
  430.7 10.7 %fusion.68 = f32[1792,768]{1,0:T(8,128)} fusion(bf16[1792,2048]{1,0:T(8,128)(2,1)} %bitcast.196, bf16[2048,768]{1,0:T(8,128)(2,1)} %bitcast.169), kind=kOutput, calls=%fused_computation.192 | convolution fusion | flops 5637144576 | bytes 15990784 | tf_op jit(solution)/shard_map/dot_general | solution.py:1303
  441.4 9.7 %fusion.69 = f32[1792,768]{1,0:T(8,128)} fusion(bf16[1792,2048]{1,0:T(8,128)(2,1)} %bitcast.197, bf16[2048,768]{1,0:T(8,128)(2,1)S(1)} %bitcast.168), kind=kOutput, calls=%fused_computation.193 | convolution fusion | flops 5637144576 | bytes 15990784 | tf_op jit(solution)/shard_map/dot_general | solution.py:1304
  451.1 17.4 %multiply_reduce_fusion = (bf16[1792]{0:T(1024)(128)(2,1)S(1)}, bf16[1792,768]{1,0:T(8,128)(2,1)}, bf16[1792,768]{1,0:T(8,128)(2,1)S(1)}, bf16[1792,768]{1,0:T(8,128)(2,1)}) fusion(f32[1792,768]{1,0:T(8,128)} %fusion.69, f32[1792,768]{1,0:T(8,128)} %fusion.68, f32[1792]{0:T(1024)S(1)} %mul.380, bf16[1792,2048]{1,0:T(8,128)(2,1)} %bitcast.192, ...), kind=kOutput, calls=%fused_computation.1 | convolution fusion | flops 5663291392 | bytes 29764096 | tf_op jit(solution)/shard_map/td,fd->tf/dot_general | solution.py:42
  468.6 7.8 convolution_convert_fusion.1
  477.6 10.4 %convolution_convert_fusion.3 = bf16[2048,768]{1,0:T(8,128)(2,1)} fusion(bf16[1792,2048]{1,0:T(8,128)(2,1)} %bitcast.198, bf16[1792,768]{1,0:T(8,128)(2,1)} %get-tuple-element.174), kind=kOutput, calls=%fused_computation.10 | convolution fusion | flops 5638717440 | bytes 13238272 | tf_op jit(solution)/shard_map/td,tf->df/dot_general | solution.py:42
  488.0 10.7 %convolution_convert_fusion.2 = bf16[2048,768]{1,0:T(8,128)(2,1)} fusion(bf16[1792,2048]{1,0:T(8,128)(2,1)} %bitcast.199, bf16[1792,768]{1,0:T(8,128)(2,1)S(1)} %copy-done.25), kind=kOutput, calls=%fused_computation.9 | convolution fusion | flops 5638717440 | bytes 13238272 | tf_op jit(solution)/shard_map/td,tf->df/dot_general | solution.py:42
  498.7 87.0 %slab_scatter_4.1 = (f32[112,2176]{1,0:T(8,128)}, bf16[4,256,768]{2,1,0:T(8,128)(2,1)}, bf16[4,256,768]{2,1,0:T(8,128)(2,1)}) custom-call(bf16[16,112,768]{2,1,0:T(8,128)(2,1)} %bitcast.171, bf16[16,112,768]{2,1,0:T(8,128)(2,1)} %bitcast.172, bf16[2048,768]{1,0:T(8,128)(2,1)} %bitcast.170, bf16[2048,768]{1,0:T(8,128)(2,1)} %bitcast.167, ...), custom_call_target="tpu_custom_call" | custom-call | tf_op jit(solution)/shard_map/slab_scatter_4/pallas_call | solution.py:1125
  585.7 3.1 fusion.4.refs_2_
  590.4 72.9 %slab_scatter_5.1 = (f32[112,2048]{1,0:T(8,128)}, bf16[4,256,768]{2,1,0:T(8,128)(2,1)}, bf16[4,256,768]{2,1,0:T(8,128)(2,1)}) custom-call(bf16[16,112,768]{2,1,0:T(8,128)(2,1)} %bitcast.173, bf16[768,2048]{1,0:T(8,128)(2,1)} %reshape.434.refs_1_, bf16[4,256,768]{2,1,0:T(8,128)(2,1)} %fusion.5.refs_2_, bf16[4,2,256,768]{3,2,1,0:T(8,128)(2,1)} %bitcast.164), custom_call_target="tpu_custom_call" | custom-call | tf_op jit(solution)/shard_map/slab_scatter_5/pallas_call | solution.py:1125
  663.4 3.0 fusion.3.refs_3_
  668.6 2.7 multiply_reduce_fusion.9
  673.6 2.3 fusion.59
  679.1 89.0 %gather_rows_6.1 = (bf16[32,112,2048]{2,1,0:T(8,128)(2,1)}, f32[32,24,128]{2,1,0:T(8,128)}, bf16[4,256,768]{2,1,0:T(8,128)(2,1)}) custom-call(bf16[112,2048]{1,0:T(8,128)(2,1)} %get-tuple-element.169.refs_0_, f32[24,128]{1,0:T(8,128)} %concatenate.32.refs_1_, bf16[4,256,768]{2,1,0:T(8,128)(2,1)} %fusion.4.refs_2_), custom_call_target="tpu_custom_call" | custom-call | tf_op jit(solution)/shard_map/gather_rows_6/pallas_call | solution.py:660
  771.4 8.4 convolution_bitcast_fusion
  781.2 5.1 convolution_convert_fusion
  786.3 4.0 convolution_convert_fusion.5
  790.3 2.4 multiply_reduce_fusion.5
  801.6 3.7 multiply_reduce_fusion.2
  805.8 2.2 multiply_convert_fusion.4
  808.1 12.0 %bitcast_convert_fusion = bf16[2048,384]{1,0:T(8,128)(2,1)} fusion(bf16[32,112,2048]{2,1,0:T(8,128)(2,1)} %get-tuple-element.41, bf16[32,112,128]{2,1,0:T(8,128)(2,1)S(1)} %copy-done.37, bf16[32,112,128]{2,1,0:T(8,128)(2,1)S(1)} %get-tuple-element.178, bf16[32,112,128]{2,1,0:T(8,128)(2,1)S(1)} %get-tuple-element.177), kind=kOutput, calls=%fused_computation.19 | convolution fusion | flops 5646188544 | bytes 19005440 | tf_op jit(solution)/shard_map/td,tq->dq/dot_general | solution.py:42
  822.0 114.0 %scatter_sum_7.1 = (f32[112,2048]{1,0:T(8,128)}, bf16[32,64,384]{2,1,0:T(8,128)(2,1)}, bf16[4,256,768]{2,1,0:T(8,128)(2,1)}, f32[32,8,128]{2,1,0:T(8,128)}, f32[32,8,128]{2,1,0:T(8,128)}) custom-call(bf16[32,112,384]{2,1,0:T(8,128)(2,1)} %pad_maximum_fusion.refs_0_, bf16[2048,384]{1,0:T(8,128)(2,1)} %bitcast.176, bf16[32,64,384]{2,1,0:T(8,128)(2,1)} %bitcast.178, ...), custom_call_target="tpu_custom_call" | custom-call | tf_op jit(solution)/shard_map/scatter_sum_7/pallas_call | solution.py:834
  945.0 1.9 convert_bitcast_fusion
  946.9 3.5 copy.147
  (228 shorter events, 65.8 us)
Async XLA Ops:
  0.6 10.9 %copy-start = (bf16[128,2048]{1,0:T(8,128)(2,1)S(1)}, bf16[128,2048]{1,0:T(8,128)(2,1)}, u32[]{:S(2)}) copy-start(bf16[128,2048]{1,0:T(8,128)(2,1)} %param.19) | copy-start | bytes 1572868
  0.7 7.9 copy-start.27
  1.5 8.7 copy-start.48
  2.1 216.9 %copy-start.52 = (f32[128]{0:T(128)}, f32[128]{0:T(128)S(1)}, u32[]{:S(2)}) copy-start(f32[128]{0:T(128)S(1)} %convert_element_type.241) | copy-start | bytes 1540
  2.8 216.3 %copy-start.54 = (f32[128]{0:T(128)}, f32[128]{0:T(128)S(1)}, u32[]{:S(2)}) copy-start(f32[128]{0:T(128)S(1)} %convert_element_type.244) | copy-start | bytes 1540
  10.6 310.2 %copy-start.4 = (f32[112,2048]{1,0:T(8,128)}, f32[112,2048]{1,0:T(8,128)S(1)}, u32[]{:S(2)}) copy-start(f32[112,2048]{1,0:T(8,128)S(1)} %get-tuple-element.207) | copy-start | bytes 2752516
  10.6 92.3 %copy-start.50 = (f32[112]{0:T(128)}, f32[112]{0:T(128)S(1)}, u32[]{:S(2)}) copy-start(f32[112]{0:T(128)S(1)} %add_rsqrt_fusion.3) | copy-start | bytes 1348
  204.6 17.0 %copy-start.8 = (f32[3584,128]{1,0:T(8,128)}, f32[3584,128]{1,0:T(8,128)S(1)}, u32[]{:S(2)}) copy-start(f32[3584,128]{1,0:T(8,128)S(1)} %fusion.10) | copy-start | bytes 5505028
  206.0 15.7 %copy-start.6 = (f32[3584,128]{1,0:T(8,128)}, f32[3584,128]{1,0:T(8,128)S(1)}, u32[]{:S(2)}) copy-start(f32[3584,128]{1,0:T(8,128)S(1)} %fusion.11) | copy-start | bytes 5505028
  430.7 10.7 %copy-start.24 = (bf16[4,2,256,768]{3,2,1,0:T(8,128)(2,1)S(1)}, bf16[4,2,256,768]{3,2,1,0:T(8,128)(2,1)}, u32[]{:S(2)}) copy-start(bf16[4,2,256,768]{3,2,1,0:T(8,128)(2,1)} %get-tuple-element.47) | copy-start | bytes 9437188
  441.4 9.7 %copy-start.10 = (bf16[768,2048]{1,0:T(8,128)(2,1)S(1)}, bf16[768,2048]{1,0:T(8,128)(2,1)}, u32[]{:S(2)}) copy-start(bf16[768,2048]{1,0:T(8,128)(2,1)} %reshape.434.refs_1_) | copy-start | bytes 9437188
  441.4 27.2 %slice-start.2 = ((s8[7340032]{0:T(1024)(128)(4,1)}), s8[3145728]{0:T(1024)(128)(4,1)S(1)}, s32[]{:S(2)}) async-start(s8[7340032]{0:T(1024)(128)(4,1)} %bitcast.193), calls=%async_computation.2 | async-start | bytes 6291456
  451.1 17.4 %slice-start.3 = ((s8[7340032]{0:T(1024)(128)(4,1)}), s8[4194304]{0:T(1024)(128)(4,1)S(1)}, s32[]{:S(2)}) async-start(s8[7340032]{0:T(1024)(128)(4,1)} %bitcast.193), calls=%async_computation.3 | async-start | bytes 8388608
  468.6 7.8 copy-start.26
  477.6 10.4 %copy-start.25 = (bf16[1792,768]{1,0:T(8,128)(2,1)S(1)}, bf16[1792,768]{1,0:T(8,128)(2,1)}, u32[]{:S(2)}) copy-start(bf16[1792,768]{1,0:T(8,128)(2,1)} %get-tuple-element.176) | copy-start | bytes 8257540
  498.7 87.1 %copy-start.15 = (bf16[2048,768]{1,0:T(8,128)(2,1)S(1)}, bf16[2048,768]{1,0:T(8,128)(2,1)}, u32[]{:S(2)}) copy-start(bf16[2048,768]{1,0:T(8,128)(2,1)} %convolution_convert_fusion.2) | copy-start | bytes 9437188
  585.7 3.1 copy-start.14
  585.7 3.1 copy-start.30
  590.4 72.9 %copy-start.16 = (bf16[2048,768]{1,0:T(8,128)(2,1)S(1)}, bf16[2048,768]{1,0:T(8,128)(2,1)}, u32[]{:S(2)}) copy-start(bf16[2048,768]{1,0:T(8,128)(2,1)} %convolution_convert_fusion.1) | copy-start | bytes 9437188
  663.3 3.0 copy-start.36
  667.5 3.8 copy-start.13
  673.5 3.6 copy-start.33
  679.1 91.8 %copy-start.56 = (f32[32]{0:T(128)S(1)}, f32[32]{0:T(128)}, u32[]{:S(2)}) copy-start(f32[32]{0:T(128)} %param.35) | copy-start | bytes 388
  679.1 92.4 %copy-start.17 = (bf16[32,112,128]{2,1,0:T(8,128)(2,1)S(1)}, bf16[32,112,128]{2,1,0:T(8,128)(2,1)}, u32[]{:S(2)}) copy-start(bf16[32,112,128]{2,1,0:T(8,128)(2,1)} %convolution_convert_fusion.6.refs_0_) | copy-start | bytes 2752516
  771.4 9.7 %copy-start.3 = (bf16[32,112,2048]{2,1,0:T(8,128)(2,1)S(1)}, bf16[32,112,2048]{2,1,0:T(8,128)(2,1)}, u32[]{:S(2)}) copy-start(bf16[32,112,2048]{2,1,0:T(8,128)(2,1)} %get-tuple-element.55) | copy-start | bytes 44040196
  771.4 9.8 %copy-start.39 = (bf16[128,2048]{1,0:T(8,128)(2,1)S(1)}, bf16[128,2048]{1,0:T(8,128)(2,1)}, u32[]{:S(2)}) copy-start(bf16[128,2048]{1,0:T(8,128)(2,1)} %refs_1_.2) | copy-start | bytes 1572868
  786.3 4.0 copy-start.11
  795.3 2.9 copy-start.23
  822.0 114.1 %copy-start.5 = (f32[112,2048]{1,0:T(8,128)S(1)}, f32[112,2048]{1,0:T(8,128)}, u32[]{:S(2)}) copy-start(f32[112,2048]{1,0:T(8,128)} %copy-done.4) | copy-start | bytes 2752516
  822.0 114.1 %copy-start.51 = (f32[112]{0:T(128)S(1)}, f32[112]{0:T(128)}, u32[]{:S(2)}) copy-start(f32[112]{0:T(128)} %copy-done.50) | copy-start | bytes 1348
  937.6 3.2 copy-start.34
  945.0 5.5 copy-start.1
  (29 other events, 52.0 us)

commit v4 on v3

--- a/solution.py
+++ b/solution.py
@@ -546,129 +546,197 @@
     return "all" in kinds or "same" in kinds
 
 
-def gather_kernel(nz, count, kinds, *refs):
-    extra = len(kinds)
+def on(allowed, action):
+    if allowed is None:
+        action()
+    else:
+        pl.when(allowed)(action)
+
+
+def along(z, nz, step):
+    if step == 0:
+        yield None, z
+    else:
+        yield z >= step, jnp.maximum(z - step, 0)
+        yield z + step < nz, jnp.minimum(z + step, nz - 1)
+
+
+class Mover:
+    def __init__(self, ins, outs, ways, sems):
+        self.ins, self.outs, self.ways = ins, outs, ways
+        self.send, self.recv, self.own = sems
+        self.pending, self.own_copies = [], []
+
+    def push(self, way, where, allowed=None, own=False):
+        for k, out in enumerate(self.outs):
+            copy = pltpu.make_async_remote_copy(
+                src_ref=self.ins[k] if own else out.at[where],
+                dst_ref=out.at[where],
+                send_sem=self.send.at[k, way, where],
+                recv_sem=self.recv.at[k, where],
+                device_id=self.ways[way],
+                device_id_type=MESH,
+            )
+            on(allowed, copy.start)
+            self.pending.append((allowed, copy))
+
+    def arrive(self, where):
+        for k, out in enumerate(self.outs):
+            pltpu.make_async_remote_copy(
+                src_ref=out.at[where],
+                dst_ref=out.at[where],
+                send_sem=self.send.at[k, 0, where],
+                recv_sem=self.recv.at[k, where],
+                device_id=self.ways[-1],
+                device_id_type=MESH,
+            ).wait_recv()
+
+    def keep(self, mine):
+        for k, out in enumerate(self.outs):
+            copy = pltpu.make_async_copy(self.ins[k], out.at[mine], self.own.at[k])
+            copy.start()
+            self.own_copies.append(copy)
+
+    def settle(self):
+        for allowed, copy in self.pending:
+            on(allowed, copy.wait_send)
+        for copy in self.own_copies:
+            copy.wait()
+
+
+class WholeGather(Mover):
+    def begin(self, nz, z, a, b, c):
+        self.nz, self.z, self.a, self.b, self.c = nz, z, a, b, c
+        mine = slot(z, a, b, c)
+        self.push(0, mine, z < nz - 1, True)
+        self.push(1, mine, z > 0, True)
+        for way in (2, 3, 4):
+            self.push(way, mine, None, True)
+        self.keep(mine)
+
+    def turn(self, turn):
+        nz, z, a, b, c = self.nz, self.z, self.a, self.b, self.c
+        if turn < nz:
+            for index, (allowed, zz) in enumerate(along(z, nz, turn)):
+                where = slot(zz, a, b, c)
+                on(allowed, functools.partial(self.arrive, where))
+                self.push(index, where, allowed & ((z > 0) if index else (z < nz - 1)))
+                for way in (2, 3, 4):
+                    self.push(way, where, allowed)
+        if turn - 1 < nz:
+            for allowed, zz in along(z, nz, turn - 1):
+                where = slot(zz, 1 - a, b, c)
+                on(allowed, functools.partial(self.arrive, where))
+                for way in (3, 4):
+                    self.push(way, where, allowed)
+            for allowed, zz in along(z, nz, turn - 1):
+                where = slot(zz, a, 1 - b, c)
+                on(allowed, functools.partial(self.arrive, where))
+                self.push(4, where, allowed)
+        if turn >= 2:
+            for allowed, zz in along(z, nz, turn - 2):
+                where = slot(zz, 1 - a, 1 - b, c)
+                on(allowed, functools.partial(self.arrive, where))
+                self.push(4, where, allowed)
+
+    def end(self):
+        for zz in range(self.nz):
+            for aa in range(2):
+                for bb in range(2):
+                    self.arrive(slot(zz, aa, bb, 1 - self.c))
+        self.settle()
+
+
+class SlabGather(Mover):
+    def begin(self, nz, z, ep, x, c):
+        self.nz, self.z, self.ep, self.c = nz, z, ep, c
+        self.other = ep + 2 - 4 * x
+        mine = z * 4 + ep
+        self.push(0, mine, z < nz - 1, True)
+        self.push(1, mine, z > 0, True)
+        for way in (2, 3):
+            self.push(way, mine, None, True)
+        self.keep(mine)
+
+    def turn(self, turn):
+        nz, z = self.nz, self.z
+        if turn < nz:
+            for index, (allowed, zz) in enumerate(along(z, nz, turn)):
+                where = zz * 4 + self.ep
+                on(allowed, functools.partial(self.arrive, where))
+                self.push(index, where, allowed & ((z > 0) if index else (z < nz - 1)))
+                for way in (2, 3):
+                    self.push(way, where, allowed)
+        if turn - 1 < nz:
+            for allowed, zz in along(z, nz, turn - 1):
+                where = zz * 4 + self.other
+                on(allowed, functools.partial(self.arrive, where))
+                self.push(3, where, allowed)
+
+    def end(self):
+        for where in range(4 * self.nz):
+            pl.when(where % 2 != self.c)(functools.partial(self.arrive, where))
+        self.settle()
+
+
+def gather_kernel(nz, counts, kinds, *refs):
+    whole, slabs = counts
+    count, extra = whole + slabs, len(kinds)
     ins = refs[:count]
     outs = refs[count + extra : 2 * count + extra]
-    send_sem, recv_sem, own_sem = refs[2 * (count + extra) : 2 * (count + extra) + 3]
+    sems = refs[2 * (count + extra) :]
     dp, ep, z, y, x, c, a, b = place()
     ways = targets(dp, ep, z, y, x, c, nz)
-    twin = ways[4]
+    up, down, near, far, twin = ways
+    side = (dp, ep + 2 - 4 * x)
+    movers = []
+    if whole:
+        movers.append(WholeGather(ins[:whole], outs[:whole], ways, sems[:3]))
+        sems = sems[3:]
+    if slabs:
+        movers.append(SlabGather(ins[whole:], outs[whole:], (up, down, side, twin), sems[:3]))
+        sems = sems[3:]
     riders = Riders(
         kinds, nz, (dp, ep, z, y),
-        refs[count : count + extra]
-        + refs[2 * count + extra : 2 * (count + extra)]
-        + refs[2 * (count + extra) + 3 :],
+        refs[count : count + extra] + refs[2 * count + extra : 2 * (count + extra)] + sems,
     )
     greet(nz, z, dp, ep, ways, wide_greeting(kinds))
-    mine = slot(z, a, b, c)
-    pending = []
-
-    def push(way, where, allowed=None, own=False):
-        for k in range(count):
-            copy = pltpu.make_async_remote_copy(
-                src_ref=ins[k] if own else outs[k].at[where],
-                dst_ref=outs[k].at[where],
-                send_sem=send_sem.at[k, way, where],
-                recv_sem=recv_sem.at[k, where],
-                device_id=ways[way],
-                device_id_type=MESH,
-            )
-            if allowed is None:
-                copy.start()
-            else:
-                pl.when(allowed)(copy.start)
-            pending.append((allowed, copy))
-
-    def arrive(where):
-        for k in range(count):
-            pltpu.make_async_remote_copy(
-                src_ref=outs[k].at[where],
-                dst_ref=outs[k].at[where],
-                send_sem=send_sem.at[k, 0, where],
-                recv_sem=recv_sem.at[k, where],
-                device_id=twin,
-                device_id_type=MESH,
-            ).wait_recv()
-
-    own_copies = [pltpu.make_async_copy(ins[k], outs[k].at[mine], own_sem.at[k]) for k in range(count)]
-    push(0, mine, z < nz - 1, True)
-    push(1, mine, z > 0, True)
-    push(2, mine, None, True)
-    push(3, mine, None, True)
-    push(4, mine, None, True)
-    for copy in own_copies:
-        copy.start()
+    for mover in movers:
+        if isinstance(mover, WholeGather):
+            mover.begin(nz, z, a, b, c)
+        else:
+            mover.begin(nz, z, ep, x, c)
     riders.begin()
-
-    def along(step):
-        if step == 0:
-            yield None, z
-        else:
-            yield z >= step, jnp.maximum(z - step, 0)
-            yield z + step < nz, jnp.minimum(z + step, nz - 1)
-
-    def on(allowed, action):
-        if allowed is None:
-            action()
-        else:
-            pl.when(allowed)(action)
-
+    riders.some(0, 1)
     for turn in range(1, nz + 2):
-        if turn <= nz:
-            riders.some(turn - 1, nz)
-        if turn < nz:
-            for index, (allowed, zz) in enumerate(along(turn)):
-                where = slot(zz, a, b, c)
-                on(allowed, functools.partial(arrive, where))
-                if index == 0:
-                    push(0, where, allowed & (z < nz - 1))
-                else:
-                    push(1, where, allowed & (z > 0))
-                for way in (2, 3, 4):
-                    push(way, where, allowed)
-        if turn - 1 < nz:
-            for allowed, zz in along(turn - 1):
-                where = slot(zz, 1 - a, b, c)
-                on(allowed, functools.partial(arrive, where))
-                for way in (3, 4):
-                    push(way, where, allowed)
-            for allowed, zz in along(turn - 1):
-                where = slot(zz, a, 1 - b, c)
-                on(allowed, functools.partial(arrive, where))
-                push(4, where, allowed)
-        if turn >= 2:
-            for allowed, zz in along(turn - 2):
-                where = slot(zz, 1 - a, 1 - b, c)
-                on(allowed, functools.partial(arrive, where))
-                push(4, where, allowed)
-    for zz in range(nz):
-        for aa in range(2):
-            for bb in range(2):
-                arrive(slot(zz, aa, bb, 1 - c))
-    for allowed, copy in pending:
-        on(allowed, copy.wait_send)
-    for copy in own_copies:
-        copy.wait()
+        for mover in movers:
+            mover.turn(turn)
+        if 2 <= turn <= nz:
+            riders.onwards(turn - 1)
+    for mover in movers:
+        mover.end()
     riders.finish()
 
 
-def gather_rows(arrays, devices, ident, riders=()):
-    count = len(arrays)
+def gather_rows(whole, slabs, devices, ident, riders=()):
+    arrays = whole + slabs
     nz = devices // 8
     kinds, ridden, rider_outs, rider_sems = rider_shapes(riders, devices)
+    blocks = (devices,) * len(whole) + (4 * nz,) * len(slabs)
+    dma = pltpu.SemaphoreType.DMA
+    sems = []
+    for count, ways, total in ((len(whole), 5, devices), (len(slabs), 4, 4 * nz)):
+        if count:
+            sems += [dma((count, ways, total)), dma((count, total)), dma((count,))]
     return pl.pallas_call(
-        functools.partial(gather_kernel, nz, count, kinds),
-        out_shape=tuple(jax.ShapeDtypeStruct((devices,) + v.shape, v.dtype) for v in arrays)
+        functools.partial(gather_kernel, nz, (len(whole), len(slabs)), kinds),
+        out_shape=tuple(
+            jax.ShapeDtypeStruct((total,) + v.shape, v.dtype) for total, v in zip(blocks, arrays)
+        )
         + rider_outs,
-        in_specs=[pl.BlockSpec(memory_space=pltpu.VMEM)] * count + rider_specs(kinds),
+        in_specs=[pl.BlockSpec(memory_space=pltpu.VMEM)] * len(arrays) + rider_specs(kinds),
         out_specs=tuple(pl.BlockSpec(memory_space=pl.ANY) for v in arrays + ridden),
-        scratch_shapes=[
-            pltpu.SemaphoreType.DMA((count, 5, devices)),
-            pltpu.SemaphoreType.DMA((count, devices)),
-            pltpu.SemaphoreType.DMA((count,)),
-        ]
-        + rider_sems,
+        scratch_shapes=sems + rider_sems,
         compiler_params=pltpu.CompilerParams(collective_id=ident, has_side_effects=True),
         name="gather_rows_%d" % ident,
     )(*arrays, *ridden)
@@ -855,141 +923,20 @@
     return result if riders else result[0]
 
 
-def slab_gather_kernel(nz, count, kinds, *refs):
-    extra = len(kinds)
-    ins = refs[:count]
-    outs = refs[count + extra : 2 * count + extra]
-    send_sem, recv_sem, own_sem = refs[2 * (count + extra) : 2 * (count + extra) + 3]
-    dp, ep, z, y, x, c, _, _ = place()
-    ways = targets(dp, ep, z, y, x, c, nz)
-    side = (dp, ep + 2 - 4 * x)
-    ways = (ways[0], ways[1], side, ways[4])
-    riders = Riders(
-        kinds, nz, (dp, ep, z, y),
-        refs[count : count + extra]
-        + refs[2 * count + extra : 2 * (count + extra)]
-        + refs[2 * (count + extra) + 3 :],
-    )
-    greet(nz, z, dp, ep, (None, None, riders.over_y, side, ways[3]), False)
-    mine = z * 4 + ep
-    pending = []
-
-    def push(way, where, allowed=None, own=False):
-        for k in range(count):
-            copy = pltpu.make_async_remote_copy(
-                src_ref=ins[k] if own else outs[k].at[where],
-                dst_ref=outs[k].at[where],
-                send_sem=send_sem.at[k, way, where],
-                recv_sem=recv_sem.at[k, where],
-                device_id=ways[way],
-                device_id_type=MESH,
-            )
-            on(allowed, copy.start)
-            pending.append((allowed, copy))
-
-    def arrive(where):
-        for k in range(count):
-            pltpu.make_async_remote_copy(
-                src_ref=outs[k].at[where],
-                dst_ref=outs[k].at[where],
-                send_sem=send_sem.at[k, 0, where],
-                recv_sem=recv_sem.at[k, where],
-                device_id=side,
-                device_id_type=MESH,
-            ).wait_recv()
-
-    def on(allowed, action):
-        if allowed is None:
-            action()
-        else:
-            pl.when(allowed)(action)
-
-    own_copies = [pltpu.make_async_copy(ins[k], outs[k].at[mine], own_sem.at[k]) for k in range(count)]
-    push(0, mine, z < nz - 1, True)
-    push(1, mine, z > 0, True)
-    push(2, mine, None, True)
-    push(3, mine, None, True)
-    for copy in own_copies:
-        copy.start()
-    riders.begin()
-    riders.some(0, 1)
-
-    def along(step):
-        if step == 0:
-            yield None, z
-        else:
-            yield z >= step, jnp.maximum(z - step, 0)
-            yield z + step < nz, jnp.minimum(z + step, nz - 1)
-
-    for turn in range(1, nz + 1):
-        if turn < nz:
-            for index, (allowed, zz) in enumerate(along(turn)):
-                where = zz * 4 + ep
-                on(allowed, functools.partial(arrive, where))
-                if index == 0:
-                    push(0, where, allowed & (z < nz - 1))
-                else:
-                    push(1, where, allowed & (z > 0))
-                push(2, where, allowed)
-                push(3, where, allowed)
-        for allowed, zz in along(turn - 1):
-            where = zz * 4 + ep + 2 - 4 * x
-            on(allowed, functools.partial(arrive, where))
-            push(3, where, allowed)
-        if turn >= 2:
-            riders.onwards(turn - 1)
-    for where in range(4 * nz):
-        pl.when(where % 2 != c)(functools.partial(arrive, where))
-    for allowed, copy in pending:
-        on(allowed, copy.wait_send)
-    for copy in own_copies:
-        copy.wait()
-    riders.finish()
-
-
-def slab_gather(arrays, devices, ident, riders=()):
-    count = len(arrays)
-    nz = devices // 8
-    kinds, ridden, rider_outs, rider_sems = rider_shapes(riders, devices)
-    return pl.pallas_call(
-        functools.partial(slab_gather_kernel, nz, count, kinds),
-        out_shape=tuple(jax.ShapeDtypeStruct((4 * nz,) + v.shape, v.dtype) for v in arrays)
-        + rider_outs,
-        in_specs=[pl.BlockSpec(memory_space=pltpu.VMEM)] * count + rider_specs(kinds),
-        out_specs=tuple(pl.BlockSpec(memory_space=pl.ANY) for v in arrays + ridden),
-        scratch_shapes=[
-            pltpu.SemaphoreType.DMA((count, 4, 4 * nz)),
-            pltpu.SemaphoreType.DMA((count, 4 * nz)),
-            pltpu.SemaphoreType.DMA((count,)),
-        ]
-        + rider_sems,
-        compiler_params=pltpu.CompilerParams(collective_id=ident, has_side_effects=True),
-        name="slab_gather_%d" % ident,
-    )(*arrays, *ridden)
-
-
-def slab_scatter_kernel(nz, pairs, turned, beside, kinds, *refs):
-    extra = len(kinds)
-    lefts, rights = refs[:pairs], refs[pairs : 2 * pairs]
-    beside_ref = refs[2 * pairs] if beside else None
-    refs = refs[2 * pairs + beside :]
-    out_ref = refs[extra]
-    sent, got, from_side, rising, falling = refs[2 * extra + 1 : 2 * extra + 6]
-    (twin_send, twin_recv, side_send, side_recv, line_send, up_recv,
-     down_recv) = refs[2 * extra + 6 : 2 * extra + 13]
-    dp, ep, z, y, x, c, _, _ = place()
-    up, down, _, _, twin = targets(dp, ep, z, y, x, c, nz)
-    side = (dp, ep + 2 - 4 * x)
-    riders = Riders(
-        kinds, nz, (dp, ep, z, y),
-        refs[:extra] + refs[extra + 1 : 2 * extra + 1] + refs[2 * extra + 13 :],
-    )
-    greet(nz, z, dp, ep, (None, None, riders.over_y, side, twin), False)
-    riders.begin()
-    plain = rights[0].shape[0 if turned else 1]
-    span = 512 if plain % 512 == 0 else plain
-
-    def zed(step):
+class SlabSum:
+    def __init__(self, nz, turned, spot, ways, refs, buffers):
+        self.nz, self.turned = nz, turned
+        self.z, self.x, self.c = spot
+        self.up, self.down, self.side, self.twin = ways
+        self.lefts, self.rights, self.beside, self.out = refs
+        (self.sent, self.got, self.from_side, self.rising, self.falling, self.held,
+         self.twin_send, self.twin_recv, self.side_send, self.side_recv, self.line_send,
+         self.up_recv, self.down_recv) = buffers
+        self.plain = self.rights[0].shape[0 if turned else 1]
+        self.span = 512 if self.plain % 512 == 0 else self.plain
+
+    def zed(self, step):
+        z, nz = self.z, self.nz
         if nz == 4:
             far_one = jnp.where(z < 2, 3, 0)
             second = jnp.where(z < 2, 2 - 2 * z, 7 - 2 * z)
@@ -997,156 +944,211 @@
             return jnp.where(step == 0, far_one, jnp.where(step == 1, second, jnp.where(step == 2, third, z)))
         return (z + 1 + step) % nz
 
-    def order(index, cc):
-        flip = 1 - index // nz
-        return zed(index % nz) * 4 + (x + flip * (1 - 2 * x)) * 2 + cc
-
-    def combine(target, where, added):
+    def order(self, index, cc):
+        flip = 1 - index // self.nz
+        return self.zed(index % self.nz) * 4 + (self.x + flip * (1 - 2 * self.x)) * 2 + cc
+
+    def combine(self, targets_, wheres, added):
+        rows = self.lefts[0].shape[1]
+
+        def put(which, at, total):
+            for ref in added[which]:
+                total = total + ref[:, at].astype(jnp.float32)
+            targets_[which][:, at] = total.astype(targets_[which].dtype)
+
         def fill(chunk, carry):
-            at = pl.ds(pl.multiple_of(chunk * span, span), span)
+            at = pl.ds(pl.multiple_of(chunk * self.span, self.span), self.span)
             total = None
-            for left_ref, right_ref in zip(lefts, rights):
+            for left_ref, right_ref in zip(self.lefts, self.rights):
                 value = lax.dot_general(
-                    left_ref[where],
-                    right_ref[at, :] if turned else right_ref[:, at],
-                    (((1,), (1 if turned else 0,)), ((), ())),
+                    jnp.concatenate([left_ref[where] for where in wheres], axis=0),
+                    right_ref[at, :] if self.turned else right_ref[:, at],
+                    (((1,), (1 if self.turned else 0,)), ((), ())),
                     preferred_element_type=jnp.float32,
                 )
                 total = value if total is None else total + value
-            for ref in added:
-                total = total + ref[:, at].astype(jnp.float32)
-            target[:, at] = total.astype(target.dtype)
+            for which in range(len(wheres)):
+                put(which, at, total[which * rows : (which + 1) * rows])
             return carry
 
-        lax.fori_loop(0, plain // span, fill, 0)
-        if beside:
-            at = pl.ds(plain, beside_ref.shape[2])
-            total = beside_ref[where].astype(jnp.float32)
-            for ref in added:
-                total = total + ref[:, at].astype(jnp.float32)
-            target[:, at] = total.astype(target.dtype)
-
-    def twin_copy(index):
+        lax.fori_loop(0, self.plain // self.span, fill, 0)
+        if self.beside is not None:
+            at = pl.ds(self.plain, self.beside.shape[2])
+            for which, where in enumerate(wheres):
+                put(which, at, self.beside[where].astype(jnp.float32))
+
+    def remote(self, source, target, send, recv, device):
         return pltpu.make_async_remote_copy(
-            src_ref=sent.at[index], dst_ref=got.at[index], send_sem=twin_send.at[index],
-            recv_sem=twin_recv.at[index], device_id=twin, device_id_type=MESH)
-
-    def side_copy(index):
-        return pltpu.make_async_remote_copy(
-            src_ref=got.at[index], dst_ref=from_side.at[index], send_sem=side_send.at[index],
-            recv_sem=side_recv.at[index], device_id=side, device_id_type=MESH)
-
-    def up_copy(index, zz):
-        return pltpu.make_async_remote_copy(
-            src_ref=got.at[nz + index], dst_ref=rising.at[zz], send_sem=line_send.at[index],
-            recv_sem=up_recv.at[zz], device_id=up, device_id_type=MESH)
-
-    def down_copy(index, zz):
-        return pltpu.make_async_remote_copy(
-            src_ref=got.at[nz + index], dst_ref=falling.at[zz], send_sem=line_send.at[index],
-            recv_sem=down_recv.at[zz], device_id=down, device_id_type=MESH)
-
-    def give(index, carry):
-        combine(sent.at[index], order(index, 1 - c), ())
-        twin_copy(index).start()
+            src_ref=source, dst_ref=target, send_sem=send, recv_sem=recv,
+            device_id=device, device_id_type=MESH)
+
+    def twin_copy(self, index):
+        return self.remote(
+            self.sent.at[index], self.got.at[index], self.twin_send.at[index],
+            self.twin_recv.at[index], self.twin)
+
+    def side_copy(self, index):
+        return self.remote(
+            self.got.at[index], self.from_side.at[index], self.side_send.at[index],
+            self.side_recv.at[index], self.side)
+
+    def line_copy(self, index, zz, rise):
+        place_, recv = (self.rising, self.up_recv) if rise else (self.falling, self.down_recv)
+        return self.remote(
+            self.got.at[self.nz + index], place_.at[zz], self.line_send.at[index], recv.at[zz],
+            self.up if rise else self.down)
+
+    def give(self, pair, carry):
+        both = (2 * pair, 2 * pair + 1)
+        self.combine(
+            [self.sent.at[index] for index in both],
+            [self.order(index, 1 - self.c) for index in both], [(), ()])
+        for index in both:
+            self.twin_copy(index).start()
         return carry
 
-    def side_step(step, carry):
-        lax.fori_loop(2 * step, 2 * step + 2, give, 0)
-        twin_copy(step).wait_recv()
-        combine(got.at[step], order(step, c), (got.at[step],))
-        side_copy(step).start()
-        riders.looped(step, nz)
-        return carry
-
-    lax.fori_loop(0, nz, side_step, 0)
-
-    def line_step(step, carry):
-        zz = zed(step)
-        twin_copy(nz + step).wait_recv()
-        side_copy(step).wait_recv()
-        combine(out_ref, order(nz + step, c), (got.at[nz + step], from_side.at[step]))
+    def to_side(self, pair):
+        lax.fori_loop(2 * pair, 2 * pair + 2, self.give, 0)
+        both = (2 * pair, 2 * pair + 1)
+        for index in both:
+            self.twin_copy(index).wait_recv()
+        self.combine(
+            [self.got.at[index] for index in both],
+            [self.order(index, self.c) for index in both],
+            [(self.got.at[index],) for index in both])
+        for index in both:
+            self.side_copy(index).start()
+
+    def to_line(self, pair):
+        both = (2 * pair, 2 * pair + 1)
+        for step in both:
+            self.twin_copy(self.nz + step).wait_recv()
+            self.side_copy(step).wait_recv()
+        self.combine(
+            [self.held.at[0], self.held.at[1]],
+            [self.order(self.nz + step, self.c) for step in both],
+            [(self.got.at[self.nz + step], self.from_side.at[step]) for step in both])
+        for which, step in enumerate(both):
+            self.along_line(self.held.at[which], step)
+
+    def along_line(self, held, step):
+        z, zz = self.z, self.zed(step)
 
         @pl.when((zz >= z) & (z > 0))
         def _():
-            up_copy(step, zz).wait_recv()
-            out_ref[...] += rising[zz].astype(jnp.float32)
-
-        @pl.when((zz <= z) & (z < nz - 1))
+            self.line_copy(step, zz, True).wait_recv()
+            held[...] += self.rising[zz].astype(jnp.float32)
+
+        @pl.when((zz <= z) & (z < self.nz - 1))
         def _():
-            down_copy(step, zz).wait_recv()
-            out_ref[...] += falling[zz].astype(jnp.float32)
-
-        @pl.when(zz > z)
+            self.line_copy(step, zz, False).wait_recv()
+            held[...] += self.falling[zz].astype(jnp.float32)
+
+        @pl.when(zz != z)
         def _():
-            got[nz + step] = out_ref[...].astype(got.dtype)
-            up_copy(step, zz).start()
-
-        @pl.when(zz < z)
-        def _():
-            got[nz + step] = out_ref[...].astype(got.dtype)
-            down_copy(step, zz).start()
-
+            self.got[self.nz + step] = held[...].astype(self.got.dtype)
+
+        pl.when(zz > z)(lambda: self.line_copy(step, zz, True).start())
+        pl.when(zz < z)(lambda: self.line_copy(step, zz, False).start())
+
+    def end(self):
+        self.out[...] = self.held[1]
+
+        def finish(step, carry):
+            self.twin_copy(step).wait_send()
+            return carry
+
+        lax.fori_loop(0, 2 * self.nz, finish, 0)
+
+        def finish_side(step, carry):
+            self.side_copy(step).wait_send()
+
+            @pl.when(step < self.nz - 1)
+            def _():
+                self.line_copy(step, 0, True).wait_send()
+
+            return carry
+
+        lax.fori_loop(0, self.nz, finish_side, 0)
+
+
+def slab_scatter_kernel(nz, forms, kinds, *refs):
+    extra, parts = len(kinds), len(forms)
+    refs = list(refs)
+
+    def take(count):
+        taken = tuple(refs[:count])
+        del refs[:count]
+        return taken
+
+    operands = []
+    for pairs, turned, beside in forms:
+        operands.append((take(pairs), take(pairs), take(1)[0] if beside else None))
+    rider_ins = take(extra)
+    outs = take(parts)
+    rider_outs = take(extra)
+    dp, ep, z, y, x, c, _, _ = place()
+    up, down, near, far, twin = targets(dp, ep, z, y, x, c, nz)
+    side = (dp, ep + 2 - 4 * x)
+    sums = [
+        SlabSum(nz, form[1], (z, x, c), (up, down, side, twin), held + (out,), take(13))
+        for form, held, out in zip(forms, operands, outs)
+    ]
+    riders = Riders(kinds, nz, (dp, ep, z, y), rider_ins + rider_outs + tuple(refs))
+    greet(nz, z, dp, ep, (up, down, near, far, twin), wide_greeting(kinds))
+    riders.begin()
+
+    def side_step(pair, carry):
+        for part in sums:
+            part.to_side(pair)
+        riders.looped(pair, nz // 2)
         return carry
 
-    lax.fori_loop(0, nz, line_step, 0)
-
-    def finish(step, carry):
-        twin_copy(step).wait_send()
+    lax.fori_loop(0, nz // 2, side_step, 0)
+
+    def line_step(pair, carry):
+        for part in sums:
+            part.to_line(pair)
         return carry
 
-    lax.fori_loop(0, 2 * nz, finish, 0)
-
-    def finish_side(step, carry):
-        side_copy(step).wait_send()
-
-        @pl.when(step < nz - 1)
-        def _():
-            up_copy(step, 0).wait_send()
-
-        return carry
-
-    lax.fori_loop(0, nz, finish_side, 0)
+    lax.fori_loop(0, nz // 2, line_step, 0)
+    for part in sums:
+        part.end()
     riders.finish()
 
 
-def slab_scatter(lefts, rights, devices, ident, turned=False, beside=None, riders=()):
+def slab_scatter(parts, devices, ident, riders=()):
     nz = devices // 8
     blocks = 4 * nz
-    rows = lefts[0].shape[0] // blocks
-    wide = rights[0].shape[0 if turned else 1]
-    held = () if beside is None else (beside.reshape(blocks, rows, -1),)
-    wide = wide + sum(v.shape[2] for v in held)
+    rows = parts[0][0][0].shape[0] // blocks
     kinds, ridden, rider_outs, rider_sems = rider_shapes(riders, devices)
-    block = (rows, wide)
-    low = jnp.bfloat16
-    dma = pltpu.SemaphoreType.DMA
-    pairs = len(lefts)
-    result = pl.pallas_call(
-        functools.partial(slab_scatter_kernel, nz, pairs, turned, len(held), kinds),
-        out_shape=(jax.ShapeDtypeStruct(block, jnp.float32),) + rider_outs,
-        in_specs=[pl.BlockSpec(memory_space=pltpu.VMEM)] * (2 * pairs + len(held))
-        + rider_specs(kinds),
-        out_specs=(pl.BlockSpec(memory_space=pltpu.VMEM),)
+    low, dma = jnp.bfloat16, pltpu.SemaphoreType.DMA
+    operands, outs, scratch, forms = (), (), [], []
+    for lefts, rights, turned, beside in parts:
+        held = () if beside is None else (beside.reshape(blocks, rows, -1),)
+        wide = rights[0].shape[0 if turned else 1] + sum(v.shape[2] for v in held)
+        block = (rows, wide)
+        operands += tuple(v.reshape(blocks, rows, -1) for v in lefts) + tuple(rights) + held
+        outs += (jax.ShapeDtypeStruct(block, jnp.float32),)
+        scratch += [pltpu.VMEM((count * nz,) + block, low) for count in (2, 2, 1, 1, 1)]
+        scratch += [pltpu.VMEM((2,) + block, jnp.float32)]
+        scratch += [dma((2 * nz,))] * 2 + [dma((nz,))] * 5
+        forms.append((len(lefts), turned, len(held)))
+    return pl.pallas_call(
+        functools.partial(slab_scatter_kernel, nz, tuple(forms), kinds),
+        out_shape=outs + rider_outs,
+        in_specs=[pl.BlockSpec(memory_space=pltpu.VMEM)] * len(operands) + rider_specs(kinds),
+        out_specs=(pl.BlockSpec(memory_space=pltpu.VMEM),) * len(outs)
         + (pl.BlockSpec(memory_space=pl.ANY),) * len(riders),
-        scratch_shapes=[
-            pltpu.VMEM((2 * nz,) + block, low),
-            pltpu.VMEM((2 * nz,) + block, low),
-            pltpu.VMEM((nz,) + block, low),
-            pltpu.VMEM((nz,) + block, low),
-            pltpu.VMEM((nz,) + block, low),
-            dma((2 * nz,)), dma((2 * nz,)), dma((nz,)), dma((nz,)), dma((nz,)), dma((nz,)), dma((nz,)),
-        ]
-        + rider_sems,
+        scratch_shapes=scratch + rider_sems,
         compiler_params=pltpu.CompilerParams(
-            collective_id=ident, has_side_effects=True, vmem_limit_bytes=58 * 2**20),
+            collective_id=ident, has_side_effects=True, vmem_limit_bytes=63 * 2**20),
         name="slab_scatter_%d" % ident,
-    )(*(v.reshape(blocks, rows, -1) for v in lefts), *rights, *held, *ridden)
-    return result if riders else result[0]
+    )(*operands, *ridden)
 
 
 def whole_rows(mesh):
-    return mesh.shape["ep"] == 4 and mesh.shape["dp"] % 2 == 0 and mesh.shape["dp"] <= 8
+    return mesh.shape["ep"] == 4 and mesh.shape["dp"] in (4, 8)
 
 
 def exact_dot(left_side, right_side):
@@ -1231,13 +1233,14 @@
     router_rows = w_router.astype(f32).reshape(-1, 128)
     note_one = jnp.concatenate([lens_row, gain_row, router_rows], axis=0)
     note_one = jnp.pad(note_one, ((0, -note_one.shape[0] % 8), (0, 0)))
-    unit_all, notes, w_heads = gather_rows(
-        (unit_one.astype(low), note_one), devices, 1, (("all", sent_heads),)
+    unit_all, notes, grad_all, w_heads, w_rise_up = gather_rows(
+        (unit_one.astype(low), note_one),
+        (grad_mid_out.astype(low),),
+        devices,
+        1,
+        (("all", sent_heads), ("cube", w_up)),
     )
     w_heads = w_heads.reshape(width, 3 * head_dim)
-    grad_all, w_rise_up = slab_gather(
-        (grad_mid_out.astype(low),), devices, 9, (("cube", w_up),)
-    )
     w_rise_up = w_rise_up.reshape(width, hidden)
     lens_all = notes[:, 0, : seq_lengths.shape[1]].astype(jnp.int32)
     gain_two = notes[:, 1, :rows_own].reshape(1, width)
@@ -1286,8 +1289,8 @@
     gate_power = jnp.where(choose, jnp.exp(picked - jnp.max(picked, axis=1, keepdims=True)), 0.0)
     route = gate_power / jnp.sum(gate_power, axis=1, keepdims=True)
     note_two = jnp.pad(route.T, ((0, 0), (0, 128 - row_count)))
-    normed_all, notes, w_rise_gate, fall_other = slab_gather(
-        (normed_mid, note_two), devices, 3, (("cube", w_gate), ("across", fall_own))
+    normed_all, notes, w_rise_gate, fall_other = gather_rows(
+        (), (normed_mid, note_two), devices, 3, (("cube", w_gate), ("across", fall_own))
     )
     w_rise_gate = w_rise_gate.reshape(width, hidden)
     w_fall = jnp.where(
@@ -1322,14 +1325,14 @@
     gate_halves = for_each_y(contract(flat_mid, grad_gate_part, "td,tf->df"))
     up_halves = for_each_y(contract(flat_mid, grad_up_part, "td,tf->df"))
     fall_halves = for_each_y(contract(flat_grad, weighted_mid, "td,tf->df"))
-    summed, gate_come, up_come = slab_scatter(
-        (grad_gate_part, grad_up_part),
-        (w_rise_gate, w_rise_up),
+    summed, moe_rows, gate_come, up_come, fall_come = slab_scatter(
+        (
+            ((grad_gate_part, grad_up_part), (w_rise_gate, w_rise_up), True, beside),
+            ((weighted_mid,), (w_fall,), False, None),
+        ),
         devices,
         4,
-        turned=True,
-        beside=beside,
-        riders=(("half", gate_halves), ("half", up_halves)),
+        (("half", gate_halves), ("half", up_halves), ("half", fall_halves)),
     )
 
     def add_halves(halves, come):
@@ -1351,8 +1354,15 @@
         ],
         axis=0,
     )
-    branch_all, notes, back_up = gather_rows(
-        (grad_branch, note_three), devices, 6, (("line", add_halves(up_halves, up_come)),)
+    branch_all, notes, back_gate, back_up = gather_rows(
+        (grad_branch, note_three),
+        (),
+        devices,
+        6,
+        (
+            ("line", add_halves(gate_halves, gate_come)),
+            ("line", add_halves(up_halves, up_come)),
+        ),
     )
     clip_factor = jnp.sqrt(clip_threshold / jnp.maximum(notes[:, -1, 0], clip_threshold))
     gain_sum = jnp.sum(notes[:, :-8], axis=0).reshape(-1)
@@ -1384,13 +1394,6 @@
         all_count, 3 * head_dim
     )
     grad_heads_w = contract(flat_unit, grad_heads, "td,tq->dq").astype(low)
-    moe_rows, back_gate, fall_come = slab_scatter(
-        (weighted_mid,),
-        (w_fall,),
-        devices,
-        5,
-        riders=(("line", add_halves(gate_halves, gate_come)), ("half", fall_halves)),
-    )
     resid_out = resid_mid + moe_rows
     undeal = (jnp.arange(tok_count, dtype=jnp.int32)[:, None] == local_order[None, :]).astype(low)
     undeal = undeal[:, :row_count]

time: 961 us -> 945 us (0.983)
  Pallas kernels: 731 us -> 715 us
    pallas_call x2, Pallas kernels: 204 us -> 195 us  [scatter_sum(): pl.pallas_call(functools.partial(scatter_kernel, nz, turned, kinds), out_...]
    pallas_call x6 -> x4, Pallas kernels: 527 us -> 521 us  [the longest x3 389 us: gather_rows(): pl.pallas_call(functools.partial(gather_kernel, nz, (len(whole), len(slab...]
where the time goes in v4:
time: 945 us; the launch traced here: 934 us
  Pallas kernels  715 us (76%)
  matrix products  127 us (13%)
  other arithmetic  53.9 us (6%)
  local copies, waits for them, and re-layouts  35.9 us (4%)
    pallas_call x3, Pallas kernels, gather_rows(): pl.pallas_call(functools.partial(gather_kernel, nz, (len(whole), len(slab...  389 us
    pallas_call x2, Pallas kernels, scatter_sum(): pl.pallas_call(functools.partial(scatter_kernel, nz, turned, kinds), out_...  195 us
    pallas_call x1, Pallas kernels, slab_scatter(): pl.pallas_call(functools.partial(slab_scatter_kernel, nz, tuple(forms), k...  131 us
    dot_general x15, matrix products, contract(): jnp.einsum(pattern, left_side, right_side, preferred_element_type=jnp.flo...  88.4 us

profile of v4, /device:TPU:1, one launch (start us, length us, event | category | flops | bytes accessed | tf_op | source)
XLA Modules:
  0.0 934.1 jit_solution(2563476625259445980)
XLA Ops:
  13.0 163.7 %gather_rows_1.1 = (bf16[32,112,2048]{2,1,0:T(8,128)(2,1)}, f32[32,16,128]{2,1,0:T(8,128)}, bf16[16,112,2048]{2,1,0:T(8,128)(2,1)}, bf16[32,64,384]{2,1,0:T(8,128)(2,1)}, bf16[4,2,256,768]{3,2,1,0:T(8,128)(2,1)}) custom-call(bf16[112,2048]{1,0:T(8,128)(2,1)} %multiply_convert_fusion.7.refs_0_, f32[16,128]{1,0:T(8,128)} %pad.27.refs_1_, ...), custom_call_target="tpu_custom_call" | custom-call | tf_op jit(solution)/shard_map/gather_rows_1/pallas_call | solution.py:731
  183.3 11.9 %fusion.66 = f32[32,112,384]{2,1,0:T(8,128)S(1)} fusion(bf16[32,112,2048]{2,1,0:T(8,128)(2,1)} %get-tuple-element.41, bf16[2048,384,1]{1,0,2:T(8,128)(2,1)S(1)} %bitcast.177), kind=kOutput, calls=%fused_computation.190 | convolution fusion | flops 5637144576 | bytes 21757952 | tf_op jit(solution)/shard_map/dot_general | solution.py:1258
  203.4 4.2 convolution_convert_fusion.6.refs_0_
  207.7 81.9 %scatter_sum_2.1 = (f32[112,2048]{1,0:T(8,128)}, bf16[4,768,256]{2,1,0:T(8,128)(2,1)}) custom-call(bf16[32,112,128]{2,1,0:T(8,128)(2,1)} %convolution_convert_fusion.6.refs_0_, bf16[128,2048]{1,0:T(8,128)(2,1)} %refs_1_.1, bf16[4,768,256]{2,1,0:T(8,128)(2,1)} %refs_2_.2), custom_call_target="tpu_custom_call" | custom-call | tf_op jit(solution)/shard_map/scatter_sum_2/pallas_call | solution.py:902
  293.4 91.1 %gather_rows_3.1 = (bf16[16,112,2048]{2,1,0:T(8,128)(2,1)}, f32[16,16,128]{2,1,0:T(8,128)}, bf16[4,2,256,768]{3,2,1,0:T(8,128)(2,1)}, bf16[4,768,256]{2,1,0:T(8,128)(2,1)}) custom-call(bf16[112,2048]{1,0:T(8,128)(2,1)} %copy-done.14, f32[16,128]{1,0:T(8,128)} %pad.28.refs_1_, bf16[4,256,768]{2,1,0:T(8,128)(2,1)} %refs_2_.3, ...), custom_call_target="tpu_custom_call" | custom-call | tf_op jit(solution)/shard_map/gather_rows_3/pallas_call | solution.py:731
  384.6 2.2 fusion.2
  386.8 4.9 copy.137
  391.7 6.5 reshape.431.refs_6_
  399.2 9.2 fusion.69
  408.4 9.7 %fusion.68 = f32[1792,768]{1,0:T(8,128)} fusion(bf16[1792,2048]{1,0:T(8,128)(2,1)} %bitcast.195, bf16[2048,768]{1,0:T(8,128)(2,1)S(1)} %bitcast.168), kind=kOutput, calls=%fused_computation.192 | convolution fusion | flops 5637144576 | bytes 15990784 | tf_op jit(solution)/shard_map/dot_general | solution.py:1307
  418.1 12.4 %multiply_reduce_fusion = (bf16[1792]{0:T(1024)(128)(2,1)S(1)}, bf16[1792,768]{1,0:T(8,128)(2,1)S(1)}, bf16[1792,768]{1,0:T(8,128)(2,1)S(1)}, bf16[1792,768]{1,0:T(8,128)(2,1)}) fusion(f32[1792,768]{1,0:T(8,128)} %fusion.68, f32[1792,768]{1,0:T(8,128)S(1)} %fusion.69, f32[1792]{0:T(1024)S(1)} %mul.378, bf16[1792,2048]{1,0:T(8,128)(2,1)} %bitcast.192, ...), kind=kOutput, calls=%fused_computation.2 | convolution fusion | flops 5663291392 | bytes 29764096 | tf_op jit(solution)/shard_map/td,fd->tf/dot_general | solution.py:42
  430.5 12.9 %convolution_convert_fusion.1 = bf16[2048,768]{1,0:T(8,128)(2,1)} fusion(bf16[1792,2048]{1,0:T(8,128)(2,1)} %bitcast.193, bf16[1792,768]{1,0:T(8,128)(2,1)S(1)} %get-tuple-element.175), kind=kOutput, calls=%fused_computation.8 | convolution fusion | flops 5638717440 | bytes 13238272 | tf_op jit(solution)/shard_map/td,tf->df/dot_general | solution.py:42
  444.5 11.0 %convolution_convert_fusion.3 = bf16[2048,768]{1,0:T(8,128)(2,1)} fusion(bf16[1792,2048]{1,0:T(8,128)(2,1)} %bitcast.196, bf16[1792,768]{1,0:T(8,128)(2,1)S(1)} %get-tuple-element.174), kind=kOutput, calls=%fused_computation.10 | convolution fusion | flops 5638717440 | bytes 13238272 | tf_op jit(solution)/shard_map/td,tf->df/dot_general | solution.py:42
  455.6 10.7 %convolution_convert_fusion.2 = bf16[2048,768]{1,0:T(8,128)(2,1)} fusion(bf16[1792,2048]{1,0:T(8,128)(2,1)} %bitcast.197, bf16[1792,768]{1,0:T(8,128)(2,1)S(1)} %copy-done.32), kind=kOutput, calls=%fused_computation.9 | convolution fusion | flops 5638717440 | bytes 13238272 | tf_op jit(solution)/shard_map/td,tf->df/dot_general | solution.py:42
  466.2 131.3 %slab_scatter_4.1 = (f32[112,2176]{1,0:T(8,128)}, f32[112,2048]{1,0:T(8,128)}, bf16[4,256,768]{2,1,0:T(8,128)(2,1)}, bf16[4,256,768]{2,1,0:T(8,128)(2,1)}, bf16[4,256,768]{2,1,0:T(8,128)(2,1)}) custom-call(bf16[16,112,768]{2,1,0:T(8,128)(2,1)} %bitcast.171, bf16[16,112,768]{2,1,0:T(8,128)(2,1)} %bitcast.173, bf16[2048,768]{1,0:T(8,128)(2,1)} %bitcast.170, ...), custom_call_target="tpu_custom_call" | custom-call | tf_op jit(solution)/shard_map/slab_scatter_4/pallas_call | solution.py:1137
  597.6 3.6 fusion.3.refs_3_
  608.0 2.7 multiply_reduce_fusion.9
  613.0 2.5 fusion.59
  616.8 134.5 %gather_rows_6.1 = (bf16[32,112,2048]{2,1,0:T(8,128)(2,1)}, f32[32,24,128]{2,1,0:T(8,128)}, bf16[4,256,768]{2,1,0:T(8,128)(2,1)}, bf16[4,256,768]{2,1,0:T(8,128)(2,1)}) custom-call(bf16[112,2048]{1,0:T(8,128)(2,1)} %get-tuple-element.169.refs_0_, f32[24,128]{1,0:T(8,128)} %concatenate.32.refs_1_, bf16[4,256,768]{2,1,0:T(8,128)(2,1)} %fusion.5.refs_2_, ...), custom_call_target="tpu_custom_call" | custom-call | tf_op jit(solution)/shard_map/gather_rows_6/pallas_call | solution.py:731
  754.7 8.4 convolution_bitcast_fusion
  764.4 5.1 convolution_convert_fusion
  769.5 3.1 convolution_convert_fusion.5
  772.6 2.4 multiply_reduce_fusion.5
  777.6 1.9 convert_element_type.281
  782.5 1.9 convert_element_type.282
  786.1 3.5 multiply_reduce_fusion.2
  790.2 2.2 multiply_convert_fusion.4
  792.4 12.0 %bitcast_convert_fusion = bf16[2048,384]{1,0:T(8,128)(2,1)} fusion(bf16[32,112,2048]{2,1,0:T(8,128)(2,1)} %get-tuple-element.41, bf16[32,112,128]{2,1,0:T(8,128)(2,1)S(1)} %convolution_convert_fusion.5, bf16[32,112,128]{2,1,0:T(8,128)(2,1)S(1)} %get-tuple-element.178, bf16[32,112,128]{2,1,0:T(8,128)(2,1)S(1)} %get-tuple-element.177), kind=kOutput, calls=%fused_computation.19 | convolution fusion | flops 5646188544 | bytes 19005440 | tf_op jit(solution)/shard_map/td,tq->dq/dot_general | solution.py:42
  804.4 1.9 pad_maximum_fusion.refs_0_
  806.3 112.8 %scatter_sum_7.1 = (f32[112,2048]{1,0:T(8,128)}, bf16[32,64,384]{2,1,0:T(8,128)(2,1)}, bf16[4,256,768]{2,1,0:T(8,128)(2,1)}, f32[32,8,128]{2,1,0:T(8,128)}, f32[32,8,128]{2,1,0:T(8,128)}) custom-call(bf16[32,112,384]{2,1,0:T(8,128)(2,1)} %pad_maximum_fusion.refs_0_, bf16[2048,384]{1,0:T(8,128)(2,1)} %bitcast.176, bf16[32,64,384]{2,1,0:T(8,128)(2,1)} %bitcast.178, ...), custom_call_target="tpu_custom_call" | custom-call | tf_op jit(solution)/shard_map/scatter_sum_7/pallas_call | solution.py:902
  928.2 1.9 convert_bitcast_fusion
  930.1 3.5 copy.147
  (233 shorter events, 64.4 us)
Async XLA Ops:
  0.6 10.9 %copy-start = (bf16[128,2048]{1,0:T(8,128)(2,1)S(1)}, bf16[128,2048]{1,0:T(8,128)(2,1)}, u32[]{:S(2)}) copy-start(bf16[128,2048]{1,0:T(8,128)(2,1)} %param.19) | copy-start | bytes 1572868
  0.7 7.9 copy-start.33
  1.5 8.7 copy-start.54
  2.1 194.3 %copy-start.58 = (f32[128]{0:T(128)}, f32[128]{0:T(128)S(1)}, u32[]{:S(2)}) copy-start(f32[128]{0:T(128)S(1)} %convert_element_type.242) | copy-start | bytes 1540
  2.8 193.7 %copy-start.60 = (f32[128]{0:T(128)}, f32[128]{0:T(128)S(1)}, u32[]{:S(2)}) copy-start(f32[128]{0:T(128)S(1)} %convert_element_type.245) | copy-start | bytes 1540
  10.6 279.0 %copy-start.6 = (f32[112,2048]{1,0:T(8,128)}, f32[112,2048]{1,0:T(8,128)S(1)}, u32[]{:S(2)}) copy-start(f32[112,2048]{1,0:T(8,128)S(1)} %get-tuple-element.207) | copy-start | bytes 2752516
  10.6 166.1 %copy-start.56 = (f32[112]{0:T(128)}, f32[112]{0:T(128)S(1)}, u32[]{:S(2)}) copy-start(f32[112]{0:T(128)S(1)} %add_rsqrt_fusion.3) | copy-start | bytes 1348
  180.6 111.4 %copy-start.19 = (bf16[2048,16]{1,0:T(8,128)(2,1)}, bf16[2048,16]{1,0:T(8,128)(2,1)S(1)}, u32[]{:S(2)}) copy-start(bf16[2048,16]{1,0:T(8,128)(2,1)S(1)} %convert_element_type.250) | copy-start | bytes 196612
  182.0 17.1 %copy-start.10 = (f32[3584,128]{1,0:T(8,128)}, f32[3584,128]{1,0:T(8,128)S(1)}, u32[]{:S(2)}) copy-start(f32[3584,128]{1,0:T(8,128)S(1)} %fusion.10) | copy-start | bytes 5505028
  183.3 15.7 %copy-start.8 = (f32[3584,128]{1,0:T(8,128)}, f32[3584,128]{1,0:T(8,128)S(1)}, u32[]{:S(2)}) copy-start(f32[3584,128]{1,0:T(8,128)S(1)} %fusion.11) | copy-start | bytes 5505028
  292.8 91.8 %copy-start.18 = (bf16[4,768,256]{2,1,0:T(8,128)(2,1)S(1)}, bf16[4,768,256]{2,1,0:T(8,128)(2,1)}, u32[]{:S(2)}) copy-start(bf16[4,768,256]{2,1,0:T(8,128)(2,1)} %get-tuple-element.45.refs_3_) | copy-start | bytes 4718596
  399.2 9.2 copy-start.29
  408.4 9.7 %copy-start.12 = (bf16[768,2048]{1,0:T(8,128)(2,1)S(1)}, bf16[768,2048]{1,0:T(8,128)(2,1)}, u32[]{:S(2)}) copy-start(bf16[768,2048]{1,0:T(8,128)(2,1)} %reshape.431.refs_6_) | copy-start | bytes 9437188
  430.5 12.9 %copy-start.31 = (bf16[1792,768]{1,0:T(8,128)(2,1)}, bf16[1792,768]{1,0:T(8,128)(2,1)S(1)}, u32[]{:S(2)}) copy-start(bf16[1792,768]{1,0:T(8,128)(2,1)S(1)} %get-tuple-element.175) | copy-start | bytes 8257540
  430.5 14.0 %copy-start.30 = (bf16[1792,768]{1,0:T(8,128)(2,1)}, bf16[1792,768]{1,0:T(8,128)(2,1)S(1)}, u32[]{:S(2)}) copy-start(bf16[1792,768]{1,0:T(8,128)(2,1)S(1)} %get-tuple-element.174) | copy-start | bytes 8257540
  444.5 11.0 %copy-start.32 = (bf16[1792,768]{1,0:T(8,128)(2,1)S(1)}, bf16[1792,768]{1,0:T(8,128)(2,1)}, u32[]{:S(2)}) copy-start(bf16[1792,768]{1,0:T(8,128)(2,1)} %get-tuple-element.176) | copy-start | bytes 8257540
  597.6 3.6 copy-start.17
  597.6 3.6 copy-start.37
  601.2 2.9 copy-start.36
  606.9 3.8 copy-start.15
  616.8 137.4 %copy-start.62 = (f32[32]{0:T(128)S(1)}, f32[32]{0:T(128)}, u32[]{:S(2)}) copy-start(f32[32]{0:T(128)} %param.35) | copy-start | bytes 388
  616.8 137.9 %copy-start.21 = (bf16[32,112,128]{2,1,0:T(8,128)(2,1)S(1)}, bf16[32,112,128]{2,1,0:T(8,128)(2,1)}, u32[]{:S(2)}) copy-start(bf16[32,112,128]{2,1,0:T(8,128)(2,1)} %convolution_convert_fusion.6.refs_0_) | copy-start | bytes 2752516
  754.7 9.7 %copy-start.3 = (bf16[32,112,2048]{2,1,0:T(8,128)(2,1)S(1)}, bf16[32,112,2048]{2,1,0:T(8,128)(2,1)}, u32[]{:S(2)}) copy-start(bf16[32,112,2048]{2,1,0:T(8,128)(2,1)} %get-tuple-element.55) | copy-start | bytes 44040196
  754.7 9.8 %copy-start.45 = (bf16[128,2048]{1,0:T(8,128)(2,1)S(1)}, bf16[128,2048]{1,0:T(8,128)(2,1)}, u32[]{:S(2)}) copy-start(bf16[128,2048]{1,0:T(8,128)(2,1)} %refs_1_.1) | copy-start | bytes 1572868
  769.5 3.1 copy-start.13
  777.6 2.9 copy-start.28
  781.1 4.2 slice-start
  782.5 2.8 slice-start.1
  806.3 112.8 %copy-start.7 = (f32[112,2048]{1,0:T(8,128)S(1)}, f32[112,2048]{1,0:T(8,128)}, u32[]{:S(2)}) copy-start(f32[112,2048]{1,0:T(8,128)} %copy-done.6) | copy-start | bytes 2752516
  806.3 112.8 %copy-start.57 = (f32[112]{0:T(128)S(1)}, f32[112]{0:T(128)}, u32[]{:S(2)}) copy-start(f32[112]{0:T(128)} %copy-done.56) | copy-start | bytes 1348
  920.8 3.2 copy-start.42
  928.2 5.5 copy-start.1
  (33 other events, 55.0 us)

commit v5 on v4

--- a/solution.py
+++ b/solution.py
@@ -407,8 +407,6 @@
                 self.spans.append((1, 8 * nz))
             else:
                 self.spans.append((1 if kind in ("line", "cube") else 0, nz))
-        self.steps = [(r, k) for r in range(count) for k in range(*self.spans[r])]
-        self.steps.sort(key=lambda step: step[1] / self.spans[step[0]][1])
         self.cubes = [r for r in range(count) if kinds[r] == "cube"]
 
     def remote(self, source, target, send, recv, device):
@@ -428,7 +426,8 @@
             target = target.at[self.z] if kind == "line" else target.at[self.z, self.y]
         else:
             source = source.at[step, 1 - self.y] if kind == "half" else source.at[step]
-            target, key, device = target.at[step], step, self.over_y
+            target = target.at[step] if kind == "half" else target.at[step, self.y]
+            key, device = step, self.over_y
         return self.remote(source, target, self.send.at[r, step], self.recv.at[r, key], device)
 
     def arrival(self, r, step):
@@ -440,7 +439,8 @@
             key = (self.z + self.nz - step) % self.nz
             target = target.at[key] if kind == "line" else target.at[key, self.y]
         else:
-            key, target = step, target.at[step]
+            key = step
+            target = target.at[step] if kind == "half" else target.at[step, 1 - self.y]
         return self.remote(target, target, self.send.at[r, step], self.recv.at[r, key], self.over_y)
 
     def passing(self, r, step, first=False):
@@ -456,22 +456,34 @@
         return self.remote(
             target, target, self.onward.at[r, step], self.recv.at[r, self.nz + key], self.over_y)
 
-    def own_copy(self, r):
+    def own_copies(self, r):
         kind, source, target = self.kinds[r], self.ins[r], self.outs[r]
         if kind in ("all", "same"):
-            source = source if kind == "same" else source.at[self.me]
-            target = target.at[self.me]
+            ends = [(source if kind == "same" else source.at[self.me], target.at[self.me])]
+        elif kind == "half":
+            ends = []
+        elif kind == "pair":
+            ends = [(source.at[k], target.at[k, self.y]) for k in range(self.nz)]
         else:
-            source = source.at[self.z]
             target = target.at[self.z] if kind == "line" else target.at[self.z, self.y]
-        return pltpu.make_async_copy(source, target, self.own.at[r])
-
-    def begin(self):
+            ends = [(source.at[self.z], target)]
+        return [pltpu.make_async_copy(here, there, self.own.at[r]) for here, there in ends]
+
+    def begin(self, early=("half", "pair")):
         for r, kind in enumerate(self.kinds):
-            if kind not in ("half", "across"):
-                self.own_copy(r).start()
+            for copy in self.own_copies(r):
+                copy.start()
             if kind == "cube":
                 self.passing(r, 0, True).start()
+        self.steps = []
+        for r, kind in enumerate(self.kinds):
+            for k in range(*self.spans[r]):
+                if kind in early:
+                    self.copy(r, k).start()
+                else:
+                    self.steps.append((r, k))
+        self.steps.sort(key=lambda step: step[1] / self.spans[step[0]][1])
+        self.later = [r for r, kind in enumerate(self.kinds) if kind not in early]
 
     def some(self, share, shares):
         total = len(self.steps)
@@ -484,7 +496,7 @@
             self.passing(r, step).start()
 
     def looped(self, step, steps):
-        for r in range(len(self.kinds)):
+        for r in self.later:
             first, last = self.spans[r]
             per = -(-(last - first) // steps)
             for k in range(per):
@@ -512,8 +524,8 @@
                     return carry
 
                 lax.fori_loop(0, self.nz, settle_y, 0)
-            if kind not in ("half", "across"):
-                self.own_copy(r).wait()
+            for copy in self.own_copies(r):
+                copy.wait()
 
 
 def rider_shapes(riders, devices):
@@ -524,7 +536,7 @@
         shape = v.shape
         if kind == "same":
             shape = (devices,) + shape
-        elif kind == "cube":
+        elif kind in ("cube", "pair"):
             shape = shape[:1] + (2,) + shape[1:]
         elif kind == "half":
             shape = shape[:1] + shape[2:]
@@ -537,7 +549,7 @@
 
 def rider_specs(kinds):
     return [
-        pl.BlockSpec(memory_space=pl.ANY if kind in ("half", "across") else pltpu.VMEM)
+        pl.BlockSpec(memory_space=pl.ANY if kind == "half" else pltpu.VMEM)
         for kind in kinds
     ]
 
@@ -614,7 +626,7 @@
             self.push(way, mine, None, True)
         self.keep(mine)
 
-    def turn(self, turn):
+    def turn_z(self, turn):
         nz, z, a, b, c = self.nz, self.z, self.a, self.b, self.c
         if turn < nz:
             for index, (allowed, zz) in enumerate(along(z, nz, turn)):
@@ -623,6 +635,9 @@
                 self.push(index, where, allowed & ((z > 0) if index else (z < nz - 1)))
                 for way in (2, 3, 4):
                     self.push(way, where, allowed)
+
+    def turn_xy(self, turn):
+        nz, z, a, b, c = self.nz, self.z, self.a, self.b, self.c
         if turn - 1 < nz:
             for allowed, zz in along(z, nz, turn - 1):
                 where = slot(zz, 1 - a, b, c)
@@ -658,7 +673,7 @@
             self.push(way, mine, None, True)
         self.keep(mine)
 
-    def turn(self, turn):
+    def turn_z(self, turn):
         nz, z = self.nz, self.z
         if turn < nz:
             for index, (allowed, zz) in enumerate(along(z, nz, turn)):
@@ -667,6 +682,9 @@
                 self.push(index, where, allowed & ((z > 0) if index else (z < nz - 1)))
                 for way in (2, 3):
                     self.push(way, where, allowed)
+
+    def turn_xy(self, turn):
+        nz, z = self.nz, self.z
         if turn - 1 < nz:
             for allowed, zz in along(z, nz, turn - 1):
                 where = zz * 4 + self.other
@@ -707,10 +725,12 @@
         else:
             mover.begin(nz, z, ep, x, c)
     riders.begin()
-    riders.some(0, 1)
     for turn in range(1, nz + 2):
+        if turn <= nz:
+            riders.some(turn - 1, nz)
         for mover in movers:
-            mover.turn(turn)
+            mover.turn_z(turn)
+            mover.turn_xy(turn)
         if 2 <= turn <= nz:
             riders.onwards(turn - 1)
     for mover in movers:
@@ -758,7 +778,7 @@
         refs[:extra] + refs[extra + 1 : 2 * extra + 1] + refs[2 * extra + 16 :]
     )
     greet(nz, z, dp, ep, ways, wide_greeting(kinds))
-    riders.begin()
+    riders.begin(("half", "line"))
     per = 4 * nz
 
     def zed(step):
@@ -1096,7 +1116,7 @@
     ]
     riders = Riders(kinds, nz, (dp, ep, z, y), rider_ins + rider_outs + tuple(refs))
     greet(nz, z, dp, ep, (up, down, near, far, twin), wide_greeting(kinds))
-    riders.begin()
+    riders.begin(("half", "line"))
 
     def side_step(pair, carry):
         for part in sums:
@@ -1277,7 +1297,7 @@
     probs_low = probs.astype(low)
     mixed = contract(probs_low, value_rows, "btu,bud->btd").astype(low).reshape(all_count, head_dim)
     largest_own = jnp.max(row_top)
-    branch, fall_own = scatter_sum(mixed, w_out, devices, 2, riders=(("line", w_down),))
+    branch, fall_own = scatter_sum(mixed, w_out, devices, 2, riders=(("line", w_down.transpose(0, 2, 1)),))
     resid_mid = resid_in + branch
 
     inv_two = rms_scale(resid_mid)
@@ -1289,14 +1309,11 @@
     gate_power = jnp.where(choose, jnp.exp(picked - jnp.max(picked, axis=1, keepdims=True)), 0.0)
     route = gate_power / jnp.sum(gate_power, axis=1, keepdims=True)
     note_two = jnp.pad(route.T, ((0, 0), (0, 128 - row_count)))
-    normed_all, notes, w_rise_gate, fall_other = gather_rows(
-        (), (normed_mid, note_two), devices, 3, (("cube", w_gate), ("across", fall_own))
+    normed_all, notes, w_rise_gate, w_fall = gather_rows(
+        (), (normed_mid, note_two), devices, 3, (("cube", w_gate), ("pair", fall_own))
     )
     w_rise_gate = w_rise_gate.reshape(width, hidden)
-    w_fall = jnp.where(
-        y == 0, jnp.stack([fall_own, fall_other], axis=1), jnp.stack([fall_other, fall_own], axis=1)
-    )
-    w_fall = w_fall.transpose(2, 0, 1, 3).reshape(hidden, width)
+    w_fall = w_fall.reshape(width, hidden)
 
     mine = ep * exp_local + z
     slab_rows = slab * row_count
@@ -1305,7 +1322,7 @@
     flat_grad = grad_all.reshape(slab_rows, width)
     gate_part = jnp.dot(flat_mid, w_rise_gate, preferred_element_type=f32)
     up_part = jnp.dot(flat_mid, w_rise_up, preferred_element_type=f32)
-    grad_plain = contract(flat_grad, w_fall, "td,fd->tf")
+    grad_plain = jnp.dot(flat_grad, w_fall, preferred_element_type=f32)
     sigmoid_gate = jax.nn.sigmoid(gate_part)
     silu_gate = gate_part * sigmoid_gate
     hidden_mid = silu_gate * up_part
@@ -1328,7 +1345,7 @@
     summed, moe_rows, gate_come, up_come, fall_come = slab_scatter(
         (
             ((grad_gate_part, grad_up_part), (w_rise_gate, w_rise_up), True, beside),
-            ((weighted_mid,), (w_fall,), False, None),
+            ((weighted_mid,), (w_fall,), True, None),
         ),
         devices,
         4,

time: 945 us -> 862 us (0.912)
  Pallas kernels: 715 us -> 650 us
  local copies, waits for them, and re-layouts: 35.9 us -> 26 us
    pallas_call x3, Pallas kernels: 389 us -> 348 us  [gather_rows(): pl.pallas_call(functools.partial(gather_kernel, nz, (len(whole), len(slab...]
    dot_general x15 -> x14, matrix products: 88.4 us -> 70.2 us  [contract(): jnp.einsum(pattern, left_side, right_side, preferred_element_type=jnp.flo...]
    pallas_call x1, Pallas kernels: 131 us -> 117 us  [slab_scatter(): pl.pallas_call(functools.partial(slab_scatter_kernel, nz, tuple(forms), k...]
    dot_general x0 -> x1, matrix products: none -> 11.7 us  [by_experts(): grad_plain = jnp.dot(flat_grad, w_fall, preferred_element_type=f32)]
    pallas_call x2, Pallas kernels: 195 us -> 185 us  [scatter_sum(): pl.pallas_call(functools.partial(scatter_kernel, nz, turned, kinds), out_...]
where the time goes in v5:
time: 862 us; the launch traced here: 850 us
  Pallas kernels  650 us (75%)
  matrix products  120 us (14%)
  other arithmetic  51.4 us (6%)
  local copies, waits for them, and re-layouts  26 us (3%)
    pallas_call x3, Pallas kernels, gather_rows(): pl.pallas_call(functools.partial(gather_kernel, nz, (len(whole), len(slab...  348 us
    pallas_call x2, Pallas kernels, scatter_sum(): pl.pallas_call(functools.partial(scatter_kernel, nz, turned, kinds), out_...  185 us
    pallas_call x1, Pallas kernels, slab_scatter(): pl.pallas_call(functools.partial(slab_scatter_kernel, nz, tuple(forms), k...  117 us
    dot_general x14, matrix products, contract(): jnp.einsum(pattern, left_side, right_side, preferred_element_type=jnp.flo...  70.2 us

profile of v5, /device:TPU:1, one launch (start us, length us, event | category | flops | bytes accessed | tf_op | source)
XLA Modules:
  0.0 849.9 jit_solution(2414264320142683829)
XLA Ops:
  14.5 146.5 %gather_rows_1.1 = (bf16[32,112,2048]{2,1,0:T(8,128)(2,1)}, f32[32,16,128]{2,1,0:T(8,128)}, bf16[16,112,2048]{2,1,0:T(8,128)(2,1)}, bf16[32,64,384]{2,1,0:T(8,128)(2,1)}, bf16[4,2,256,768]{3,2,1,0:T(8,128)(2,1)}) custom-call(bf16[112,2048]{1,0:T(8,128)(2,1)} %multiply_convert_fusion.7.refs_0_, f32[16,128]{1,0:T(8,128)} %pad.27.refs_1_, ...), custom_call_target="tpu_custom_call" | custom-call | tf_op jit(solution)/shard_map/gather_rows_1/pallas_call | solution.py:751
  167.6 11.9 %fusion.65 = f32[32,112,384]{2,1,0:T(8,128)S(1)} fusion(bf16[32,112,2048]{2,1,0:T(8,128)(2,1)} %get-tuple-element.41, bf16[2048,384,1]{1,0,2:T(8,128)(2,1)S(1)} %bitcast.177), kind=kOutput, calls=%fused_computation.188 | convolution fusion | flops 5637144576 | bytes 21757952 | tf_op jit(solution)/shard_map/dot_general | solution.py:1278
  185.7 1.8 fusion.62
  187.5 3.1 convolution_convert_fusion.6.refs_0_
  190.6 77.0 %scatter_sum_2.1 = (f32[112,2048]{1,0:T(8,128)}, bf16[4,256,768]{2,1,0:T(8,128)(2,1)}) custom-call(bf16[32,112,128]{2,1,0:T(8,128)(2,1)} %convolution_convert_fusion.6.refs_0_, bf16[128,2048]{1,0:T(8,128)(2,1)} %refs_1_.1, bf16[4,256,768]{2,1,0:T(8,128)(2,1)} %bitcast.164), custom_call_target="tpu_custom_call" | custom-call | tf_op jit(solution)/shard_map/scatter_sum_2/pallas_call | solution.py:922
  271.5 83.8 %gather_rows_3.1 = (bf16[16,112,2048]{2,1,0:T(8,128)(2,1)}, f32[16,16,128]{2,1,0:T(8,128)}, bf16[4,2,256,768]{3,2,1,0:T(8,128)(2,1)}, bf16[4,2,256,768]{3,2,1,0:T(8,128)(2,1)}) custom-call(bf16[112,2048]{1,0:T(8,128)(2,1)} %copy-done.13, f32[16,128]{1,0:T(8,128)} %pad.28.refs_1_, bf16[4,256,768]{2,1,0:T(8,128)(2,1)} %refs_2_.1, ...), custom_call_target="tpu_custom_call" | custom-call | tf_op jit(solution)/shard_map/gather_rows_3/pallas_call | solution.py:751
  356.4 10.7 %fusion.68 = f32[1792,768]{1,0:T(8,128)} fusion(bf16[1792,2048]{1,0:T(8,128)(2,1)} %bitcast.195, bf16[2048,768]{1,0:T(8,128)(2,1)} %bitcast.167), kind=kOutput, calls=%fused_computation.191 | convolution fusion | flops 5637144576 | bytes 15990784 | tf_op jit(solution)/shard_map/dot_general | solution.py:1323
  367.1 7.9 fusion.67
  375.0 11.7 %multiply_reduce_fusion = (bf16[1792]{0:T(1024)(128)(2,1)S(1)}, bf16[1792,768]{1,0:T(8,128)(2,1)S(1)}, bf16[1792,768]{1,0:T(8,128)(2,1)S(1)}, bf16[1792,768]{1,0:T(8,128)(2,1)}) fusion(f32[1792,768]{1,0:T(8,128)} %fusion.67, f32[1792,768]{1,0:T(8,128)} %fusion.68, f32[1792]{0:T(1024)S(1)} %mul.378, bf16[1792,2048]{1,0:T(8,128)(2,1)S(1)} %bitcast.193, ...), kind=kOutput, calls=%fused_computation.2 | convolution fusion | flops 5663291392 | bytes 29764096 | tf_op jit(solution)/shard_map/dot_general | solution.py:1325
  386.8 7.7 convolution_convert_fusion.1
  395.6 10.8 %convolution_convert_fusion.3 = bf16[2048,768]{1,0:T(8,128)(2,1)} fusion(bf16[1792,2048]{1,0:T(8,128)(2,1)} %bitcast.196, bf16[1792,768]{1,0:T(8,128)(2,1)S(1)} %get-tuple-element.174), kind=kOutput, calls=%fused_computation.10 | convolution fusion | flops 5638717440 | bytes 13238272 | tf_op jit(solution)/shard_map/td,tf->df/dot_general | solution.py:42
  406.4 10.9 %convolution_convert_fusion.2 = bf16[2048,768]{1,0:T(8,128)(2,1)} fusion(bf16[1792,2048]{1,0:T(8,128)(2,1)} %bitcast.197, bf16[1792,768]{1,0:T(8,128)(2,1)S(1)} %copy-done.31), kind=kOutput, calls=%fused_computation.9 | convolution fusion | flops 5638717440 | bytes 13238272 | tf_op jit(solution)/shard_map/td,tf->df/dot_general | solution.py:42
  417.3 117.5 %slab_scatter_4.1 = (f32[112,2176]{1,0:T(8,128)}, f32[112,2048]{1,0:T(8,128)}, bf16[4,256,768]{2,1,0:T(8,128)(2,1)}, bf16[4,256,768]{2,1,0:T(8,128)(2,1)}, bf16[4,256,768]{2,1,0:T(8,128)(2,1)}) custom-call(bf16[16,112,768]{2,1,0:T(8,128)(2,1)} %bitcast.171, bf16[16,112,768]{2,1,0:T(8,128)(2,1)} %bitcast.173, bf16[2048,768]{1,0:T(8,128)(2,1)} %bitcast.168, ...), custom_call_target="tpu_custom_call" | custom-call | tf_op jit(solution)/shard_map/slab_scatter_4/pallas_call | solution.py:1157
  534.8 3.5 fusion.2.refs_3_
  541.3 1.6 fusion.4.refs_2_
  545.2 3.2 multiply_reduce_fusion.9
  550.7 2.5 fusion.58
  554.5 117.7 %gather_rows_6.1 = (bf16[32,112,2048]{2,1,0:T(8,128)(2,1)}, f32[32,24,128]{2,1,0:T(8,128)}, bf16[4,256,768]{2,1,0:T(8,128)(2,1)}, bf16[4,256,768]{2,1,0:T(8,128)(2,1)}) custom-call(bf16[112,2048]{1,0:T(8,128)(2,1)} %get-tuple-element.169.refs_0_, f32[24,128]{1,0:T(8,128)} %concatenate.32.refs_1_, bf16[4,256,768]{2,1,0:T(8,128)(2,1)} %fusion.4.refs_2_, ...), custom_call_target="tpu_custom_call" | custom-call | tf_op jit(solution)/shard_map/gather_rows_6/pallas_call | solution.py:751
  675.5 8.4 convolution_bitcast_fusion
  685.2 5.1 convolution_convert_fusion
  690.3 3.1 convolution_convert_fusion.5
  693.4 2.4 multiply_reduce_fusion.5
  698.4 1.9 convert_element_type.281
  703.3 1.9 convert_element_type.282
  706.8 3.5 multiply_reduce_fusion.2
  710.9 2.2 multiply_convert_fusion.4
  713.2 12.0 %bitcast_convert_fusion = bf16[2048,384]{1,0:T(8,128)(2,1)} fusion(bf16[32,112,2048]{2,1,0:T(8,128)(2,1)} %get-tuple-element.41, bf16[32,112,128]{2,1,0:T(8,128)(2,1)S(1)} %convolution_convert_fusion.5, bf16[32,112,128]{2,1,0:T(8,128)(2,1)S(1)} %get-tuple-element.178, bf16[32,112,128]{2,1,0:T(8,128)(2,1)S(1)} %get-tuple-element.177), kind=kOutput, calls=%fused_computation.17 | convolution fusion | flops 5646188544 | bytes 19005440 | tf_op jit(solution)/shard_map/td,tq->dq/dot_general | solution.py:42
  725.1 1.9 pad_maximum_fusion.refs_0_
  727.0 107.9 %scatter_sum_7.1 = (f32[112,2048]{1,0:T(8,128)}, bf16[32,64,384]{2,1,0:T(8,128)(2,1)}, bf16[4,256,768]{2,1,0:T(8,128)(2,1)}, f32[32,8,128]{2,1,0:T(8,128)}, f32[32,8,128]{2,1,0:T(8,128)}) custom-call(bf16[32,112,384]{2,1,0:T(8,128)(2,1)} %pad_maximum_fusion.refs_0_, bf16[2048,384]{1,0:T(8,128)(2,1)} %bitcast.176, bf16[32,64,384]{2,1,0:T(8,128)(2,1)} %bitcast.178, ...), custom_call_target="tpu_custom_call" | custom-call | tf_op jit(solution)/shard_map/scatter_sum_7/pallas_call | solution.py:922
  836.6 1.8 fusion.15
  844.0 1.9 convert_bitcast_fusion
  845.9 3.5 copy.147
  (240 shorter events, 60.5 us)
Async XLA Ops:
  0.6 10.8 %copy-start = (bf16[128,2048]{1,0:T(8,128)(2,1)S(1)}, bf16[128,2048]{1,0:T(8,128)(2,1)}, u32[]{:S(2)}) copy-start(bf16[128,2048]{1,0:T(8,128)(2,1)} %param.19) | copy-start | bytes 1572868
  0.7 7.9 copy-start.32
  1.5 8.7 %copy-start.52 = (f32[64]{0:T(128)}, f32[64]{0:T(128)S(1)}, u32[]{:S(2)}) copy-start(f32[64]{0:T(128)S(1)} %convert_element_type.231) | copy-start | bytes 772
  2.1 178.5 %copy-start.56 = (f32[128]{0:T(128)}, f32[128]{0:T(128)S(1)}, u32[]{:S(2)}) copy-start(f32[128]{0:T(128)S(1)} %convert_element_type.242) | copy-start | bytes 1540
  2.8 177.9 %copy-start.58 = (f32[128]{0:T(128)}, f32[128]{0:T(128)S(1)}, u32[]{:S(2)}) copy-start(f32[128]{0:T(128)S(1)} %convert_element_type.245) | copy-start | bytes 1540
  3.5 539.4 %copy-start.50 = (s32[128]{0:T(128)}, s32[128]{0:T(128)S(1)}, u32[]{:S(2)}) copy-start(s32[128]{0:T(128)S(1)} %and_select_fusion) | copy-start | bytes 1540
  10.6 257.1 %copy-start.6 = (f32[112,2048]{1,0:T(8,128)}, f32[112,2048]{1,0:T(8,128)S(1)}, u32[]{:S(2)}) copy-start(f32[112,2048]{1,0:T(8,128)S(1)} %get-tuple-element.207) | copy-start | bytes 2752516
  10.6 3.9 copy-start.54
  164.9 105.3 %copy-start.17 = (bf16[2048,16]{1,0:T(8,128)(2,1)}, bf16[2048,16]{1,0:T(8,128)(2,1)S(1)}, u32[]{:S(2)}) copy-start(bf16[2048,16]{1,0:T(8,128)(2,1)S(1)} %convert_element_type.250) | copy-start | bytes 196612
  166.2 17.0 %copy-start.10 = (f32[3584,128]{1,0:T(8,128)}, f32[3584,128]{1,0:T(8,128)S(1)}, u32[]{:S(2)}) copy-start(f32[3584,128]{1,0:T(8,128)S(1)} %fusion.9) | copy-start | bytes 5505028
  167.5 15.7 %copy-start.8 = (f32[3584,128]{1,0:T(8,128)}, f32[3584,128]{1,0:T(8,128)S(1)}, u32[]{:S(2)}) copy-start(f32[3584,128]{1,0:T(8,128)S(1)} %fusion.10) | copy-start | bytes 5505028
  270.0 275.2 %copy-start.60 = (f32[112]{0:T(128)}, f32[112]{0:T(128)S(1)}, u32[]{:S(2)}) copy-start(f32[112]{0:T(128)S(1)} %add_rsqrt_fusion.2) | copy-start | bytes 1348
  356.3 10.7 %copy-start.27 = (bf16[4,2,256,768]{3,2,1,0:T(8,128)(2,1)S(1)}, bf16[4,2,256,768]{3,2,1,0:T(8,128)(2,1)}, u32[]{:S(2)}) copy-start(bf16[4,2,256,768]{3,2,1,0:T(8,128)(2,1)} %get-tuple-element.49) | copy-start | bytes 9437188
  356.3 10.7 %copy-start.63 = (bf16[16,112,2048]{2,1,0:T(8,128)(2,1)S(1)}, bf16[16,112,2048]{2,1,0:T(8,128)(2,1)}, u32[]{:S(2)}) copy-start(bf16[16,112,2048]{2,1,0:T(8,128)(2,1)} %get-tuple-element.48) | copy-start | bytes 22020100
  356.3 18.7 %slice-start.2 = ((s8[7340032]{0:T(1024)(128)(4,1)}), s8[4194304]{0:T(1024)(128)(4,1)S(1)}, s32[]{:S(2)}) async-start(s8[7340032]{0:T(1024)(128)(4,1)} %bitcast.191), calls=%async_computation.2 | async-start | bytes 8388608
  367.1 8.0 copy-start.28
  367.1 8.0 slice-start.3
  386.8 7.7 copy-start.30
  386.8 8.8 %copy-start.29 = (bf16[1792,768]{1,0:T(8,128)(2,1)}, bf16[1792,768]{1,0:T(8,128)(2,1)S(1)}, u32[]{:S(2)}) copy-start(bf16[1792,768]{1,0:T(8,128)(2,1)S(1)} %get-tuple-element.174) | copy-start | bytes 8257540
  395.6 10.8 %copy-start.31 = (bf16[1792,768]{1,0:T(8,128)(2,1)S(1)}, bf16[1792,768]{1,0:T(8,128)(2,1)}, u32[]{:S(2)}) copy-start(bf16[1792,768]{1,0:T(8,128)(2,1)} %get-tuple-element.176) | copy-start | bytes 8257540
  534.8 3.6 copy-start.16
  534.8 3.6 copy-start.36
  544.1 4.3 copy-start.14
  554.4 120.5 %copy-start.64 = (f32[32]{0:T(128)S(1)}, f32[32]{0:T(128)}, u32[]{:S(2)}) copy-start(f32[32]{0:T(128)} %param.35) | copy-start | bytes 388
  554.5 121.0 %copy-start.19 = (bf16[32,112,128]{2,1,0:T(8,128)(2,1)S(1)}, bf16[32,112,128]{2,1,0:T(8,128)(2,1)}, u32[]{:S(2)}) copy-start(bf16[32,112,128]{2,1,0:T(8,128)(2,1)} %convolution_convert_fusion.6.refs_0_) | copy-start | bytes 2752516
  675.5 9.7 %copy-start.3 = (bf16[32,112,2048]{2,1,0:T(8,128)(2,1)S(1)}, bf16[32,112,2048]{2,1,0:T(8,128)(2,1)}, u32[]{:S(2)}) copy-start(bf16[32,112,2048]{2,1,0:T(8,128)(2,1)} %get-tuple-element.55) | copy-start | bytes 44040196
  675.5 9.8 %copy-start.45 = (bf16[128,2048]{1,0:T(8,128)(2,1)S(1)}, bf16[128,2048]{1,0:T(8,128)(2,1)}, u32[]{:S(2)}) copy-start(bf16[128,2048]{1,0:T(8,128)(2,1)} %refs_1_.1) | copy-start | bytes 1572868
  701.9 4.2 slice-start
  727.0 107.9 %copy-start.7 = (f32[112,2048]{1,0:T(8,128)S(1)}, f32[112,2048]{1,0:T(8,128)}, u32[]{:S(2)}) copy-start(f32[112,2048]{1,0:T(8,128)} %copy-done.6) | copy-start | bytes 2752516
  727.0 107.9 %copy-start.55 = (f32[112]{0:T(128)S(1)}, f32[112]{0:T(128)}, u32[]{:S(2)}) copy-start(f32[112]{0:T(128)} %copy-done.54) | copy-start | bytes 1348
  836.6 3.2 copy-start.42
  844.0 5.5 copy-start.1
  (37 other events, 69.2 us)

commit v6 on v5

--- a/solution.py
+++ b/solution.py
@@ -762,11 +762,65 @@
     )(*arrays, *ridden)
 
 
-def scatter_kernel(nz, turned, kinds, *refs):
+class Job:
+    def __init__(self, held, stream, out, chunk, arrived):
+        self.held, self.stream, self.out = held, stream, out
+        self.chunk, self.arrived = chunk, arrived
+        self.span = chunk.shape[2]
+        self.count = stream.shape[1] // self.span
+
+    def columns(self, index):
+        return pl.ds(pl.multiple_of(index * self.span, self.span), self.span)
+
+    def load(self, index):
+        return pltpu.make_async_copy(
+            self.stream.at[:, self.columns(index)], self.chunk.at[index % 2],
+            self.arrived.at[index % 2])
+
+    def begin(self):
+        self.load(0).start()
+        self.load(1).start()
+
+    def run(self, index):
+        self.load(index).wait()
+        value = jnp.dot(
+            self.held[...], self.chunk[index % 2], preferred_element_type=jnp.float32
+        ).astype(self.out.dtype)
+        if len(self.out.shape) == 3:
+            self.out[index] = value
+        else:
+            self.out[:, self.columns(index)] = value
+
+        @pl.when(index + 2 < self.count)
+        def _():
+            self.load(index + 2).start()
+
+
+def job_shapes(job, blocked):
+    if job is None:
+        return (), (), [], []
+    held, stream = job
+    span = 256
+    if blocked:
+        shape, dtype = (stream.shape[1] // span, held.shape[0], span), jnp.bfloat16
+    else:
+        shape, dtype = (held.shape[0], stream.shape[1]), jnp.float32
+    specs = [pl.BlockSpec(memory_space=pltpu.VMEM), pl.BlockSpec(memory_space=pl.ANY)]
+    scratch = [pltpu.VMEM((2, stream.shape[0], span), stream.dtype), pltpu.SemaphoreType.DMA((2,))]
+    return job, (jax.ShapeDtypeStruct(shape, dtype),), specs, scratch
+
+
+def scatter_kernel(nz, turned, jobs, kinds, *refs):
     extra = len(kinds)
     left_ref, right_ref = refs[:2]
-    refs = refs[2:]
+    held = refs[2 : 2 + 2 * jobs]
+    refs = refs[2 + 2 * jobs :]
     out_ref = refs[extra]
+    held += refs[extra + 1 : extra + 1 + jobs]
+    refs = refs[: extra + 1] + refs[extra + 1 + jobs :]
+    held += refs[2 * extra + 16 : 2 * extra + 16 + 2 * jobs]
+    refs = refs[: 2 * extra + 16] + refs[2 * extra + 16 + 2 * jobs :]
+    job = Job(*held) if jobs else None
     sent, got, from_far, from_near, rising, falling = refs[2 * extra + 1 : 2 * extra + 7]
     (twin_send, twin_recv, far_send, far_recv, near_send, near_recv, line_send, up_recv,
      down_recv) = refs[2 * extra + 7 : 2 * extra + 16]
@@ -779,6 +833,8 @@
     )
     greet(nz, z, dp, ep, ways, wide_greeting(kinds))
     riders.begin(("half", "line"))
+    if jobs:
+        job.begin()
     per = 4 * nz
 
     def zed(step):
@@ -845,12 +901,19 @@
 
     lax.fori_loop(0, 2 * nz, far_step, 0)
 
+    def work(index, carry):
+        job.run(index)
+        return carry
+
     def near_step(step, carry):
         value = taken(2 * nz + step)
         far_copy(step).wait_recv()
         value = value + from_far[step].astype(jnp.float32)
         got[2 * nz + step] = value.astype(got.dtype)
         near_copy(step).start()
+        if jobs:
+            share = job.count // nz
+            lax.fori_loop(step * share, step * share + share, work, 0)
         return carry
 
     lax.fori_loop(0, nz, near_step, 0)
@@ -911,19 +974,20 @@
     riders.finish()
 
 
-def scatter_sum(left, right, devices, ident, turned=False, riders=()):
+def scatter_sum(left, right, devices, ident, turned=False, riders=(), job=None):
     nz = devices // 8
     rows = left.shape[0] // devices
     depth, wide = right.shape[::-1] if turned else right.shape
     kinds, ridden, rider_outs, rider_sems = rider_shapes(riders, devices)
+    job_ins, job_outs, job_specs, job_scratch = job_shapes(job, False)
     block = (rows, wide)
     low = jnp.bfloat16
     dma = pltpu.SemaphoreType.DMA
     result = pl.pallas_call(
-        functools.partial(scatter_kernel, nz, turned, kinds),
-        out_shape=(jax.ShapeDtypeStruct(block, jnp.float32),) + rider_outs,
-        in_specs=[pl.BlockSpec(memory_space=pltpu.VMEM)] * 2 + rider_specs(kinds),
-        out_specs=(pl.BlockSpec(memory_space=pltpu.VMEM),)
+        functools.partial(scatter_kernel, nz, turned, len(job_outs), kinds),
+        out_shape=(jax.ShapeDtypeStruct(block, jnp.float32),) + job_outs + rider_outs,
+        in_specs=[pl.BlockSpec(memory_space=pltpu.VMEM)] * 2 + job_specs + rider_specs(kinds),
+        out_specs=(pl.BlockSpec(memory_space=pltpu.VMEM),) * (1 + len(job_outs))
         + (pl.BlockSpec(memory_space=pl.ANY),) * len(riders),
         scratch_shapes=[
             pltpu.VMEM((4 * nz,) + block, low),
@@ -935,11 +999,12 @@
             dma((4 * nz,)), dma((4 * nz,)), dma((2 * nz,)), dma((2 * nz,)),
             dma((nz,)), dma((nz,)), dma((nz,)), dma((nz,)), dma((nz,)),
         ]
+        + job_scratch
         + rider_sems,
         compiler_params=pltpu.CompilerParams(
             collective_id=ident, has_side_effects=True, vmem_limit_bytes=58 * 2**20),
         name="scatter_sum_%d" % ident,
-    )(left.reshape(devices, rows, depth), right, *ridden)
+    )(left.reshape(devices, rows, depth), right, *job_ins, *ridden)
     return result if riders else result[0]
 
 
@@ -1092,7 +1157,7 @@
         lax.fori_loop(0, self.nz, finish_side, 0)
 
 
-def slab_scatter_kernel(nz, forms, kinds, *refs):
+def slab_scatter_kernel(nz, forms, jobs, kinds, *refs):
     extra, parts = len(kinds), len(forms)
     refs = list(refs)
 
@@ -1104,19 +1169,27 @@
     operands = []
     for pairs, turned, beside in forms:
         operands.append((take(pairs), take(pairs), take(1)[0] if beside else None))
+    held = take(2 * jobs)
     rider_ins = take(extra)
     outs = take(parts)
+    held += take(jobs)
+    come = take(jobs)
     rider_outs = take(extra)
     dp, ep, z, y, x, c, _, _ = place()
     up, down, near, far, twin = targets(dp, ep, z, y, x, c, nz)
     side = (dp, ep + 2 - 4 * x)
     sums = [
-        SlabSum(nz, form[1], (z, x, c), (up, down, side, twin), held + (out,), take(13))
-        for form, held, out in zip(forms, operands, outs)
+        SlabSum(nz, form[1], (z, x, c), (up, down, side, twin), given + (out,), take(13))
+        for form, given, out in zip(forms, operands, outs)
     ]
+    if jobs:
+        job = Job(*(held + take(2)))
+        made_send, made_recv = take(2)
     riders = Riders(kinds, nz, (dp, ep, z, y), rider_ins + rider_outs + tuple(refs))
     greet(nz, z, dp, ep, (up, down, near, far, twin), wide_greeting(kinds))
     riders.begin(("half", "line"))
+    if jobs:
+        job.begin()
 
     def side_step(pair, carry):
         for part in sums:
@@ -1126,23 +1199,47 @@
 
     lax.fori_loop(0, nz // 2, side_step, 0)
 
+    def work(index, carry):
+        job.run(index)
+        return carry
+
+    def made_copy(step):
+        return pltpu.make_async_remote_copy(
+            src_ref=job.out.at[2 * step + 1 - y], dst_ref=come[0].at[step],
+            send_sem=made_send.at[step], recv_sem=made_recv.at[step],
+            device_id=riders.over_y, device_id_type=MESH)
+
     def line_step(pair, carry):
         for part in sums:
             part.to_line(pair)
+        if jobs:
+            lax.fori_loop(0, jnp.where(pair == 0, job.count, 0), work, 0)
+
+            @pl.when(pair == 0)
+            def _():
+                for step in range(nz):
+                    made_copy(step).start()
+
         return carry
 
     lax.fori_loop(0, nz // 2, line_step, 0)
     for part in sums:
         part.end()
+    if jobs:
+        for step in range(nz):
+            made_copy(step).wait()
     riders.finish()
 
 
-def slab_scatter(parts, devices, ident, riders=()):
+def slab_scatter(parts, devices, ident, riders=(), job=None):
     nz = devices // 8
     blocks = 4 * nz
     rows = parts[0][0][0].shape[0] // blocks
     kinds, ridden, rider_outs, rider_sems = rider_shapes(riders, devices)
+    job_ins, job_outs, job_specs, job_scratch = job_shapes(job, True)
     low, dma = jnp.bfloat16, pltpu.SemaphoreType.DMA
+    come = tuple(jax.ShapeDtypeStruct((nz,) + v.shape[1:], v.dtype) for v in job_outs)
+    job_scratch += [dma((nz,))] * (2 * len(come))
     operands, outs, scratch, forms = (), (), [], []
     for lefts, rights, turned, beside in parts:
         held = () if beside is None else (beside.reshape(blocks, rows, -1),)
@@ -1155,16 +1252,16 @@
         scratch += [dma((2 * nz,))] * 2 + [dma((nz,))] * 5
         forms.append((len(lefts), turned, len(held)))
     return pl.pallas_call(
-        functools.partial(slab_scatter_kernel, nz, tuple(forms), kinds),
-        out_shape=outs + rider_outs,
-        in_specs=[pl.BlockSpec(memory_space=pltpu.VMEM)] * len(operands) + rider_specs(kinds),
-        out_specs=(pl.BlockSpec(memory_space=pltpu.VMEM),) * len(outs)
-        + (pl.BlockSpec(memory_space=pl.ANY),) * len(riders),
-        scratch_shapes=scratch + rider_sems,
+        functools.partial(slab_scatter_kernel, nz, tuple(forms), len(job_outs), kinds),
+        out_shape=outs + job_outs + come + rider_outs,
+        in_specs=[pl.BlockSpec(memory_space=pltpu.VMEM)] * len(operands) + job_specs + rider_specs(kinds),
+        out_specs=(pl.BlockSpec(memory_space=pltpu.VMEM),) * (len(outs) + len(job_outs))
+        + (pl.BlockSpec(memory_space=pl.ANY),) * (len(come) + len(riders)),
+        scratch_shapes=scratch + job_scratch + rider_sems,
         compiler_params=pltpu.CompilerParams(
             collective_id=ident, has_side_effects=True, vmem_limit_bytes=63 * 2**20),
         name="slab_scatter_%d" % ident,
-    )(*operands, *ridden)
+    )(*operands, *job_ins, *ridden)
 
 
 def whole_rows(mesh):
@@ -1341,16 +1438,17 @@
 
     gate_halves = for_each_y(contract(flat_mid, grad_gate_part, "td,tf->df"))
     up_halves = for_each_y(contract(flat_mid, grad_up_part, "td,tf->df"))
-    fall_halves = for_each_y(contract(flat_grad, weighted_mid, "td,tf->df"))
-    summed, moe_rows, gate_come, up_come, fall_come = slab_scatter(
+    summed, moe_rows, fall_halves, fall_come, gate_come, up_come = slab_scatter(
         (
             ((grad_gate_part, grad_up_part), (w_rise_gate, w_rise_up), True, beside),
             ((weighted_mid,), (w_fall,), True, None),
         ),
         devices,
         4,
-        (("half", gate_halves), ("half", up_halves), ("half", fall_halves)),
-    )
+        (("half", gate_halves), ("half", up_halves)),
+        (weighted_mid.T, flat_grad),
+    )
+    fall_halves = fall_halves.reshape(lines, 2, hidden, wide_own)
 
     def add_halves(halves, come):
         kept = lax.dynamic_index_in_dim(halves, y, axis=1, keepdims=False)
@@ -1386,7 +1484,6 @@
     grad_gain_moe = lax.dynamic_slice_in_dim(gain_sum, me * rows_own, rows_own)
 
     flat_branch = branch_all.reshape(all_count, width)
-    grad_out = contract(mixed, flat_branch, "tq,td->qd")
     grad_mixed = (
         contract(flat_branch, w_out, "td,qd->tq").astype(low).reshape(devices, row_count, head_dim)
     )
@@ -1415,7 +1512,7 @@
     undeal = (jnp.arange(tok_count, dtype=jnp.int32)[:, None] == local_order[None, :]).astype(low)
     undeal = undeal[:, :row_count]
     block_out = jnp.dot(undeal, resid_out.astype(low), preferred_element_type=f32).astype(low)
-    grad_unit_one, back_heads, back_fall, gain_pairs, router_parts = scatter_sum(
+    grad_unit_one, grad_out, back_heads, back_fall, gain_pairs, router_parts = scatter_sum(
         grad_heads,
         w_heads,
         devices,
@@ -1427,11 +1524,12 @@
             ("same", jnp.pad(gain_pair, ((0, 6), (0, 0)))),
             ("all", router_part),
         ),
+        job=(mixed.T, flat_branch),
     )
     back_heads = back_heads.astype(f32)
     grad_gate = back_gate.astype(f32)
     grad_up = back_up.astype(f32)
-    grad_down = back_fall.transpose(0, 2, 1).astype(f32)
+    grad_down = back_fall.astype(f32)
     grad_router = jnp.sum(router_parts, axis=0).reshape(rows_own, experts)
     gain_pair = jnp.sum(gain_pairs, axis=0)
     plain_query = back_heads[..., :head_dim].transpose(1, 0, 2).reshape(rows_own, -1)

time: 862 us -> 889 us (1.031)
  Pallas kernels: 650 us -> 670 us
  local copies, waits for them, and re-layouts: 26 us -> 37 us
  matrix products: 120 us -> 110 us
    pallas_call x3, Pallas kernels: 348 us -> 366 us  [gather_rows(): pl.pallas_call(functools.partial(gather_kernel, nz, (len(whole), len(slab...]
    dot_general x0 -> x2, local copies, waits for them, and re-layouts: none -> 13.2 us  [the longest x1 7.1 us: by_experts(): gate_part = jnp.dot(flat_mid, w_rise_gate, preferred_element_type=f32)]
    dot_general x14 -> x12, matrix products: 70.2 us -> 57.3 us  [contract(): jnp.einsum(pattern, left_side, right_side, preferred_element_type=jnp.flo...]
where the time goes in v6:
time: 889 us; the launch traced here: 878 us
  Pallas kernels  670 us (75%)
  matrix products  110 us (12%)
  other arithmetic  58.6 us (7%)
  local copies, waits for them, and re-layouts  37 us (4%)
    pallas_call x3, Pallas kernels, gather_rows(): pl.pallas_call(functools.partial(gather_kernel, nz, (len(whole), len(slab...  366 us
    pallas_call x2, Pallas kernels, scatter_sum(): pl.pallas_call(functools.partial(scatter_kernel, nz, turned, len(job_outs...  186 us
    pallas_call x1, Pallas kernels, slab_scatter(): pl.pallas_call(functools.partial(slab_scatter_kernel, nz, tuple(forms), l...  118 us
    dot_general x12, matrix products, contract(): jnp.einsum(pattern, left_side, right_side, preferred_element_type=jnp.flo...  57.3 us

profile of v6, /device:TPU:1, one launch (start us, length us, event | category | flops | bytes accessed | tf_op | source)
XLA Modules:
  0.0 878.0 jit_solution(12473736576447072423)
XLA Ops:
  14.4 146.5 %gather_rows_1.1 = (bf16[32,112,2048]{2,1,0:T(8,128)(2,1)}, f32[32,16,128]{2,1,0:T(8,128)}, bf16[16,112,2048]{2,1,0:T(8,128)(2,1)}, bf16[32,64,384]{2,1,0:T(8,128)(2,1)}, bf16[4,2,256,768]{3,2,1,0:T(8,128)(2,1)}) custom-call(bf16[112,2048]{1,0:T(8,128)(2,1)} %multiply_convert_fusion.7.refs_0_, f32[16,128]{1,0:T(8,128)} %pad.27.refs_1_, ...), custom_call_target="tpu_custom_call" | custom-call | tf_op jit(solution)/shard_map/gather_rows_1/pallas_call | solution.py:751
  167.6 11.9 %fusion.70 = f32[32,112,384]{2,1,0:T(8,128)S(1)} fusion(bf16[32,112,2048]{2,1,0:T(8,128)(2,1)} %get-tuple-element.43, bf16[2048,384,1]{1,0,2:T(8,128)(2,1)S(1)} %bitcast.193), kind=kOutput, calls=%fused_computation.193 | convolution fusion | flops 5637144576 | bytes 21757952 | tf_op jit(solution)/shard_map/dot_general | solution.py:1375
  185.7 1.9 fusion.67
  187.6 3.4 convolution_convert_fusion.5.refs_0_
  192.3 77.0 %scatter_sum_2.1 = (f32[112,2048]{1,0:T(8,128)}, bf16[4,256,768]{2,1,0:T(8,128)(2,1)}) custom-call(bf16[32,112,128]{2,1,0:T(8,128)(2,1)} %copy-done.18, bf16[128,2048]{1,0:T(8,128)(2,1)} %refs_1_.1, bf16[4,256,768]{2,1,0:T(8,128)(2,1)} %bitcast.178), custom_call_target="tpu_custom_call" | custom-call | tf_op jit(solution)/shard_map/scatter_sum_2/pallas_call | solution.py:986
  273.1 83.7 %gather_rows_3.1 = (bf16[16,112,2048]{2,1,0:T(8,128)(2,1)}, f32[16,16,128]{2,1,0:T(8,128)}, bf16[4,2,256,768]{3,2,1,0:T(8,128)(2,1)}, bf16[4,2,256,768]{3,2,1,0:T(8,128)(2,1)}) custom-call(bf16[112,2048]{1,0:T(8,128)(2,1)} %copy-done.12, f32[16,128]{1,0:T(8,128)} %pad.28.refs_1_, bf16[4,256,768]{2,1,0:T(8,128)(2,1)} %refs_2_.1, ...), custom_call_target="tpu_custom_call" | custom-call | tf_op jit(solution)/shard_map/gather_rows_3/pallas_call | solution.py:751
  357.8 10.7 %fusion.73 = f32[1792,768]{1,0:T(8,128)} fusion(bf16[1792,2048]{1,0:T(8,128)(2,1)} %bitcast.208, bf16[2048,768]{1,0:T(8,128)(2,1)} %bitcast.183), kind=kOutput, calls=%fused_computation.196 | convolution fusion | flops 5637144576 | bytes 15990784 | tf_op jit(solution)/shard_map/dot_general | solution.py:1420
  368.5 8.0 fusion.72
  376.4 6.1 copy.148
  382.5 14.8 %multiply_reduce_fusion = (bf16[1792]{0:T(1024)(128)(2,1)S(1)}, bf16[1792,768]{1,0:T(8,128)(2,1)S(1)}, bf16[1792,768]{1,0:T(8,128)(2,1)}, bf16[1792,768]{1,0:T(8,128)(2,1)}) fusion(f32[1792,768]{1,0:T(8,128)} %fusion.72, f32[1792,768]{1,0:T(8,128)} %fusion.73, f32[1792]{0:T(1024)S(1)} %mul.389, bf16[1792,2048]{1,0:T(8,128)(2,1)} %bitcast.172, ...), kind=kOutput, calls=%fused_computation.10 | convolution fusion | flops 5663291392 | bytes 29764096 | tf_op jit(solution)/shard_map/dot_general | solution.py:1422
  397.3 7.1 copy.147
  404.4 7.4 fusion.2.refs_7_
  413.0 10.8 %convolution_convert_fusion.2 = bf16[2048,768]{1,0:T(8,128)(2,1)} fusion(bf16[1792,2048]{1,0:T(8,128)(2,1)} %bitcast.209, bf16[1792,768]{1,0:T(8,128)(2,1)S(1)} %get-tuple-element.163), kind=kOutput, calls=%fused_computation.17 | convolution fusion | flops 5638717440 | bytes 13238272 | tf_op jit(solution)/shard_map/td,tf->df/dot_general | solution.py:42
  423.8 10.9 %convolution_convert_fusion.1 = bf16[2048,768]{1,0:T(8,128)(2,1)} fusion(bf16[1792,2048]{1,0:T(8,128)(2,1)} %bitcast.210, bf16[1792,768]{1,0:T(8,128)(2,1)S(1)} %copy-done.27), kind=kOutput, calls=%fused_computation.16 | convolution fusion | flops 5638717440 | bytes 13238272 | tf_op jit(solution)/shard_map/td,tf->df/dot_general | solution.py:42
  434.7 118.4 %slab_scatter_4.1 = (f32[112,2176]{1,0:T(8,128)}, f32[112,2048]{1,0:T(8,128)}, bf16[8,768,256]{2,1,0:T(8,128)(2,1)}, bf16[4,768,256]{2,1,0:T(8,128)(2,1)}, bf16[...) custom-call(bf16[16,112,768]{2,1,0:T(8,128)(2,1)} %bitcast.187, bf16[16,112,768]{2,1,0:T(8,128)(2,1)} %bitcast.189, ...), custom_call_target="tpu_custom_call" | custom-call | tf_op jit(solution)/shard_map/slab_scatter_4/pallas_call | solution.py:1254
  553.1 3.5 fusion.8.refs_3_
  559.6 1.6 fusion.7.refs_5_
  563.5 2.7 multiply_reduce_fusion.9
  568.5 2.5 fusion.63
  572.2 136.0 %gather_rows_6.1 = (bf16[32,112,2048]{2,1,0:T(8,128)(2,1)}, f32[32,24,128]{2,1,0:T(8,128)}, bf16[4,256,768]{2,1,0:T(8,128)(2,1)}, bf16[4,256,768]{2,1,0:T(8,128)(2,1)}) custom-call(bf16[112,2048]{1,0:T(8,128)(2,1)} %get-tuple-element.158.refs_0_, f32[24,128]{1,0:T(8,128)} %concatenate.32.refs_1_, bf16[4,256,768]{2,1,0:T(8,128)(2,1)} %fusion.9.refs_2_, ...), custom_call_target="tpu_custom_call" | custom-call | tf_op jit(solution)/shard_map/gather_rows_6/pallas_call | solution.py:751
  711.6 8.4 convolution_convert_fusion
  720.0 3.1 convolution_convert_fusion.4
  723.1 2.4 multiply_reduce_fusion.5
  730.5 1.9 convert_element_type.278
  733.4 1.9 convert_element_type.279
  736.8 3.5 multiply_reduce_fusion.2
  740.9 2.2 multiply_convert_fusion.4
  743.1 12.0 %bitcast_convert_fusion = bf16[2048,384]{1,0:T(8,128)(2,1)} fusion(bf16[32,112,2048]{2,1,0:T(8,128)(2,1)} %get-tuple-element.43, bf16[32,112,128]{2,1,0:T(8,128)(2,1)S(1)} %convolution_convert_fusion.4, bf16[32,112,128]{2,1,0:T(8,128)(2,1)S(1)} %get-tuple-element.167, bf16[32,112,128]{2,1,0:T(8,128)(2,1)S(1)} %get-tuple-element.166), kind=kOutput, calls=%fused_computation.24 | convolution fusion | flops 5646188544 | bytes 19005440 | tf_op jit(solution)/shard_map/td,tq->dq/dot_general | solution.py:42
  755.1 1.9 pad_maximum_fusion.refs_0_
  757.0 108.6 %scatter_sum_7.1 = (f32[112,2048]{1,0:T(8,128)}, f32[128,2048]{1,0:T(8,128)}, bf16[32,64,384]{2,1,0:T(8,128)(2,1)}, bf16[4,768,256]{2,1,0:T(8,128)(2,1)}, f32[32,8,128]{2,1,0:T(8,128)}, /*index=5*/f32[32,8,128]{2,1,0:T(8,128)}) custom-call(bf16[32,112,384]{2,1,0:T(8,128)(2,1)} %pad_maximum_fusion.refs_0_, bf16[2048,384]{1,0:T(8,128)(2,1)} %bitcast.192, ...), custom_call_target="tpu_custom_call" | custom-call | tf_op jit(solution)/shard_map/scatter_sum_7/pallas_call | solution.py:986
  867.3 1.8 fusion.20
  874.7 1.9 convert_element_type.280
  (215 shorter events, 61.6 us)
Async XLA Ops:
  0.6 10.8 %copy-start = (bf16[128,2048]{1,0:T(8,128)(2,1)S(1)}, bf16[128,2048]{1,0:T(8,128)(2,1)}, u32[]{:S(2)}) copy-start(bf16[128,2048]{1,0:T(8,128)(2,1)} %param.19) | copy-start | bytes 1572868
  0.7 7.9 copy-start.28
  1.5 8.7 copy-start.48
  10.6 258.7 %copy-start.5 = (f32[112,2048]{1,0:T(8,128)}, f32[112,2048]{1,0:T(8,128)S(1)}, u32[]{:S(2)}) copy-start(f32[112,2048]{1,0:T(8,128)S(1)} %get-tuple-element.196) | copy-start | bytes 2752516
  10.6 2.3 copy-start.34
  10.6 3.9 copy-start.50
  164.9 106.9 %copy-start.15 = (bf16[2048,16]{1,0:T(8,128)(2,1)}, bf16[2048,16]{1,0:T(8,128)(2,1)S(1)}, u32[]{:S(2)}) copy-start(bf16[2048,16]{1,0:T(8,128)(2,1)S(1)} %convert_element_type.247) | copy-start | bytes 196612
  164.9 2.7 copy-start.31
  166.2 17.0 %copy-start.9 = (f32[3584,128]{1,0:T(8,128)}, f32[3584,128]{1,0:T(8,128)S(1)}, u32[]{:S(2)}) copy-start(f32[3584,128]{1,0:T(8,128)S(1)} %fusion.14) | copy-start | bytes 5505028
  167.5 15.7 %copy-start.7 = (f32[3584,128]{1,0:T(8,128)}, f32[3584,128]{1,0:T(8,128)S(1)}, u32[]{:S(2)}) copy-start(f32[3584,128]{1,0:T(8,128)S(1)} %fusion.15) | copy-start | bytes 5505028
  179.4 2.5 copy-start.2
  357.8 10.7 %copy-start.25 = (bf16[4,2,256,768]{3,2,1,0:T(8,128)(2,1)S(1)}, bf16[4,2,256,768]{3,2,1,0:T(8,128)(2,1)}, u32[]{:S(2)}) copy-start(bf16[4,2,256,768]{3,2,1,0:T(8,128)(2,1)} %get-tuple-element.51) | copy-start | bytes 9437188
  357.8 10.7 %copy-start.52 = (bf16[16,112,2048]{2,1,0:T(8,128)(2,1)S(1)}, bf16[16,112,2048]{2,1,0:T(8,128)(2,1)}, u32[]{:S(2)}) copy-start(bf16[16,112,2048]{2,1,0:T(8,128)(2,1)} %get-tuple-element.50) | copy-start | bytes 22020100
  397.3 15.7 %copy-start.26 = (bf16[1792,768]{1,0:T(8,128)(2,1)}, bf16[1792,768]{1,0:T(8,128)(2,1)S(1)}, u32[]{:S(2)}) copy-start(bf16[1792,768]{1,0:T(8,128)(2,1)S(1)} %get-tuple-element.163) | copy-start | bytes 8257540
  413.0 10.8 %copy-start.27 = (bf16[1792,768]{1,0:T(8,128)(2,1)S(1)}, bf16[1792,768]{1,0:T(8,128)(2,1)}, u32[]{:S(2)}) copy-start(bf16[1792,768]{1,0:T(8,128)(2,1)} %get-tuple-element.165) | copy-start | bytes 8257540
  553.1 3.6 copy-start.14
  553.1 3.6 copy-start.33
  556.7 2.9 copy-start.41
  561.3 2.2 copy-start.16
  562.4 3.8 copy-start.13
  566.2 2.3 copy-start.19
  572.2 138.8 %copy-start.53 = (f32[32]{0:T(128)S(1)}, f32[32]{0:T(128)}, u32[]{:S(2)}) copy-start(f32[32]{0:T(128)} %param.35) | copy-start | bytes 388
  572.2 139.4 %copy-start.43 = (bf16[128,2048]{1,0:T(8,128)(2,1)S(1)}, bf16[128,2048]{1,0:T(8,128)(2,1)}, u32[]{:S(2)}) copy-start(bf16[128,2048]{1,0:T(8,128)(2,1)} %refs_1_.1) | copy-start | bytes 1572868
  720.0 3.1 copy-start.11
  729.1 6.8 slice-start
  730.5 2.8 copy-start.36
  733.4 2.6 slice-start.1
  757.0 108.7 %copy-start.6 = (f32[112,2048]{1,0:T(8,128)S(1)}, f32[112,2048]{1,0:T(8,128)}, u32[]{:S(2)}) copy-start(f32[112,2048]{1,0:T(8,128)} %copy-done.5) | copy-start | bytes 2752516
  757.0 108.7 %copy-start.51 = (f32[112]{0:T(128)S(1)}, f32[112]{0:T(128)}, u32[]{:S(2)}) copy-start(f32[112]{0:T(128)} %copy-done.50) | copy-start | bytes 1348
  867.3 3.2 copy-start.38
  872.0 2.7 copy-start.35
  874.7 2.9 copy-start.1
  (24 other events, 35.4 us)

commit v7 on v5

--- a/solution.py
+++ b/solution.py
@@ -949,7 +949,7 @@
         self.z, self.x, self.c = spot
         self.up, self.down, self.side, self.twin = ways
         self.lefts, self.rights, self.beside, self.out = refs
-        (self.sent, self.got, self.from_side, self.rising, self.falling, self.held,
+        (self.sent, self.got, self.from_side, self.rising, self.falling,
          self.twin_send, self.twin_recv, self.side_send, self.side_recv, self.line_send,
          self.up_recv, self.down_recv) = buffers
         self.plain = self.rights[0].shape[0 if turned else 1]
@@ -1036,20 +1036,16 @@
             [self.got.at[index] for index in both],
             [self.order(index, self.c) for index in both],
             [(self.got.at[index],) for index in both])
-        for index in both:
-            self.side_copy(index).start()
-
-    def to_line(self, pair):
-        both = (2 * pair, 2 * pair + 1)
-        for step in both:
-            self.twin_copy(self.nz + step).wait_recv()
-            self.side_copy(step).wait_recv()
+        self.side_copy(both[0]).start()
+
+    def to_line(self, step):
+        self.twin_copy(self.nz + step).wait_recv()
+        self.side_copy(step).wait_recv()
         self.combine(
-            [self.held.at[0], self.held.at[1]],
-            [self.order(self.nz + step, self.c) for step in both],
-            [(self.got.at[self.nz + step], self.from_side.at[step]) for step in both])
-        for which, step in enumerate(both):
-            self.along_line(self.held.at[which], step)
+            [self.out],
+            [self.order(self.nz + step, self.c)],
+            [(self.got.at[self.nz + step], self.from_side.at[step])])
+        self.along_line(self.out, step)
 
     def along_line(self, held, step):
         z, zz = self.z, self.zed(step)
@@ -1072,8 +1068,6 @@
         pl.when(zz < z)(lambda: self.line_copy(step, zz, False).start())
 
     def end(self):
-        self.out[...] = self.held[1]
-
         def finish(step, carry):
             self.twin_copy(step).wait_send()
             return carry
@@ -1111,7 +1105,7 @@
     up, down, near, far, twin = targets(dp, ep, z, y, x, c, nz)
     side = (dp, ep + 2 - 4 * x)
     sums = [
-        SlabSum(nz, form[1], (z, x, c), (up, down, side, twin), held + (out,), take(13))
+        SlabSum(nz, form[1], (z, x, c), (up, down, side, twin), held + (out,), take(12))
         for form, held, out in zip(forms, operands, outs)
     ]
     riders = Riders(kinds, nz, (dp, ep, z, y), rider_ins + rider_outs + tuple(refs))
@@ -1121,17 +1115,19 @@
     def side_step(pair, carry):
         for part in sums:
             part.to_side(pair)
+        for part in sums:
+            part.side_copy(2 * pair + 1).start()
         riders.looped(pair, nz // 2)
         return carry
 
     lax.fori_loop(0, nz // 2, side_step, 0)
 
-    def line_step(pair, carry):
+    def line_step(step, carry):
         for part in sums:
-            part.to_line(pair)
+            part.to_line(step)
         return carry
 
-    lax.fori_loop(0, nz // 2, line_step, 0)
+    lax.fori_loop(0, nz, line_step, 0)
     for part in sums:
         part.end()
     riders.finish()
@@ -1151,7 +1147,6 @@
         operands += tuple(v.reshape(blocks, rows, -1) for v in lefts) + tuple(rights) + held
         outs += (jax.ShapeDtypeStruct(block, jnp.float32),)
         scratch += [pltpu.VMEM((count * nz,) + block, low) for count in (2, 2, 1, 1, 1)]
-        scratch += [pltpu.VMEM((2,) + block, jnp.float32)]
         scratch += [dma((2 * nz,))] * 2 + [dma((nz,))] * 5
         forms.append((len(lefts), turned, len(held)))
     return pl.pallas_call(

time: 862 us -> 861 us (level)
  no operation moved by 1% of the time
where the time goes in v7:
time: 861 us; the launch traced here: 849 us
  Pallas kernels  650 us (75%)
  matrix products  120 us (14%)
  other arithmetic  51.4 us (6%)
  local copies, waits for them, and re-layouts  26 us (3%)
    pallas_call x3, Pallas kernels, gather_rows(): pl.pallas_call(functools.partial(gather_kernel, nz, (len(whole), len(slab...  347 us
    pallas_call x2, Pallas kernels, scatter_sum(): pl.pallas_call(functools.partial(scatter_kernel, nz, turned, kinds), out_...  185 us
    pallas_call x1, Pallas kernels, slab_scatter(): pl.pallas_call(functools.partial(slab_scatter_kernel, nz, tuple(forms), k...  117 us
    dot_general x14, matrix products, contract(): jnp.einsum(pattern, left_side, right_side, preferred_element_type=jnp.flo...  70.2 us

profile of v7, /device:TPU:1, one launch (start us, length us, event | category | flops | bytes accessed | tf_op | source)
XLA Modules:
  0.0 849.1 jit_solution(3078476767352526582)
XLA Ops:
  14.5 146.5 %gather_rows_1.1 = (bf16[32,112,2048]{2,1,0:T(8,128)(2,1)}, f32[32,16,128]{2,1,0:T(8,128)}, bf16[16,112,2048]{2,1,0:T(8,128)(2,1)}, bf16[32,64,384]{2,1,0:T(8,128)(2,1)}, bf16[4,2,256,768]{3,2,1,0:T(8,128)(2,1)}) custom-call(bf16[112,2048]{1,0:T(8,128)(2,1)} %multiply_convert_fusion.7.refs_0_, f32[16,128]{1,0:T(8,128)} %pad.27.refs_1_, ...), custom_call_target="tpu_custom_call" | custom-call | tf_op jit(solution)/shard_map/gather_rows_1/pallas_call | solution.py:751
  167.6 11.9 %fusion.65 = f32[32,112,384]{2,1,0:T(8,128)S(1)} fusion(bf16[32,112,2048]{2,1,0:T(8,128)(2,1)} %get-tuple-element.41, bf16[2048,384,1]{1,0,2:T(8,128)(2,1)S(1)} %bitcast.177), kind=kOutput, calls=%fused_computation.188 | convolution fusion | flops 5637144576 | bytes 21757952 | tf_op jit(solution)/shard_map/dot_general | solution.py:1273
  185.7 1.8 fusion.62
  187.5 3.1 convolution_convert_fusion.6.refs_0_
  190.6 77.0 %scatter_sum_2.1 = (f32[112,2048]{1,0:T(8,128)}, bf16[4,256,768]{2,1,0:T(8,128)(2,1)}) custom-call(bf16[32,112,128]{2,1,0:T(8,128)(2,1)} %convolution_convert_fusion.6.refs_0_, bf16[128,2048]{1,0:T(8,128)(2,1)} %refs_1_.1, bf16[4,256,768]{2,1,0:T(8,128)(2,1)} %bitcast.164), custom_call_target="tpu_custom_call" | custom-call | tf_op jit(solution)/shard_map/scatter_sum_2/pallas_call | solution.py:922
  271.5 83.8 %gather_rows_3.1 = (bf16[16,112,2048]{2,1,0:T(8,128)(2,1)}, f32[16,16,128]{2,1,0:T(8,128)}, bf16[4,2,256,768]{3,2,1,0:T(8,128)(2,1)}, bf16[4,2,256,768]{3,2,1,0:T(8,128)(2,1)}) custom-call(bf16[112,2048]{1,0:T(8,128)(2,1)} %copy-done.13, f32[16,128]{1,0:T(8,128)} %pad.28.refs_1_, bf16[4,256,768]{2,1,0:T(8,128)(2,1)} %refs_2_.1, ...), custom_call_target="tpu_custom_call" | custom-call | tf_op jit(solution)/shard_map/gather_rows_3/pallas_call | solution.py:751
  356.4 10.7 %fusion.68 = f32[1792,768]{1,0:T(8,128)} fusion(bf16[1792,2048]{1,0:T(8,128)(2,1)} %bitcast.195, bf16[2048,768]{1,0:T(8,128)(2,1)} %bitcast.167), kind=kOutput, calls=%fused_computation.191 | convolution fusion | flops 5637144576 | bytes 15990784 | tf_op jit(solution)/shard_map/dot_general | solution.py:1318
  367.1 7.9 fusion.67
  375.0 11.7 %multiply_reduce_fusion = (bf16[1792]{0:T(1024)(128)(2,1)S(1)}, bf16[1792,768]{1,0:T(8,128)(2,1)S(1)}, bf16[1792,768]{1,0:T(8,128)(2,1)S(1)}, bf16[1792,768]{1,0:T(8,128)(2,1)}) fusion(f32[1792,768]{1,0:T(8,128)} %fusion.67, f32[1792,768]{1,0:T(8,128)} %fusion.68, f32[1792]{0:T(1024)S(1)} %mul.378, bf16[1792,2048]{1,0:T(8,128)(2,1)S(1)} %bitcast.193, ...), kind=kOutput, calls=%fused_computation.2 | convolution fusion | flops 5663291392 | bytes 29764096 | tf_op jit(solution)/shard_map/dot_general | solution.py:1320
  386.8 7.7 convolution_convert_fusion.1
  395.6 10.8 %convolution_convert_fusion.3 = bf16[2048,768]{1,0:T(8,128)(2,1)} fusion(bf16[1792,2048]{1,0:T(8,128)(2,1)} %bitcast.196, bf16[1792,768]{1,0:T(8,128)(2,1)S(1)} %get-tuple-element.174), kind=kOutput, calls=%fused_computation.10 | convolution fusion | flops 5638717440 | bytes 13238272 | tf_op jit(solution)/shard_map/td,tf->df/dot_general | solution.py:42
  406.4 10.9 %convolution_convert_fusion.2 = bf16[2048,768]{1,0:T(8,128)(2,1)} fusion(bf16[1792,2048]{1,0:T(8,128)(2,1)} %bitcast.197, bf16[1792,768]{1,0:T(8,128)(2,1)S(1)} %copy-done.31), kind=kOutput, calls=%fused_computation.9 | convolution fusion | flops 5638717440 | bytes 13238272 | tf_op jit(solution)/shard_map/td,tf->df/dot_general | solution.py:42
  417.3 117.5 %slab_scatter_4.1 = (f32[112,2176]{1,0:T(8,128)}, f32[112,2048]{1,0:T(8,128)}, bf16[4,256,768]{2,1,0:T(8,128)(2,1)}, bf16[4,256,768]{2,1,0:T(8,128)(2,1)}, bf16[4,256,768]{2,1,0:T(8,128)(2,1)}) custom-call(bf16[16,112,768]{2,1,0:T(8,128)(2,1)} %bitcast.171, bf16[16,112,768]{2,1,0:T(8,128)(2,1)} %bitcast.173, bf16[2048,768]{1,0:T(8,128)(2,1)} %bitcast.168, ...), custom_call_target="tpu_custom_call" | custom-call | tf_op jit(solution)/shard_map/slab_scatter_4/pallas_call | solution.py:1152
  534.8 3.5 fusion.2.refs_3_
  541.3 1.6 fusion.4.refs_2_
  545.2 3.2 multiply_reduce_fusion.9
  550.7 2.5 fusion.58
  554.5 116.4 %gather_rows_6.1 = (bf16[32,112,2048]{2,1,0:T(8,128)(2,1)}, f32[32,24,128]{2,1,0:T(8,128)}, bf16[4,256,768]{2,1,0:T(8,128)(2,1)}, bf16[4,256,768]{2,1,0:T(8,128)(2,1)}) custom-call(bf16[112,2048]{1,0:T(8,128)(2,1)} %get-tuple-element.169.refs_0_, f32[24,128]{1,0:T(8,128)} %concatenate.32.refs_1_, bf16[4,256,768]{2,1,0:T(8,128)(2,1)} %fusion.4.refs_2_, ...), custom_call_target="tpu_custom_call" | custom-call | tf_op jit(solution)/shard_map/gather_rows_6/pallas_call | solution.py:751
  674.2 8.4 convolution_bitcast_fusion
  684.0 5.1 convolution_convert_fusion
  689.0 3.1 convolution_convert_fusion.5
  692.1 2.4 multiply_reduce_fusion.5
  697.1 1.9 convert_element_type.281
  702.1 1.9 convert_element_type.282
  705.6 3.5 multiply_reduce_fusion.2
  709.7 2.2 multiply_convert_fusion.4
  711.9 12.0 %bitcast_convert_fusion = bf16[2048,384]{1,0:T(8,128)(2,1)} fusion(bf16[32,112,2048]{2,1,0:T(8,128)(2,1)} %get-tuple-element.41, bf16[32,112,128]{2,1,0:T(8,128)(2,1)S(1)} %convolution_convert_fusion.5, bf16[32,112,128]{2,1,0:T(8,128)(2,1)S(1)} %get-tuple-element.178, bf16[32,112,128]{2,1,0:T(8,128)(2,1)S(1)} %get-tuple-element.177), kind=kOutput, calls=%fused_computation.17 | convolution fusion | flops 5646188544 | bytes 19005440 | tf_op jit(solution)/shard_map/td,tq->dq/dot_general | solution.py:42
  723.9 1.9 pad_maximum_fusion.refs_0_
  725.8 108.4 %scatter_sum_7.1 = (f32[112,2048]{1,0:T(8,128)}, bf16[32,64,384]{2,1,0:T(8,128)(2,1)}, bf16[4,256,768]{2,1,0:T(8,128)(2,1)}, f32[32,8,128]{2,1,0:T(8,128)}, f32[32,8,128]{2,1,0:T(8,128)}) custom-call(bf16[32,112,384]{2,1,0:T(8,128)(2,1)} %pad_maximum_fusion.refs_0_, bf16[2048,384]{1,0:T(8,128)(2,1)} %bitcast.176, bf16[32,64,384]{2,1,0:T(8,128)(2,1)} %bitcast.178, ...), custom_call_target="tpu_custom_call" | custom-call | tf_op jit(solution)/shard_map/scatter_sum_7/pallas_call | solution.py:922
  835.9 1.9 fusion.15
  843.2 1.9 convert_bitcast_fusion
  845.2 3.5 copy.147
  (240 shorter events, 60.6 us)
Async XLA Ops:
  0.6 10.8 %copy-start = (bf16[128,2048]{1,0:T(8,128)(2,1)S(1)}, bf16[128,2048]{1,0:T(8,128)(2,1)}, u32[]{:S(2)}) copy-start(bf16[128,2048]{1,0:T(8,128)(2,1)} %param.19) | copy-start | bytes 1572868
  0.7 7.9 copy-start.32
  1.5 8.7 %copy-start.52 = (f32[64]{0:T(128)}, f32[64]{0:T(128)S(1)}, u32[]{:S(2)}) copy-start(f32[64]{0:T(128)S(1)} %convert_element_type.231) | copy-start | bytes 772
  2.1 178.5 %copy-start.56 = (f32[128]{0:T(128)}, f32[128]{0:T(128)S(1)}, u32[]{:S(2)}) copy-start(f32[128]{0:T(128)S(1)} %convert_element_type.242) | copy-start | bytes 1540
  2.8 177.9 %copy-start.58 = (f32[128]{0:T(128)}, f32[128]{0:T(128)S(1)}, u32[]{:S(2)}) copy-start(f32[128]{0:T(128)S(1)} %convert_element_type.245) | copy-start | bytes 1540
  3.5 539.4 %copy-start.50 = (s32[128]{0:T(128)}, s32[128]{0:T(128)S(1)}, u32[]{:S(2)}) copy-start(s32[128]{0:T(128)S(1)} %and_select_fusion) | copy-start | bytes 1540
  10.6 257.1 %copy-start.6 = (f32[112,2048]{1,0:T(8,128)}, f32[112,2048]{1,0:T(8,128)S(1)}, u32[]{:S(2)}) copy-start(f32[112,2048]{1,0:T(8,128)S(1)} %get-tuple-element.207) | copy-start | bytes 2752516
  10.6 3.9 copy-start.54
  164.9 105.3 %copy-start.17 = (bf16[2048,16]{1,0:T(8,128)(2,1)}, bf16[2048,16]{1,0:T(8,128)(2,1)S(1)}, u32[]{:S(2)}) copy-start(bf16[2048,16]{1,0:T(8,128)(2,1)S(1)} %convert_element_type.250) | copy-start | bytes 196612
  166.2 17.0 %copy-start.10 = (f32[3584,128]{1,0:T(8,128)}, f32[3584,128]{1,0:T(8,128)S(1)}, u32[]{:S(2)}) copy-start(f32[3584,128]{1,0:T(8,128)S(1)} %fusion.9) | copy-start | bytes 5505028
  167.5 15.7 %copy-start.8 = (f32[3584,128]{1,0:T(8,128)}, f32[3584,128]{1,0:T(8,128)S(1)}, u32[]{:S(2)}) copy-start(f32[3584,128]{1,0:T(8,128)S(1)} %fusion.10) | copy-start | bytes 5505028
  270.0 275.2 %copy-start.60 = (f32[112]{0:T(128)}, f32[112]{0:T(128)S(1)}, u32[]{:S(2)}) copy-start(f32[112]{0:T(128)S(1)} %add_rsqrt_fusion.2) | copy-start | bytes 1348
  356.3 10.7 %copy-start.27 = (bf16[4,2,256,768]{3,2,1,0:T(8,128)(2,1)S(1)}, bf16[4,2,256,768]{3,2,1,0:T(8,128)(2,1)}, u32[]{:S(2)}) copy-start(bf16[4,2,256,768]{3,2,1,0:T(8,128)(2,1)} %get-tuple-element.49) | copy-start | bytes 9437188
  356.3 10.7 %copy-start.63 = (bf16[16,112,2048]{2,1,0:T(8,128)(2,1)S(1)}, bf16[16,112,2048]{2,1,0:T(8,128)(2,1)}, u32[]{:S(2)}) copy-start(bf16[16,112,2048]{2,1,0:T(8,128)(2,1)} %get-tuple-element.48) | copy-start | bytes 22020100
  356.3 18.7 %slice-start.2 = ((s8[7340032]{0:T(1024)(128)(4,1)}), s8[4194304]{0:T(1024)(128)(4,1)S(1)}, s32[]{:S(2)}) async-start(s8[7340032]{0:T(1024)(128)(4,1)} %bitcast.191), calls=%async_computation.2 | async-start | bytes 8388608
  367.1 8.0 copy-start.28
  367.1 8.0 slice-start.3
  386.8 7.7 copy-start.30
  386.8 8.8 %copy-start.29 = (bf16[1792,768]{1,0:T(8,128)(2,1)}, bf16[1792,768]{1,0:T(8,128)(2,1)S(1)}, u32[]{:S(2)}) copy-start(bf16[1792,768]{1,0:T(8,128)(2,1)S(1)} %get-tuple-element.174) | copy-start | bytes 8257540
  395.6 10.8 %copy-start.31 = (bf16[1792,768]{1,0:T(8,128)(2,1)S(1)}, bf16[1792,768]{1,0:T(8,128)(2,1)}, u32[]{:S(2)}) copy-start(bf16[1792,768]{1,0:T(8,128)(2,1)} %get-tuple-element.176) | copy-start | bytes 8257540
  534.8 3.6 copy-start.16
  534.8 3.6 copy-start.36
  544.1 4.3 copy-start.14
  554.4 119.2 %copy-start.64 = (f32[32]{0:T(128)S(1)}, f32[32]{0:T(128)}, u32[]{:S(2)}) copy-start(f32[32]{0:T(128)} %param.35) | copy-start | bytes 388
  554.5 119.7 %copy-start.19 = (bf16[32,112,128]{2,1,0:T(8,128)(2,1)S(1)}, bf16[32,112,128]{2,1,0:T(8,128)(2,1)}, u32[]{:S(2)}) copy-start(bf16[32,112,128]{2,1,0:T(8,128)(2,1)} %convolution_convert_fusion.6.refs_0_) | copy-start | bytes 2752516
  674.2 9.7 %copy-start.3 = (bf16[32,112,2048]{2,1,0:T(8,128)(2,1)S(1)}, bf16[32,112,2048]{2,1,0:T(8,128)(2,1)}, u32[]{:S(2)}) copy-start(bf16[32,112,2048]{2,1,0:T(8,128)(2,1)} %get-tuple-element.55) | copy-start | bytes 44040196
  674.2 9.8 %copy-start.45 = (bf16[128,2048]{1,0:T(8,128)(2,1)S(1)}, bf16[128,2048]{1,0:T(8,128)(2,1)}, u32[]{:S(2)}) copy-start(bf16[128,2048]{1,0:T(8,128)(2,1)} %refs_1_.1) | copy-start | bytes 1572868
  700.7 4.2 slice-start
  725.8 108.4 %copy-start.7 = (f32[112,2048]{1,0:T(8,128)S(1)}, f32[112,2048]{1,0:T(8,128)}, u32[]{:S(2)}) copy-start(f32[112,2048]{1,0:T(8,128)} %copy-done.6) | copy-start | bytes 2752516
  725.8 108.4 %copy-start.55 = (f32[112]{0:T(128)S(1)}, f32[112]{0:T(128)}, u32[]{:S(2)}) copy-start(f32[112]{0:T(128)} %copy-done.54) | copy-start | bytes 1348
  835.9 3.2 copy-start.42
  843.2 5.5 copy-start.1
  (37 other events, 69.2 us)
